TPU v7x, 32 devices: a whole 2x2x4 slice. The times are simulated.
32 devices in a mesh: seq: 4 (over y, core), fsdp: 8 (over z, x).
Axes of the slice: x: 2, y: 2, z: 4, core: 2. Of those that a mesh axis runs over, the one named last changes fastest.
Arguments:
- tokens: bfloat16 [8, 1024, 2048], P('fsdp', 'seq'), may hold values from -6 to 6
- teacher: bfloat16 [8, 1024, 2048], P('fsdp', 'seq'), may hold values from -6 to 6
- segments: int32 [8, 1024], P('fsdp'), may hold values from 0 to 3, never falling along the last dimension, each value on 1 to 512 neighbouring positions
- valid: int32 [8, 1024], P('fsdp', 'seq'), may hold values from 0 to 1, as said below
- ln1_gain: bfloat16 [2048], P('fsdp'), may hold values from 0.099609375 to 1.8984375
- ln1_bias: bfloat16 [2048], P('fsdp'), may hold values from -1.75 to 1.75
- w_qkv: bfloat16 [2048, 6144], P('fsdp'), may hold values from -0.125 to 0.125
- b_qkv: bfloat16 [6144], P('fsdp'), may hold values from -1.75 to 1.75
- w_out: bfloat16 [2048, 2048], P('fsdp'), may hold values from -0.5 to 0.5
- ln2_gain: bfloat16 [2048], P('fsdp'), may hold values from 0.099609375 to 1.8984375
- ln2_bias: bfloat16 [2048], P('fsdp'), may hold values from -1.75 to 1.75
- w_gate_up: bfloat16 [5632, 2, 2048], P('fsdp'), may hold values from -0.125 to 0.125
- w_down: bfloat16 [5632, 2048], P('fsdp'), may hold values from -0.15625 to 0.15625
Outputs:
- layer_out: bfloat16 [8, 1024, 2048], P('fsdp', 'seq')
- loss: float32 [], replicated
- grad_tokens: bfloat16 [8, 1024, 2048], P('fsdp', 'seq')
- grad_ln1_gain: float32 [2048], P('fsdp')
- grad_ln1_bias: float32 [2048], P('fsdp')
- grad_w_qkv: float32 [2048, 6144], P('fsdp')
- grad_b_qkv: float32 [6144], P('fsdp')
- grad_w_out: float32 [2048, 2048], P('fsdp')
- grad_ln2_gain: float32 [2048], P('fsdp')
- grad_ln2_bias: float32 [2048], P('fsdp')
- grad_w_gate_up: float32 [5632, 2, 2048], P('fsdp')
- grad_w_down: float32 [5632, 2048], P('fsdp')
Inputs may be any that keep to these rules, and one draw needn't show every extreme that they name: `segments`: segment numbers start at 0 in each sequence and never fall; each document has 1 to 512 tokens and one document of each sequence has exactly that many. `valid`: the first token of every sequence counts.
All inputs are finite; a program needn't handle non-finite values.
Results may differ from a plain program's by a relative error of at most 0.01.
Values may be sent and summed in bfloat16 or wider, within the bound.
No kernel may reach another device: no remote copies, remote signals or barrier semaphores. Data moves between devices by JAX's collectives and lax.ppermute only.
A program may use at most 704 MiB of HBM per device.

v0:
```python
import jax
import jax.numpy as jnp
from jax import lax
from jax.sharding import PartitionSpec as P

H = 32
HD = 64
ROT = 16


EPSILON = 1e-05
MASKED_VALUE = -1e30


def norm_parts(values):
    mean_value = jnp.mean(values, axis=-1, keepdims=True)
    centered = values - mean_value
    variance = jnp.mean(centered * centered, axis=-1, keepdims=True)
    inv_std = lax.rsqrt(variance + EPSILON)
    return (centered * inv_std, inv_std)


def norm_back(grad_out, normed, inv_std, gain_vec):
    scaled = grad_out * gain_vec
    mean_scaled = jnp.mean(scaled, axis=-1, keepdims=True)
    mean_cross = jnp.mean(scaled * normed, axis=-1, keepdims=True)
    return inv_std * (scaled - mean_scaled - normed * mean_cross)


def doc_positions(segment):
    places = jnp.arange(segment.shape[0], dtype=jnp.int32)
    change = jnp.concatenate([jnp.ones((1,), dtype=bool), segment[1:] != segment[:-1]])
    starts = lax.cummax(jnp.where(change, places, 0), axis=0)
    return places - starts


def rotate(values, positions, turn_sign):
    half_rot = ROT // 2
    inverse = 10000.0 ** (-(jnp.arange(half_rot, dtype=jnp.float32) * 2.0) / ROT)
    angles = positions.astype(jnp.float32)[:, None] * inverse[None, :]
    cosine = jnp.cos(angles)[:, None, :]
    sine_part = turn_sign * jnp.sin(angles)[:, None, :]
    front_half = values[..., :half_rot]
    back_half = values[..., half_rot:ROT]
    return jnp.concatenate(
        [
            front_half * cosine - back_half * sine_part,
            back_half * cosine + front_half * sine_part,
            values[..., ROT:],
        ],
        axis=-1,
    )


def gate_backward(gate_up, hidden_grad):
    gate_part = gate_up[:, 0]
    up_part = gate_up[:, 1]
    gate_sig = jax.nn.sigmoid(gate_part)
    up_grad = hidden_grad * (gate_part * gate_sig)
    silu_grad = hidden_grad * up_part
    gate_grad = silu_grad * gate_sig + silu_grad * gate_part * gate_sig * (1.0 - gate_sig)
    return jnp.stack([gate_grad, up_grad], axis=1).astype(jnp.bfloat16)


def block_scores(query_block, key_rows, block_seg, segment, first_row, score_scale):
    block_size = query_block.shape[0]
    places = jnp.arange(segment.shape[0], dtype=jnp.int32)
    block_places = first_row + jnp.arange(block_size, dtype=jnp.int32)
    allowed = (block_seg[:, None] == segment[None, :]) & (block_places[:, None] >= places[None, :])
    scores = (
        jnp.einsum("bhd,lhd->hbl", query_block, key_rows, preferred_element_type=jnp.float32)
        * score_scale
    )
    return jnp.where(allowed[None], scores, MASKED_VALUE)


def attention_forward(query_rows, key_rows, value_rows, segment, block_size, score_scale):
    length_total = key_rows.shape[0]

    def one_block(unused, first_row):
        query_block = lax.dynamic_slice_in_dim(query_rows, first_row, block_size, 0)
        block_seg = lax.dynamic_slice_in_dim(segment, first_row, block_size, 0)
        scores = block_scores(query_block, key_rows, block_seg, segment, first_row, score_scale)
        row_max = jnp.max(scores, axis=-1, keepdims=True)
        exp_scores = jnp.exp(scores - row_max)
        row_sum = jnp.sum(exp_scores, axis=-1, keepdims=True)
        probs = (exp_scores / row_sum).astype(jnp.bfloat16)
        block_out = jnp.einsum(
            "hbl,lhd->bhd", probs, value_rows, preferred_element_type=jnp.float32
        )
        return (unused, (block_out.astype(jnp.bfloat16), (row_max + jnp.log(row_sum))[..., 0]))

    firsts = jnp.arange(length_total // block_size, dtype=jnp.int32) * block_size
    unused, (block_outs, log_totals) = lax.scan(one_block, jnp.zeros((), jnp.int32), firsts)
    return (block_outs.reshape(length_total, query_rows.shape[1], query_rows.shape[2]), log_totals)


def attention_backward(
    query_rows, key_rows, value_rows, out_grad, log_totals, segment, block_size, score_scale
):
    length_total = key_rows.shape[0]

    def one_block(grad_carry, block_inputs):
        key_grad, value_grad = grad_carry
        first_row, block_log = block_inputs
        query_block = lax.dynamic_slice_in_dim(query_rows, first_row, block_size, 0)
        grad_block = lax.dynamic_slice_in_dim(out_grad, first_row, block_size, 0)
        block_seg = lax.dynamic_slice_in_dim(segment, first_row, block_size, 0)
        scores = block_scores(query_block, key_rows, block_seg, segment, first_row, score_scale)
        probs = jnp.exp(scores - block_log[..., None])
        prob_low = probs.astype(jnp.bfloat16)
        value_grad = value_grad + jnp.einsum(
            "hbl,bhd->lhd", prob_low, grad_block, preferred_element_type=jnp.float32
        )
        prob_grad = jnp.einsum(
            "bhd,lhd->hbl", grad_block, value_rows, preferred_element_type=jnp.float32
        )
        row_dot = jnp.sum(probs * prob_grad, axis=-1, keepdims=True)
        score_grad = (probs * (prob_grad - row_dot)).astype(jnp.bfloat16)
        query_grad = (
            jnp.einsum("hbl,lhd->bhd", score_grad, key_rows, preferred_element_type=jnp.float32)
            * score_scale
        )
        key_grad = (
            key_grad
            + jnp.einsum(
                "hbl,bhd->lhd", score_grad, query_block, preferred_element_type=jnp.float32
            )
            * score_scale
        )
        return ((key_grad, value_grad), query_grad)

    firsts = jnp.arange(length_total // block_size, dtype=jnp.int32) * block_size
    zero_grad = jnp.zeros(key_rows.shape, jnp.float32)
    (key_grad, value_grad), query_grads = lax.scan(
        one_block, (zero_grad, zero_grad), (firsts, log_totals)
    )
    return (query_grads.reshape(key_rows.shape), key_grad, value_grad)


def reduce_rows(term_rows, row_share):
    return lax.psum_scatter(
        term_rows(jnp.int32(0), row_share * lax.axis_size("fsdp")).astype(jnp.bfloat16),
        "fsdp",
        scatter_dimension=0,
        tiled=True,
    ).astype(jnp.float32)


def per_device(
    tokens,
    teacher,
    segments,
    valid,
    ln1_gain,
    ln1_bias,
    w_qkv,
    b_qkv,
    w_out,
    ln2_gain,
    ln2_bias,
    w_gate_up,
    w_down,
):
    seq_count = lax.axis_size("seq")
    fsdp_count = lax.axis_size("fsdp")
    seq_index = lax.axis_index("seq")
    fsdp_index = lax.axis_index("fsdp")
    row_count = tokens.shape[1]
    model_width = tokens.shape[2]
    length_total = segments.shape[1]
    heads_here = H // seq_count
    group_width = heads_here * HD
    block_size = min(512, length_total)
    score_scale = HD ** (-0.5)
    tokens_total = row_count * seq_count * fsdp_count
    full_qkv, full_out, full_bias, gain_one, shift_one, gain_two, shift_two = (
        lax.all_gather(w_qkv, "fsdp", axis=0, tiled=True),
        lax.all_gather(w_out, "fsdp", axis=0, tiled=True),
        lax.all_gather(b_qkv, "fsdp", axis=0, tiled=True),
        lax.all_gather(ln1_gain, "fsdp", axis=0, tiled=True),
        lax.all_gather(ln1_bias, "fsdp", axis=0, tiled=True),
        lax.all_gather(ln2_gain, "fsdp", axis=0, tiled=True),
        lax.all_gather(ln2_bias, "fsdp", axis=0, tiled=True),
    )
    gain_one = gain_one.astype(jnp.float32)
    gain_two = gain_two.astype(jnp.float32)
    segment = segments[0]
    positions_all = doc_positions(segment)
    positions = lax.dynamic_slice_in_dim(positions_all, seq_index * row_count, row_count, 0)
    tokens_in = tokens[0].astype(jnp.float32)
    teacher_in = teacher[0].astype(jnp.float32)
    counted = valid[0].astype(jnp.float32)
    normed_one, inv_std_one = norm_parts(tokens_in)
    hidden_one = (normed_one * gain_one + shift_one.astype(jnp.float32)).astype(jnp.bfloat16)
    qkv_float = jnp.dot(
        hidden_one, full_qkv, preferred_element_type=jnp.float32
    ) + full_bias.astype(jnp.float32)
    split_rows = qkv_float.reshape(row_count, 3, H, HD)
    packed = jnp.stack(
        [
            rotate(split_rows[:, 0], positions, 1.0),
            rotate(split_rows[:, 1], positions, 1.0),
            split_rows[:, 2],
        ],
        axis=1,
    )
    packed = packed.astype(jnp.bfloat16).reshape(row_count, 3, seq_count, group_width)
    spread = lax.all_to_all(packed, "seq", split_axis=2, concat_axis=0, tiled=True)
    head_rows = spread.reshape(length_total, 3, heads_here, HD)
    query_rows = head_rows[:, 0]
    key_rows = head_rows[:, 1]
    value_rows = head_rows[:, 2]
    heads_out, log_totals = attention_forward(
        query_rows, key_rows, value_rows, segment, block_size, score_scale
    )
    returned = lax.all_to_all(
        heads_out.reshape(length_total, 1, group_width),
        "seq",
        split_axis=0,
        concat_axis=1,
        tiled=True,
    )
    attn_rows = returned.reshape(row_count, model_width)
    resid = tokens_in + jnp.dot(attn_rows, full_out, preferred_element_type=jnp.float32)
    normed_two, inv_std_two = norm_parts(resid)
    hidden_two = (normed_two * gain_two + shift_two.astype(jnp.float32)).astype(jnp.bfloat16)
    piece_gate = lax.all_gather(w_gate_up, "fsdp", axis=0, tiled=True)
    piece_down = lax.all_gather(w_down, "fsdp", axis=0, tiled=True)
    gate_up = jnp.einsum("td,ukd->tku", hidden_two, piece_gate, preferred_element_type=jnp.float32)
    hidden_piece = (jax.nn.silu(gate_up[:, 0]) * gate_up[:, 1]).astype(jnp.bfloat16)
    running = jnp.dot(hidden_piece, piece_down, preferred_element_type=jnp.float32)
    outputs = resid + running
    differ = outputs - teacher_in
    cot = counted[:, None] * differ
    half_sum = 0.5 * jnp.sum(cot * differ)
    count_here = jnp.sum(counted)
    cot_low = cot.astype(jnp.bfloat16)
    piece_gate = lax.all_gather(w_gate_up, "fsdp", axis=0, tiled=True)
    piece_down = lax.all_gather(w_down, "fsdp", axis=0, tiled=True)
    hidden_grad = jnp.einsum("tc,uc->tu", cot_low, piece_down, preferred_element_type=jnp.float32)
    piece_grads = gate_backward(gate_up, hidden_grad)
    grad_running = jnp.einsum(
        "tku,ukd->td", piece_grads, piece_gate, preferred_element_type=jnp.float32
    )

    def unit_rows(first_row, row_total):
        gate_term = jnp.einsum(
            "tku,td->ukd", piece_grads, hidden_two, preferred_element_type=jnp.float32
        )
        down_term = jnp.einsum(
            "tu,td->ud", hidden_piece, cot_low, preferred_element_type=jnp.float32
        )
        return jnp.concatenate([gate_term, down_term[:, None]], axis=1)

    ff_shard = reduce_rows(unit_rows, w_down.shape[0])
    resid_grad = cot + norm_back(grad_running, normed_two, inv_std_two, gain_two)
    gain_two_grad = jnp.sum(grad_running * normed_two, axis=0)
    shift_two_grad = jnp.sum(grad_running, axis=0)
    resid_low = resid_grad.astype(jnp.bfloat16)
    out_grad = jnp.einsum(
        "tc,ec->te", resid_low, full_out, preferred_element_type=jnp.float32
    ).astype(jnp.bfloat16)
    head_grad = lax.all_to_all(
        out_grad.reshape(row_count, seq_count, group_width),
        "seq",
        split_axis=1,
        concat_axis=0,
        tiled=True,
    )
    head_grad = head_grad.reshape(length_total, heads_here, HD)
    query_grad, key_grad, value_grad = attention_backward(
        query_rows, key_rows, value_rows, head_grad, log_totals, segment, block_size, score_scale
    )
    back_packed = jnp.stack(
        [
            rotate(query_grad, positions_all, -1.0),
            rotate(key_grad, positions_all, -1.0),
            value_grad,
        ],
        axis=1,
    )
    back_packed = back_packed.astype(jnp.bfloat16).reshape(length_total, 3, 1, group_width)
    qkv_grad = lax.all_to_all(back_packed, "seq", split_axis=0, concat_axis=2, tiled=True).reshape(
        row_count, 3 * model_width
    )
    grad_one = jnp.einsum("tc,ec->te", qkv_grad, full_qkv, preferred_element_type=jnp.float32)
    tokens_grad = resid_grad + norm_back(grad_one, normed_one, inv_std_one, gain_one)
    gain_one_grad = jnp.sum(grad_one * normed_one, axis=0)
    shift_one_grad = jnp.sum(grad_one, axis=0)
    bias_grad = jnp.sum(qkv_grad.astype(jnp.float32), axis=0)

    def feature_rows(first_row, row_total):
        qkv_term = jnp.einsum("tr,tc->rc", hidden_one, qkv_grad, preferred_element_type=jnp.float32)
        out_term = jnp.einsum("tr,tc->rc", attn_rows, resid_low, preferred_element_type=jnp.float32)
        return jnp.concatenate([qkv_term, out_term], axis=1)

    attn_shard = reduce_rows(feature_rows, w_qkv.shape[0])
    attn_total, ff_total = (
        lax.psum(attn_shard.astype(jnp.bfloat16), "seq").astype(jnp.float32),
        lax.psum(ff_shard.astype(jnp.bfloat16), "seq").astype(jnp.float32),
    )
    (
        sum_half,
        sum_count,
        total_gain_one,
        total_shift_one,
        total_gain_two,
        total_shift_two,
        total_bias,
    ) = lax.psum(
        (
            half_sum,
            count_here,
            gain_one_grad,
            shift_one_grad,
            gain_two_grad,
            shift_two_grad,
            bias_grad,
        ),
        ("seq", "fsdp"),
    )
    factor = tokens_total / sum_count
    loss = 2.0 * sum_half / (sum_count * model_width)

    def own_part(total_vec):
        share = total_vec.shape[0] // fsdp_count
        return factor * lax.dynamic_slice_in_dim(total_vec, fsdp_index * share, share, 0)

    layer_out = outputs.astype(jnp.bfloat16)[None]
    grad_tokens = (factor * tokens_grad).astype(jnp.bfloat16)[None]
    return (
        layer_out,
        loss,
        grad_tokens,
        own_part(total_gain_one),
        own_part(total_shift_one),
        factor * attn_total[:, : 3 * model_width],
        own_part(total_bias),
        factor * attn_total[:, 3 * model_width :],
        own_part(total_gain_two),
        own_part(total_shift_two),
        factor * ff_total[:, :2],
        factor * ff_total[:, 2],
    )


def solution(mesh):
    placed = (
        P("fsdp", "seq", None),
        P("fsdp", "seq", None),
        P("fsdp", None),
        P("fsdp", "seq"),
        P("fsdp"),
        P("fsdp"),
        P("fsdp", None),
        P("fsdp"),
        P("fsdp", None),
        P("fsdp"),
        P("fsdp"),
        P("fsdp", None, None),
        P("fsdp", None),
    )
    return jax.shard_map(
        per_device,
        mesh=mesh,
        in_specs=placed,
        out_specs=(
            P("fsdp", "seq", None),
            P(),
            P("fsdp", "seq", None),
            P("fsdp"),
            P("fsdp"),
            P("fsdp", None),
            P("fsdp"),
            P("fsdp", None),
            P("fsdp"),
            P("fsdp"),
            P("fsdp", None, None),
            P("fsdp", None),
        ),
        check_vma=False,
    )
```

profile of v0, /device:TPU:0, one launch (start us, length us, event | category | flops | bytes accessed | tf_op | source)
XLA Modules:
  0.0 4082.9 jit_solution(5188963605835579992)
XLA Ops:
  17.8 48.8 %all-gather.1 = bf16[8,1,256]{2,1,0:T(2,128)(2,1)S(1)} all-gather(bf16[1,1,256]{2,1,0:T(2,128)(2,1)S(1)} %reshape.465), channel_id=1, replica_groups=mesh['seq'=4,'fsdp'=8] {'fsdp'}, dimensions={0}, use_global_device_ids=true | all-gather | bytes 4608 | tf_op jit(solution)/shard_map/all_gather | solution.py:182
  66.6 30.9 all-gather
  97.5 39.9 all-gather.2
  139.2 354.2 %all-gather.10.cloned.1.call-done = bf16[2048,6144]{1,0:T(8,128)(2,1)} async-done(((bf16[256,6144]{1,0:T(8,128)(2,1)}), bf16[2048,6144]{1,0:T(8,128)(2,1)}) %all-gather.10.cloned.1.call-update) | async-done | bytes 25165840 | tf_op jit(solution)/shard_map/all_gather | solution.py:178
  493.4 13.4 convolution_add_fusion
  524.5 36.8 all-to-all-done
  575.3 37.4 while.27
  638.5 64.3 %all-gather.4 = bf16[8,1,256]{2,1,0:T(2,128)(2,1)S(1)} all-gather(bf16[1,1,256]{2,1,0:T(2,128)(2,1)S(1)} %reshape.471), channel_id=1, replica_groups=mesh['seq'=4,'fsdp'=8] {'fsdp'}, dimensions={0}, use_global_device_ids=true | all-gather | bytes 4608 | tf_op jit(solution)/shard_map/all_gather | solution.py:184
  702.8 30.6 all-gather.3
  745.9 748.3 %all-gather.14.cloned.1.call-done = bf16[5632,2,2048]{2,0,1:T(8,128)(2,1)} async-done(((bf16[704,2,2048]{2,0,1:T(8,128)(2,1)}), bf16[5632,2,2048]{2,0,1:T(8,128)(2,1)}) %all-gather.14.cloned.1.call-update) | async-done | bytes 46137360 | tf_op jit(solution)/shard_map/all_gather | solution.py:228
  1494.3 23.7 convolution_bitcast_fusion
  1524.3 412.4 %all-gather.16.cloned.1.call-done = bf16[5632,2048]{1,0:T(8,128)(2,1)} async-done(((bf16[704,2048]{1,0:T(8,128)(2,1)}), bf16[5632,2048]{1,0:T(8,128)(2,1)}) %all-gather.16.cloned.1.call-update) | async-done | bytes 23068688 | tf_op jit(solution)/shard_map/all_gather | solution.py:229
  1961.9 25.6 fusion.31
  1987.4 21.2 convert_bitcast_fusion
  2008.6 46.8 %pad_maximum_fusion = bf16[5632,3,2048]{0,2,1:T(8,128)(2,1)} fusion(bf16[5632,1,2048]{0,2,1:T(8,128)(2,1)} %convert_bitcast_fusion.1, bf16[5632,2,2048]{0,2,1:T(8,128)(2,1)} %convert_bitcast_fusion), kind=kLoop, calls=%fused_computation.40 | loop fusion | flops 34603008 | bytes 138412032 | tf_op jit(solution)/shard_map/concatenate | solution.py:254
  2055.4 88.8 %copy.142 = bf16[5632,6144]{1,0:T(8,128)(2,1)} copy(bf16[5632,6144]{0,1:T(8,128)(2,1)} %bitcast.64) | data formatting | bytes 138412032
  2144.3 22.0 multiply_reduce_fusion.1
  2181.6 13.5 all-to-all-done.2
  2197.4 154.1 %while.28 = (s32[]{:T(128)}, f32[1024,8,64]{0,2,1:T(8,128)}, f32[1024,8,64]{0,2,1:T(8,128)}, f32[2,512,8,64]{1,0,3,2:T(2,128)}, s32[2]{0:T(128)S(1)}, /*index=5*...) while((s32[]{:T(128)}, f32[1024,8,64]{0,2,1:T(8,128)}, ...), condition=%wide.region_18.19_spmd.clone, body=%wide.region_16.18_spmd.clone.sunk | while | flops 2726556160 | bytes 233929072 | solution.py:135
  2211.3 13.8 multiply_reduce_fusion.7
  2254.5 19.7 dynamic_update_slice.20
  2287.8 13.9 multiply_reduce_fusion.7
  2331.7 19.6 dynamic_update_slice.20
  2376.5 42.4 %all-to-all-done.3 = bf16[1024,3,1,512]{3,1,2,0:T(4,128)(2,1)} async-done(((bf16[1024,3,1,512]{3,1,2,0:T(4,128)(2,1)}), bf16[1024,3,1,512]{3,1,2,0:T(4,128)(2,1)}, u32[]{:S(2)}, u32[]{:S(2)}) %all-to-all-start.3) | async-done | bytes 3145760 | tf_op jit(solution)/shard_map/all_to_all | solution.py:284
  2428.5 14.3 convolution_convert_fusion
  2442.9 22.9 pad_maximum_fusion.1
  2465.8 764.0 %reduce-scatter.7.cloned.1.call-done = bf16[704,6144]{1,0:T(8,128)(2,1)} async-done(((bf16[5632,6144]{1,0:T(8,128)(2,1)}), bf16[704,6144]{1,0:T(8,128)(2,1)}) %reduce-scatter.7.cloned.1.call-update) | async-done | bytes 8650768
  3242.6 529.5 %reduce-scatter.5.cloned.1.call-done = bf16[256,8192]{1,0:T(8,128)(2,1)} async-done(((bf16[2048,8192]{1,0:T(8,128)(2,1)}), bf16[256,8192]{1,0:T(8,128)(2,1)}) %reduce-scatter.5.cloned.1.call-update) | async-done | bytes 4194320 | tf_op jit(solution)/shard_map/reduce_scatter | solution.py:142
  3776.4 15.2 fusion.49
  3791.6 41.5 %all-reduce = (f32[]{:T(128)}, f32[]{:T(128)}, f32[2048]{0:T(1024)S(1)}, f32[2048]{0:T(1024)S(1)}, f32[6144]{0:T(1024)S(1)}, /*index=5*/f32[2048]{0:T(1024)S(1)}, f32[2048]{0:T(1024)S(1)}) all-reduce(f32[]{:T(128)S(6)} %mul_shard_map.3, f32[]{:T(128)} %convert_reduce_fusion.2, ...), channel_id=1, replica_groups=mesh['seq'=4,'fsdp'=8] {'seq','fsdp'}, use_global_device_ids=true, to_apply=%region_11.12 | all-reduce | flops 14338 | bytes 114704 | tf_op jit(solution)/shard_map/psum | solution.py:311
  3841.8 171.7 %all-reduce.4.cloned.1.call-done = (bf16[256,8192]{1,0:T(8,128)(2,1)}, bf16[704,3,2048]{0,2,1:T(8,128)(2,1)}) async-done(((bf16[256,8192]{1,0:T(8,128)(2,1)}, bf16[704,3,2048]{0,2,1:T(8,128)(2,1)}), (bf16[256,8192]{1,0:T(8,128)(2,1)}, bf16[704,3,2048]{0,2,1:T(8,128)(2,1)})) %all-reduce.4.cloned.1.call-update) | async-done | bytes 12845072 | tf_op jit(solution)/shard_map/psum | solution.py:300
  4049.0 19.1 copy.132
  (260 shorter events, 346.7 us)
Async XLA Ops:
  7.2 486.2 %all-gather.10.cloned.1.call-start = ((), (), s32[]{:S(2)}) async-start(), calls=%async_computation.6 | async-start | bytes 28311552 | tf_op jit(solution)/shard_map/all_gather | solution.py:178
  7.9 731.3 %all-gather.12.cloned.1.call-start = ((), (), s32[]{:S(2)}) async-start(), calls=%async_computation.7 | async-start | bytes 9437184 | tf_op jit(solution)/shard_map/all_gather | solution.py:179
  8.7 1485.6 %all-gather.14.cloned.1.call-start = ((), (), s32[]{:S(2)}) async-start(), calls=%async_computation.8 | async-start | bytes 51904512 | tf_op jit(solution)/shard_map/all_gather | solution.py:228
  16.5 121.9 %copy-start.8 = (bf16[1,256,2048]{2,1,0:T(8,128)(2,1)S(1)}, bf16[1,256,2048]{2,1,0:T(8,128)(2,1)}, u32[]{:S(2)}) copy-start(bf16[1,256,2048]{2,1,0:T(8,128)(2,1)} %param.17) | copy-start | bytes 3145732
  16.6 1920.1 %all-gather.16.cloned.1.call-start = ((), (), s32[]{:S(2)}) async-start(), calls=%async_computation.9 | async-start | bytes 25952256 | tf_op jit(solution)/shard_map/all_gather | solution.py:229
  66.6 440.2 %copy-start.22 = (f32[8,1,256]{2,1,0:T(1,128)}, f32[8,1,256]{2,1,0:T(1,128)S(1)}, u32[]{:S(2)}) copy-start(f32[8,1,256]{2,1,0:T(1,128)S(1)} %convert_element_type.149) | copy-start | bytes 24580
  97.5 409.3 %copy-start.20 = (f32[8,1,256]{2,1,0:T(1,128)}, f32[8,1,256]{2,1,0:T(1,128)S(1)}, u32[]{:S(2)}) copy-start(f32[8,1,256]{2,1,0:T(1,128)S(1)} %convert_element_type.148) | copy-start | bytes 24580
  137.5 369.3 %copy-start.37 = (f32[8]{0:T(128)}, f32[8]{0:T(128)S(1)}, u32[]{:S(2)}) copy-start(f32[8]{0:T(128)S(1)} %multiply_power_fusion) | copy-start | bytes 100
  138.6 368.2 %copy-start.28 = (f32[256]{0:T(256)}, f32[256]{0:T(256)S(1)}, u32[]{:S(2)}) copy-start(f32[256]{0:T(256)S(1)} %broadcast_multiply_fusion.5) | copy-start | bytes 3076
  139.0 367.8 %copy-start.30 = (f32[256]{0:T(256)}, f32[256]{0:T(256)S(1)}, u32[]{:S(2)}) copy-start(f32[256]{0:T(256)S(1)} %add_rsqrt_fusion.1) | copy-start | bytes 3076
  520.6 40.8 all-to-all-start
  612.8 125.1 %copy-start.1 = (bf16[1024,8,64]{0,2,1:T(8,128)(2,1)}, bf16[1024,8,64]{0,2,1:T(8,128)(2,1)S(1)}, u32[]{:S(2)}) copy-start(bf16[1024,8,64]{0,2,1:T(8,128)(2,1)S(1)} %get-tuple-element.590) | copy-start | bytes 3145732
  623.0 15.5 copy-start.40
  634.8 98.6 %all-to-all-start.1 = ((bf16[4,2,65536]{2,1,0:T(2,128)(2,1)}), bf16[4,2,65536]{2,1,0:T(2,128)(2,1)S(1)}, u32[]{:S(2)}, u32[]{:S(2)}) async-start(bf16[4,2,65536]{2,1,0:T(2,128)(2,1)} %reshape.486), calls=%async_computation.1 | async-start | bytes 2097152 | tf_op jit(solution)/shard_map/all_to_all | solution.py:217
  638.4 2591.4 %reduce-scatter.7.cloned.1.call-start = ((), (), s32[]{:S(2)}) async-start(), calls=%async_computation.11 | async-start | bytes 77856768
  638.5 1298.2 %copy-start.35 = (f32[1,256]{1,0:T(1,128)}, f32[1,256]{1,0:T(1,128)S(1)}, u32[]{:S(2)}) copy-start(f32[1,256]{1,0:T(1,128)S(1)} %convert_element_type.133) | copy-start | bytes 3076
  1518.0 418.7 %copy-start.17 = (bf16[1,256,2048]{2,1,0:T(8,128)(2,1)S(1)}, bf16[1,256,2048]{2,1,0:T(8,128)(2,1)}, u32[]{:S(2)}) copy-start(bf16[1,256,2048]{2,1,0:T(8,128)(2,1)} %param.18) | copy-start | bytes 3145732
  2144.2 22.0 copy-start.14
  2144.2 22.0 copy-start.18
  2144.3 22.0 copy-start.36
  2177.1 20.3 copy-start.2
  2177.1 20.3 copy-start.16
  2177.1 20.3 copy-start.25
  2177.1 20.3 copy-start.47
  2177.1 18.1 all-to-all-start.2
  2225.1 15.9 copy-start
  2253.4 20.7 copy-start.3
  2301.7 15.8 copy-start
  2330.6 20.7 copy-start.3
  2365.6 53.3 %all-to-all-start.3 = ((bf16[1024,3,1,512]{3,1,2,0:T(4,128)(2,1)}), bf16[1024,3,1,512]{3,1,2,0:T(4,128)(2,1)}, u32[]{:S(2)}, u32[]{:S(2)}) async-start(bf16[1024,3,1,512]{3,1,2,0:T(4,128)(2,1)} %copy.126), calls=%async_computation.3 | async-start | bytes 8388608 | tf_op jit(solution)/shard_map/all_to_all | solution.py:284
  2370.7 1401.4 %reduce-scatter.5.cloned.1.call-start = ((), (), s32[]{:S(2)}) async-start(), calls=%async_computation.10 | async-start | bytes 37748736 | tf_op jit(solution)/shard_map/reduce_scatter | solution.py:142
  2465.8 1547.7 %all-reduce.4.cloned.1.call-start = ((), (), s32[]{:S(2)}) async-start(), calls=%async_computation.12 | async-start | bytes 27262976 | tf_op jit(solution)/shard_map/psum | solution.py:300
  (31 other events, 163.8 us)
Sparse Core Ops, SparseCore 0:
  9.5 483.8 all-gather.9
  495.5 124.4 all-gather.11
  622.1 872.0 all-gather.13
  1495.6 441.0 all-gather.15
  2144.4 1085.4 reduce-scatter.6
  3233.5 538.6 reduce-scatter.4
  3775.3 238.1 all-reduce.3
where the time goes:
time: 4100 us; the launch traced here: 4080 us
  waiting for transfers between devices  3070 us (75%)
  matrix products  270 us (7%)
  local copies, waits for them, and re-layouts  262 us (6%)
  blocking collectives  256 us (6%)
  other arithmetic  175 us (4%)
    unnamed x8, waiting for transfers between devices  766 us
    all_gather x1, waiting for transfers between devices, per_device(): piece_gate = lax.all_gather(w_gate_up, 'fsdp', axis=0, tiled=True)  748 us
    reduce_scatter x1, waiting for transfers between devices, reduce_rows(): lax.psum_scatter(term_rows(jnp.int32(0), row_share * lax.axis_size('fsdp'...  530 us
    all_gather x1, waiting for transfers between devices, per_device(): piece_down = lax.all_gather(w_down, 'fsdp', axis=0, tiled=True)  412 us
    all_gather x1, waiting for transfers between devices, per_device(): lax.all_gather(w_qkv, 'fsdp', axis=0, tiled=True)  354 us
    psum x1, waiting for transfers between devices, per_device(): lax.psum(attn_shard.astype(jnp.bfloat16), 'seq').astype(jnp.float32)  172 us
    unnamed x102, local copies, waits for them, and re-layouts  144 us
  transfers between devices with their start and end apart: 11, of which 9 were waited for; matrix products, arithmetic and copies ran while one was open for 10% of the time, Pallas kernels for 0%

commit v1 on v0

v1 whole, which is shorter than its diff:
```python
import functools

import jax
import jax.numpy as jnp
import numpy as np
from jax import lax
from jax.experimental import pallas as pl
from jax.experimental.pallas import tpu as pltpu
from jax.sharding import PartitionSpec as P

H = 32
HD = 64
ROT = 16
LANES = 128

EPSILON = 1e-05
MASKED_VALUE = -1e30

F32 = jnp.float32
BF16 = jnp.bfloat16
VMEM_LIMIT = 60 * 1024 * 1024

RING = (0, 2, 4, 6, 7, 5, 3, 1)
NEXT = [(RING[i], RING[(i + 1) % 8]) for i in range(8)]
PREV = [(RING[(i + 1) % 8], RING[i]) for i in range(8)]
ORDER = np.array([[RING[(RING.index(f) + j) % 8] for j in range(8)] for f in range(8)], np.int32)
CORE = [(s, s ^ 1) for s in range(4)]
ROW = [(s, s ^ 2) for s in range(4)]


def dot_nn(a, b):
    return lax.dot_general(a, b, (((1,), (0,)), ((), ())), preferred_element_type=F32)


def dot_nt(a, b):
    return lax.dot_general(a, b, (((1,), (1,)), ((), ())), preferred_element_type=F32)


def dot_tn(a, b):
    return lax.dot_general(a, b, (((0,), (0,)), ((), ())), preferred_element_type=F32)


def norm_parts(values):
    mean_value = jnp.mean(values, axis=-1, keepdims=True)
    centered = values - mean_value
    variance = jnp.mean(centered * centered, axis=-1, keepdims=True)
    inv_std = lax.rsqrt(variance + EPSILON)
    return (centered * inv_std, inv_std)


def norm_back(grad_out, normed, inv_std, gain_vec):
    scaled = grad_out * gain_vec
    mean_scaled = jnp.mean(scaled, axis=-1, keepdims=True)
    mean_cross = jnp.mean(scaled * normed, axis=-1, keepdims=True)
    return inv_std * (scaled - mean_scaled - normed * mean_cross)


def ring_gather(block, after=()):
    if after:
        block = lax.optimization_barrier((block,) + tuple(after))[0]
    half = block.shape[0] // 2
    blocks = [block] + [None] * 7
    ahead = behind = block
    for step in range(1, 4):
        ahead = lax.ppermute(ahead, "fsdp", NEXT)
        behind = lax.ppermute(behind, "fsdp", PREV)
        blocks[8 - step] = ahead
        blocks[step] = behind
    top = lax.ppermute(ahead[:half], "fsdp", NEXT)
    bottom = lax.ppermute(behind[half:], "fsdp", PREV)
    blocks[4] = (top, bottom)
    return blocks, (ahead, behind)


def ring_scatter(blocks):
    half = blocks[0].shape[0] // 2
    ahead = lax.ppermute(blocks[4][:half], "fsdp", NEXT)
    behind = lax.ppermute(blocks[4][half:], "fsdp", PREV)
    up, down = blocks[3].astype(F32), blocks[5].astype(F32)
    ahead = jnp.concatenate([up[:half] + ahead.astype(F32), up[half:]]).astype(BF16)
    behind = jnp.concatenate([down[:half], down[half:] + behind.astype(F32)]).astype(BF16)
    for step in (2, 1):
        ahead = lax.ppermute(ahead, "fsdp", NEXT)
        behind = lax.ppermute(behind, "fsdp", PREV)
        ahead = (blocks[step].astype(F32) + ahead.astype(F32)).astype(BF16)
        behind = (blocks[8 - step].astype(F32) + behind.astype(F32)).astype(BF16)
    ahead = lax.ppermute(ahead, "fsdp", NEXT)
    behind = lax.ppermute(behind, "fsdp", PREV)
    return blocks[0].astype(F32) + ahead.astype(F32) + behind.astype(F32)


def seq_gather(mine):
    over = lax.ppermute(mine, "seq", ROW)
    beside = lax.ppermute(mine, "seq", CORE)
    return [mine, beside, over, lax.ppermute(over, "seq", CORE)]


def seq_scatter(parts):
    corner = lax.ppermute(parts[3].astype(BF16), "seq", CORE)
    beside = lax.ppermute(parts[1].astype(BF16), "seq", CORE)
    far = (parts[2] + corner.astype(F32)).astype(BF16)
    over = lax.ppermute(far, "seq", ROW)
    return parts[0] + beside.astype(F32) + over.astype(F32)


class Fast:
    def __init__(self, s, f):
        self.s, self.f = s, f
        table = lax.dynamic_index_in_dim(jnp.asarray(ORDER), f, 0, keepdims=False)
        self.order = [table[j] for j in range(8)]
        self.slots = jnp.arange(4, dtype=jnp.int32) ^ s
        self.after = ()

    def weights(self, block):
        blocks, self.after = ring_gather(block, self.after)
        return blocks

    def weights_in_order(self, block):
        size = block.shape[0]
        blocks = self.weights(block)
        whole = jnp.zeros((8 * size, block.shape[1]), BF16)
        for j, part in enumerate(blocks):
            at = self.order[j] * size
            if j == 4:
                whole = lax.dynamic_update_slice(whole, part[0], (at, 0))
                whole = lax.dynamic_update_slice(whole, part[1], (at + size // 2, 0))
            else:
                whole = lax.dynamic_update_slice(whole, part, (at, 0))
        return whole

    def weights_as_found(self, block):
        blocks = self.weights(block)
        return jnp.concatenate(list(blocks[:4]) + list(blocks[4]) + list(blocks[5:]))

    def reduce_in_order(self, whole):
        size = whole.shape[0] // 8
        return ring_scatter(
            [lax.dynamic_slice_in_dim(whole, self.order[j] * size, size, 0) for j in range(8)]
        )

    def reduce_as_found(self, whole):
        size = whole.shape[0] // 8
        return ring_scatter([whole[j * size : (j + 1) * size] for j in range(8)])

    def pick_qkv(self, w_qkv):
        return pick_columns(w_qkv, self.s)

    def gather_out(self, w_out):
        rows = w_out.shape[0] // 4
        return self.weights_in_order(lax.dynamic_slice_in_dim(w_out, self.s * rows, rows, 0))

    def reduce_out(self, raw_out):
        return self.reduce_in_order(raw_out)

    def bias_of_heads(self, full_bias):
        split = full_bias.reshape(3, 4, 2, 4, HD)
        own = lax.dynamic_index_in_dim(split, self.s, 3, keepdims=False)
        return own.transpose(1, 0, 2, 3).reshape(1, 12 * LANES)

    def bias_of_all(self, own):
        split = own.reshape(4, 3, 2, HD).transpose(1, 0, 2, 3)
        here = (jnp.arange(4) == self.s).astype(F32)[None, None, None, :, None]
        return (split[:, :, :, None, :] * here).reshape(-1)

    def final_qkv(self, share, factor):
        return unpick_columns(seq_gather(share.astype(BF16)), self.s, factor)

    def final_rows(self, share, factor):
        return place_rows(seq_gather(share.astype(BF16)), self.s, factor)

    def final_out(self, share, factor):
        return self.final_rows(share, factor)

    def final_pairs(self, share, factor):
        return place_pairs(seq_gather(share.astype(BF16)), self.s, factor)

    def tokens(self, mine):
        return jnp.concatenate(seq_gather(mine))

    def tokens_sum(self, partial):
        rows = partial.shape[0] // 4
        return seq_scatter([partial[i * rows : (i + 1) * rows] for i in range(4)])

    def by_slot(self, values):
        split = values.reshape((4, values.shape[0] // 4) + values.shape[1:])
        return jnp.take(split, self.slots, axis=0).reshape(values.shape)

    def small_gather(self, mine):
        got = [mine] + [
            lax.ppermute(mine, "fsdp", [(i, (i + k) % 8) for i in range(8)]) for k in range(1, 8)
        ]
        return jnp.take(jnp.stack(got), (self.f - jnp.arange(8)) % 8, axis=0)

    def small_reduce(self, values):
        rolled = jnp.take(values, (self.f + jnp.arange(8)) % 8, axis=0)
        got = [rolled[0]] + [
            lax.ppermute(rolled[k], "fsdp", [(i, (i + k) % 8) for i in range(8)])
            for k in range(1, 8)
        ]
        total = jnp.sum(jnp.take(jnp.stack(got), (self.f - jnp.arange(8)) % 8, axis=0), axis=0)
        total = total + lax.ppermute(total, "seq", CORE)
        return total + lax.ppermute(total, "seq", ROW)


class General:
    def __init__(self, s, f):
        self.s, self.f = s, f
        self.members, self.shards = lax.axis_size("seq"), lax.axis_size("fsdp")
        self.slots = jnp.arange(self.members, dtype=jnp.int32)
        self.pairs = H // self.members // 2

    def weights_in_order(self, block):
        return lax.all_gather(block, "fsdp", axis=0, tiled=True)

    weights_as_found = weights_in_order

    def reduce_in_order(self, whole):
        return lax.psum_scatter(whole, "fsdp", scatter_dimension=0, tiled=True).astype(F32)

    reduce_as_found = reduce_in_order

    def pick_qkv(self, w_qkv):
        split = w_qkv.reshape(w_qkv.shape[0], 3, self.members, self.pairs, LANES)
        own = lax.dynamic_index_in_dim(split, self.s, 2, keepdims=False)
        return own.transpose(0, 2, 1, 3).reshape(w_qkv.shape[0], -1)

    def gather_out(self, w_out):
        rows = w_out.shape[0] * self.shards // self.members
        return lax.dynamic_slice_in_dim(self.weights_in_order(w_out), self.s * rows, rows, 0)

    def reduce_out(self, raw_out):
        rows = raw_out.shape[0]
        whole = jnp.zeros((rows * self.members, raw_out.shape[1]), raw_out.dtype)
        whole = lax.dynamic_update_slice(whole, raw_out, (self.s * rows, 0))
        return self.reduce_in_order(whole)

    def bias_of_heads(self, full_bias):
        split = full_bias.reshape(3, self.members, self.pairs, LANES)
        own = lax.dynamic_index_in_dim(split, self.s, 1, keepdims=False)
        return own.transpose(1, 0, 2).reshape(1, -1)

    def bias_of_all(self, own):
        split = own.reshape(self.pairs, 3, LANES).transpose(1, 0, 2)
        here = (jnp.arange(self.members) == self.s).astype(F32)[None, :, None, None]
        return (split[:, None] * here).reshape(-1)

    def gathered(self, share):
        return lax.all_gather(share.astype(BF16), "seq", axis=0, tiled=False)

    def final_qkv(self, share, factor):
        parts = self.gathered(share).reshape(self.members, -1, self.pairs, 3, LANES)
        return factor * parts.transpose(1, 3, 0, 2, 4).reshape(parts.shape[1], -1).astype(F32)

    def final_rows(self, share, factor):
        return factor * self.gathered(share).reshape(-1, share.shape[1]).astype(F32)

    def final_out(self, share, factor):
        return factor * lax.psum(share.astype(BF16), "seq").astype(F32)

    def final_pairs(self, share, factor):
        parts = self.gathered(share).reshape(self.members, 2, -1, share.shape[1])
        return factor * parts.transpose(0, 2, 1, 3).reshape(-1, 2, share.shape[1]).astype(F32)

    def tokens(self, mine):
        return lax.all_gather(mine, "seq", axis=0, tiled=True)

    def tokens_sum(self, partial):
        return lax.psum_scatter(partial.astype(BF16), "seq", scatter_dimension=0, tiled=True).astype(
            F32
        )

    def by_slot(self, values):
        return values

    def small_gather(self, mine):
        return lax.all_gather(mine, "fsdp", axis=0, tiled=False)

    def small_reduce(self, values):
        total = lax.psum(values, ("seq", "fsdp"))
        return lax.dynamic_index_in_dim(total, self.f, 0, keepdims=False)


def call(kernel, grid, in_specs, out_specs, out_shape, scratch=(), prefetch=0, cost=None):
    return pl.pallas_call(
        kernel,
        grid_spec=pltpu.PrefetchScalarGridSpec(
            num_scalar_prefetch=prefetch,
            grid=grid,
            in_specs=in_specs,
            out_specs=out_specs,
            scratch_shapes=list(scratch),
        ),
        out_shape=out_shape,
        compiler_params=pltpu.CompilerParams(vmem_limit_bytes=VMEM_LIMIT),
        cost_estimate=cost,
    )


def pick_matrix(member, rows, cols, turned):
    lane = lax.broadcasted_iota(jnp.int32, (rows, cols), 0 if turned else 1)
    place = lax.broadcasted_iota(jnp.int32, (rows, cols), 1 if turned else 0)
    source = jnp.where(lane < HD, lane, lane + (256 - HD)) + member * HD
    return jnp.where(place == source, 1.0, 0.0).astype(BF16)


def pick_kernel(s_ref, w_ref, out_ref):
    out_ref[...] = dot_nn(w_ref[...], pick_matrix(s_ref[0], 512, LANES, False)).astype(BF16)


def pick_columns(w_qkv, s):
    rows = w_qkv.shape[0]
    return call(
        pick_kernel,
        (12,),
        [pl.BlockSpec((rows, 512), lambda g, s_ref: (0, (g % 3) * 4 + g // 3))],
        pl.BlockSpec((rows, LANES), lambda g, s_ref: (0, g)),
        jax.ShapeDtypeStruct((rows, 12 * LANES), BF16),
        prefetch=1,
    )(s.reshape(1), w_qkv)


def unpick_kernel(s_ref, factor_ref, p0, p1, p2, p3, out_ref):
    total = None
    for r, part in enumerate((p0, p1, p2, p3)):
        term = dot_nn(part[...], pick_matrix(s_ref[0] ^ r, LANES, 512, True))
        total = term if total is None else total + term
    out_ref[...] = total * factor_ref[0]


def unpick_columns(parts, s, factor):
    rows = parts[0].shape[0]
    return call(
        unpick_kernel,
        (12,),
        [pl.BlockSpec(memory_space=pltpu.SMEM)]
        + [pl.BlockSpec((rows, LANES), lambda g, s_ref: (0, g))] * 4,
        pl.BlockSpec((rows, 512), lambda g, s_ref: (0, (g % 3) * 4 + g // 3)),
        jax.ShapeDtypeStruct((rows, 12 * 512), F32),
        prefetch=1,
    )(s.reshape(1), factor.reshape(1), *parts)


def place_kernel(s_ref, factor_ref, p0, p1, p2, p3, out_ref):
    r = pl.program_id(0)
    for k, part in enumerate((p0, p1, p2, p3)):

        @pl.when(r == k)
        def _(part=part):
            out_ref[...] = part[...].astype(F32) * factor_ref[0]


def place_rows(parts, s, factor):
    rows, cols = parts[0].shape
    return call(
        place_kernel,
        (4,),
        [pl.BlockSpec(memory_space=pltpu.SMEM)]
        + [pl.BlockSpec((rows, cols), lambda r, s_ref: (0, 0))] * 4,
        pl.BlockSpec((rows, cols), lambda r, s_ref: (s_ref[0] ^ r, 0)),
        jax.ShapeDtypeStruct((4 * rows, cols), F32),
        prefetch=1,
    )(s.reshape(1), factor.reshape(1), *parts)


def place_pair_kernel(s_ref, factor_ref, p0, p1, p2, p3, out_ref):
    r = pl.program_id(0)
    rows = out_ref.shape[0]
    for k, part in enumerate((p0, p1, p2, p3)):

        @pl.when(r == k)
        def _(part=part):
            out_ref[:, 0, :] = part[:rows].astype(F32) * factor_ref[0]
            out_ref[:, 1, :] = part[rows:].astype(F32) * factor_ref[0]


def place_pairs(parts, s, factor):
    rows, cols = parts[0].shape
    rows = rows // 2
    return call(
        place_pair_kernel,
        (4,),
        [pl.BlockSpec(memory_space=pltpu.SMEM)]
        + [pl.BlockSpec((2 * rows, cols), lambda r, s_ref: (0, 0))] * 4,
        pl.BlockSpec((rows, 2, cols), lambda r, s_ref: (s_ref[0] ^ r, 0, 0)),
        jax.ShapeDtypeStruct((4 * rows, 2, cols), F32),
        prefetch=1,
    )(s.reshape(1), factor.reshape(1), *parts)


def turn(values, cosine, sine_low, sine_high, sign):
    half = ROT // 2
    moved = (
        pltpu.roll(values, LANES - half, 1) * sine_low + pltpu.roll(values, half, 1) * sine_high
    )
    return values * cosine + moved if sign > 0 else values * cosine - moved


def two_heads(values):
    lane = lax.broadcasted_iota(jnp.int32, values.shape, 1)
    nothing = jnp.zeros_like(values)
    return jnp.concatenate(
        [jnp.where(lane < HD, values, nothing), jnp.where(lane < HD, nothing, values)], axis=0
    )


def one_pair(stacked):
    rows = stacked.shape[0] // 2
    lane = lax.broadcasted_iota(jnp.int32, (rows, LANES), 1)
    return jnp.where(lane < HD, stacked[:rows], stacked[rows:])


def forward_kernel(
    block, slots, slot_ref, first_ref, qkv, bias, cosine, low, high, start, turned, out
):
    scale = HD ** (-0.5)

    def rotate_block(i, unused):
        rows = pl.ds(pl.multiple_of(i * block, block), block)
        tables = (cosine[rows, :], low[rows, :], high[rows, :], 1)
        query = qkv[rows, 0:LANES] + bias[:, 0:LANES]
        key = qkv[rows, LANES : 2 * LANES] + bias[:, LANES : 2 * LANES]
        value = qkv[rows, 2 * LANES : 3 * LANES] + bias[:, 2 * LANES : 3 * LANES]
        turned[rows, 0:LANES] = turn(query, *tables).astype(BF16)
        turned[rows, LANES : 2 * LANES] = turn(key, *tables).astype(BF16)
        turned[rows, 2 * LANES : 3 * LANES] = value.astype(BF16)
        return unused

    lax.fori_loop(0, slots, rotate_block, 0)

    column = lax.broadcasted_iota(jnp.int32, (2 * block, block), 1)
    line = lax.broadcasted_iota(jnp.int32, (2 * block, block), 0) & (block - 1)

    def query_block(i, unused):
        rows = pl.ds(pl.multiple_of(slot_ref[i] * block, block), block)
        query = two_heads((turned[rows, 0:LANES].astype(F32) * scale).astype(BF16))
        first = start[rows, :]
        first = jnp.concatenate([first, first], axis=0)

        def scores(j):
            keys = pl.ds(pl.multiple_of(slot_ref[j] * block, block), block)
            result = dot_nt(query, turned[keys, LANES : 2 * LANES])
            allowed = column >= first - j * block
            return result, allowed, turned[keys, 2 * LANES : 3 * LANES]

        result, allowed, value = scores(i)
        result = jnp.where(allowed & (column <= line), result, MASKED_VALUE)
        peak = jnp.max(result, axis=1, keepdims=True)
        weight = jnp.exp(result - peak)
        total = jnp.sum(weight, axis=1, keepdims=True)
        gathered = dot_nn(weight.astype(BF16), value)

        def key_block(j, carry):
            peak, total, gathered = carry
            result, allowed, value = scores(j)
            result = jnp.where(allowed, result, MASKED_VALUE)
            higher = jnp.maximum(peak, jnp.max(result, axis=1, keepdims=True))
            shrink = jnp.exp(peak - higher)
            weight = jnp.exp(result - higher)
            total = total * shrink + jnp.sum(weight, axis=1, keepdims=True)
            gathered = gathered * shrink + dot_nn(weight.astype(BF16), value)
            return higher, total, gathered

        peak, total, gathered = lax.fori_loop(first_ref[i], i, key_block, (peak, total, gathered))
        out[rows, :] = one_pair(gathered / total).astype(BF16)
        return unused

    lax.fori_loop(0, slots, query_block, 0)


def attention_forward(qkv, bias, tables, start, slot_of, first_slot, block):
    length, width = qkv.shape
    pairs = width // (3 * LANES)
    slots = length // block
    whole = pl.BlockSpec((length, LANES), lambda p, *_: (0, 0))
    return call(
        functools.partial(forward_kernel, block, slots),
        (pairs,),
        [
            pl.BlockSpec((length, 3 * LANES), lambda p, *_: (0, p)),
            pl.BlockSpec((1, 3 * LANES), lambda p, *_: (0, p)),
            whole,
            whole,
            whole,
            pl.BlockSpec((length, 1), lambda p, *_: (0, 0)),
        ],
        [
            pl.BlockSpec((length, 3 * LANES), lambda p, *_: (0, p)),
            pl.BlockSpec((length, LANES), lambda p, *_: (0, p)),
        ],
        [
            jax.ShapeDtypeStruct((length, width), BF16),
            jax.ShapeDtypeStruct((length, width // 3), BF16),
        ],
        prefetch=2,
        cost=pl.CostEstimate(
            flops=length * length * width * 2,
            bytes_accessed=length * width * 8,
            transcendentals=length * length * width // (3 * HD),
        ),
    )(slot_of, first_slot, qkv, bias, *tables, start)


def backward_kernel(
    block,
    slots,
    slot_ref,
    first_ref,
    turned,
    out_grad,
    cosine,
    low,
    high,
    start,
    grads,
    key_sum,
    value_sum,
    weights,
    products,
):
    scale = HD ** (-0.5)
    key_sum[...] = jnp.zeros_like(key_sum)
    value_sum[...] = jnp.zeros_like(value_sum)
    column = lax.broadcasted_iota(jnp.int32, (block, 2 * block), 1) & (block - 1)
    line = lax.broadcasted_iota(jnp.int32, (block, 2 * block), 0)

    def query_block(i, unused):
        begin = pl.multiple_of(slot_ref[i] * block, block)
        rows = pl.ds(begin, block)
        query = two_heads((turned[rows, 0:LANES].astype(F32) * scale).astype(BF16))
        grad = two_heads(out_grad[rows, :])
        first = start[:, pl.ds(begin, block)]
        first = jnp.concatenate([first, first], axis=1)

        def scores(j):
            keys = pl.ds(pl.multiple_of(slot_ref[j] * block, block), block)
            result = dot_nt(turned[keys, LANES : 2 * LANES], query)
            return result, line >= first - j * block

        result, allowed = scores(i)
        result = jnp.where(allowed & (line <= column), result, MASKED_VALUE)
        weights[0] = result
        peak = jnp.max(result, axis=0, keepdims=True)

        def score_block(j, peak):
            result, allowed = scores(j)
            result = jnp.where(allowed, result, MASKED_VALUE)
            weights[i - j] = result
            return jnp.maximum(peak, jnp.max(result, axis=0, keepdims=True))

        peak = lax.fori_loop(first_ref[i], i, score_block, peak)

        def weight_block(j, carry):
            total, cross = carry
            keys = pl.ds(pl.multiple_of(slot_ref[j] * block, block), block)
            weight = jnp.exp(weights[i - j] - peak)
            product = dot_nt(turned[keys, 2 * LANES : 3 * LANES], grad)
            weights[i - j] = weight
            products[i - j] = product
            total = total + jnp.sum(weight, axis=0, keepdims=True)
            cross = cross + jnp.sum(weight * product, axis=0, keepdims=True)
            return total, cross

        zero = jnp.zeros((1, 2 * block), F32)
        total, cross = lax.fori_loop(first_ref[i], i + 1, weight_block, (zero, zero))
        share = 1.0 / total
        cross = cross * share

        def grad_block(j, query_sum):
            keys = pl.ds(pl.multiple_of(slot_ref[j] * block, block), block)
            weight = weights[i - j] * share
            score_grad = (weight * (products[i - j] - cross)).astype(BF16)
            value_sum[keys, :] += dot_nn(weight.astype(BF16), grad)
            key_sum[keys, :] += dot_nn(score_grad, query)
            return query_sum + dot_tn(score_grad, turned[keys, LANES : 2 * LANES])

        query_sum = lax.fori_loop(
            first_ref[i], i + 1, grad_block, jnp.zeros((2 * block, LANES), F32)
        )
        tables = (cosine[rows, :], low[rows, :], high[rows, :], -1)
        grads[rows, 0:LANES] = turn(one_pair(query_sum) * scale, *tables).astype(BF16)
        return unused

    lax.fori_loop(0, slots, query_block, 0)

    def finish(i, unused):
        rows = pl.ds(pl.multiple_of(i * block, block), block)
        tables = (cosine[rows, :], low[rows, :], high[rows, :], -1)
        grads[rows, LANES : 2 * LANES] = turn(key_sum[rows, :], *tables).astype(BF16)
        grads[rows, 2 * LANES : 3 * LANES] = value_sum[rows, :].astype(BF16)
        return unused

    lax.fori_loop(0, slots, finish, 0)


def attention_backward(turned, out_grad, tables, start, slot_of, first_slot, block):
    length, width = turned.shape
    pairs = width // (3 * LANES)
    slots = length // block
    whole = pl.BlockSpec((length, LANES), lambda p, *_: (0, 0))
    return call(
        functools.partial(backward_kernel, block, slots),
        (pairs,),
        [
            pl.BlockSpec((length, 3 * LANES), lambda p, *_: (0, p)),
            pl.BlockSpec((length, LANES), lambda p, *_: (0, p)),
            whole,
            whole,
            whole,
            pl.BlockSpec((1, length), lambda p, *_: (0, 0)),
        ],
        pl.BlockSpec((length, 3 * LANES), lambda p, *_: (0, p)),
        jax.ShapeDtypeStruct((length, width), BF16),
        scratch=[
            pltpu.VMEM((length, LANES), F32),
            pltpu.VMEM((length, LANES), F32),
            pltpu.VMEM((slots, block, 2 * block), F32),
            pltpu.VMEM((slots, block, 2 * block), F32),
        ],
        prefetch=2,
        cost=pl.CostEstimate(
            flops=length * length * width * 5,
            bytes_accessed=length * width * 6,
            transcendentals=length * length * width // (3 * HD),
        ),
    )(slot_of, first_slot, turned, out_grad, *tables, start)


def doc_starts(segment):
    places = jnp.arange(segment.shape[0], dtype=jnp.int32)
    change = jnp.concatenate([jnp.ones((1,), dtype=bool), segment[1:] != segment[:-1]])
    return lax.cummax(jnp.where(change, places, 0), axis=0)


def turn_tables(positions):
    half = ROT // 2
    inverse = 10000.0 ** (-(jnp.arange(half, dtype=F32) * 2.0) / ROT)
    angles = inverse[:, None] * positions.astype(F32)[None, :]
    cosine, sine = jnp.cos(angles).T, jnp.sin(angles).T
    length = positions.shape[0]
    rest = jnp.zeros((length, HD - ROT), F32)
    none = jnp.zeros_like(sine)

    def twice(*pieces):
        return jnp.concatenate(pieces * 2, axis=1)

    return (
        twice(cosine, cosine, rest + 1.0),
        twice(-sine, none, rest),
        twice(none, sine, rest),
    )


def per_device(
    tokens,
    teacher,
    segments,
    valid,
    ln1_gain,
    ln1_bias,
    w_qkv,
    b_qkv,
    w_out,
    ln2_gain,
    ln2_bias,
    w_gate_up,
    w_down,
):
    s = lax.axis_index("seq")
    f = lax.axis_index("fsdp")
    members, shards = lax.axis_size("seq"), lax.axis_size("fsdp")
    net = (Fast if (members, shards) == (4, 8) else General)(s, f)
    rows = tokens.shape[1]
    width = tokens.shape[2]
    length = segments.shape[1]
    units = w_down.shape[0] // members
    vec = ln1_gain.shape[0]
    bias_share = b_qkv.shape[0]

    mine_gate_up = lax.dynamic_slice_in_dim(w_gate_up, s * units, units, 0)
    mine_gate_up = jnp.concatenate([mine_gate_up[:, 0], mine_gate_up[:, 1]])
    mine_down = lax.dynamic_slice_in_dim(w_down, s * units, units, 0)

    small = jnp.concatenate([ln1_gain, ln1_bias, ln2_gain, ln2_bias, b_qkv])
    small = net.small_gather(small.reshape(-1, LANES).astype(F32))
    small = small.reshape(shards, 4 * vec + bias_share)
    gain_one, shift_one, gain_two, shift_two = (
        small[:, i * vec : (i + 1) * vec].reshape(width) for i in range(4)
    )
    own_bias = net.bias_of_heads(small[:, 4 * vec :].reshape(-1))

    tokens_all = net.tokens(tokens[0])
    full_qkv = net.weights_in_order(net.pick_qkv(w_qkv))
    full_out = net.gather_out(w_out)
    full_gate_up = net.weights_as_found(mine_gate_up)
    full_down = net.weights_as_found(mine_down)

    starts = doc_starts(segments[0])
    positions = jnp.arange(length, dtype=jnp.int32) - starts
    first_slot = starts.reshape(members, rows)[:, 0] // rows
    slot_start = net.by_slot(starts)
    tables = turn_tables(net.by_slot(positions))

    normed_all, unused = norm_parts(tokens_all.astype(F32))
    hidden_one = (normed_all * gain_one + shift_one).astype(BF16)
    qkv = dot_nn(hidden_one, full_qkv)
    turned, heads_out = attention_forward(
        qkv, own_bias, tables, slot_start[:, None], net.slots, first_slot, rows
    )
    tokens_in = tokens[0].astype(F32)
    resid = tokens_in + net.tokens_sum(dot_nn(heads_out, full_out))

    normed_two, inv_std_two = norm_parts(resid)
    hidden_two = net.tokens((normed_two * gain_two + shift_two).astype(BF16))
    gate_up = dot_nt(full_gate_up, hidden_two).reshape(shards, 2, units, length)
    gate, up = gate_up[:, 0], gate_up[:, 1]
    hidden = (jax.nn.silu(gate) * up).astype(BF16).reshape(shards * units, length)
    outputs = resid + net.tokens_sum(dot_tn(hidden, full_down))
    counted = valid[0].astype(F32)
    differ = outputs - teacher[0].astype(F32)
    cot = counted[:, None] * differ
    half_sum = 0.5 * jnp.sum(cot * differ)
    count_here = jnp.sum(counted)
    cot_low = net.tokens(cot.astype(BF16))

    raw_down = dot_nn(hidden, cot_low).astype(BF16)
    sum_down = net.reduce_as_found(raw_down)
    hidden_grad = dot_nt(full_down, cot_low).reshape(shards, units, length)
    sigma = jax.nn.sigmoid(gate)
    silu_grad = hidden_grad * up
    gate_grad = silu_grad * sigma + silu_grad * gate * sigma * (1.0 - sigma)
    up_grad = hidden_grad * (gate * sigma)
    grads = jnp.stack([gate_grad, up_grad], axis=1).astype(BF16).reshape(2 * shards * units, length)
    two_grad = net.tokens_sum(dot_tn(grads, full_gate_up))
    raw_gate_up = dot_nn(grads, hidden_two).astype(BF16)
    sum_gate_up = net.reduce_as_found(raw_gate_up)
    resid_grad = cot + norm_back(two_grad, normed_two, inv_std_two, gain_two)
    gain_two_grad = jnp.sum(two_grad * normed_two, axis=0)
    shift_two_grad = jnp.sum(two_grad, axis=0)
    resid_low = net.tokens(resid_grad.astype(BF16))

    out_grad = dot_nt(resid_low, full_out).astype(BF16)
    raw_out = dot_tn(heads_out, resid_low).astype(BF16)
    sum_out = net.reduce_out(raw_out)
    qkv_grad = attention_backward(
        turned, out_grad, tables, slot_start[None, :], net.slots, first_slot, rows
    )
    grad_one = net.tokens_sum(dot_nt(qkv_grad, full_qkv))
    raw_qkv = dot_tn(hidden_one, qkv_grad).astype(BF16)
    sum_qkv = net.reduce_in_order(raw_qkv)
    normed_one, inv_std_one = norm_parts(tokens_in)
    tokens_grad = resid_grad + norm_back(grad_one, normed_one, inv_std_one, gain_one)
    gain_one_grad = jnp.sum(grad_one * normed_one, axis=0)
    shift_one_grad = jnp.sum(grad_one, axis=0)

    bias_grad = net.bias_of_all(jnp.sum(qkv_grad.astype(F32), axis=0)).reshape(shards, -1)

    vectors = jnp.concatenate(
        [
            v.reshape(shards, vec)
            for v in (gain_one_grad, shift_one_grad, gain_two_grad, shift_two_grad)
        ]
        + [
            bias_grad,
            jnp.full((shards, LANES), half_sum),
            jnp.full((shards, LANES), count_here),
        ],
        axis=1,
    )
    vectors = net.small_reduce(vectors.reshape(shards, -1, LANES)).reshape(-1)
    sum_half = vectors[4 * vec + bias_share]
    sum_count = vectors[4 * vec + bias_share + LANES]
    factor = (rows * members * shards) / sum_count
    loss = 2.0 * sum_half / (sum_count * width)
    scaled = factor * vectors

    return (
        outputs.astype(BF16)[None],
        loss,
        (factor * tokens_grad).astype(BF16)[None],
        scaled[:vec],
        scaled[vec : 2 * vec],
        net.final_qkv(sum_qkv, factor),
        scaled[4 * vec : 4 * vec + bias_share],
        net.final_out(sum_out, factor),
        scaled[2 * vec : 3 * vec],
        scaled[3 * vec : 4 * vec],
        net.final_pairs(sum_gate_up, factor),
        net.final_rows(sum_down, factor),
    )


def solution(mesh):
    placed = (
        P("fsdp", "seq", None),
        P("fsdp", "seq", None),
        P("fsdp", None),
        P("fsdp", "seq"),
        P("fsdp"),
        P("fsdp"),
        P("fsdp", None),
        P("fsdp"),
        P("fsdp", None),
        P("fsdp"),
        P("fsdp"),
        P("fsdp", None, None),
        P("fsdp", None),
    )
    return jax.shard_map(
        per_device,
        mesh=mesh,
        in_specs=placed,
        out_specs=(
            P("fsdp", "seq", None),
            P(),
            P("fsdp", "seq", None),
            P("fsdp"),
            P("fsdp"),
            P("fsdp", None),
            P("fsdp"),
            P("fsdp", None),
            P("fsdp"),
            P("fsdp"),
            P("fsdp", None, None),
            P("fsdp", None),
        ),
        check_vma=False,
    )
```

time: 4100 us -> 972 us (0.24)
  waiting for transfers between devices: 3070 us -> 418 us
  blocking collectives: 256 us -> 0 us
  local copies, waits for them, and re-layouts: 262 us -> 96.2 us
  matrix products: 270 us -> 133 us
  Pallas kernels: 0 us -> 101 us
  starting transfers between devices: 16.5 us -> 108 us
  other arithmetic: 175 us -> 89.9 us
    all_gather x4 -> x0, waiting for transfers between devices: 1510 us -> none  [the longest x1 748 us: per_device(): piece_gate = lax.all_gather(w_gate_up, 'fsdp', axis=0, tiled=True)]
    unnamed x8 -> x0, waiting for transfers between devices: 766 us -> none
    reduce_scatter x1 -> x0, waiting for transfers between devices: 530 us -> none  [reduce_rows(): lax.psum_scatter(term_rows(jnp.int32(0), row_share * lax.axis_size('fsdp'...]
    ppermute x0 -> x116, waiting for transfers between devices: none -> 418 us  [the longest x12 103 us: ring_scatter(): ahead = lax.ppermute(ahead, 'fsdp', NEXT)]
    all_gather x5 -> x0, blocking collectives: 215 us -> none  [the longest x1 64.3 us: per_device(): lax.all_gather(ln2_bias, 'fsdp', axis=0, tiled=True)]
    psum x1 -> x0, waiting for transfers between devices: 172 us -> none  [per_device(): lax.psum(attn_shard.astype(jnp.bfloat16), 'seq').astype(jnp.float32)]
    dot_general x26 -> x12, matrix products: 270 us -> 133 us  [the longest x4 48.6 us: dot_nt(): lax.dot_general(a, b, (((1,), (1,)), ((), ())), preferred_element_type=F32)]
    unnamed x102 -> x176, local copies, waits for them, and re-layouts: 144 us -> 24.8 us
  transfers between devices with their start and end apart: 11 -> 116, of which waited for: 9 -> 46; matrix products, arithmetic and copies ran while one was open for 10% -> 29% of each run, Pallas kernels for 0% -> 9%
where the time goes in v1:
time: 972 us; the launch traced here: 962 us
  waiting for transfers between devices  418 us (43%)
  matrix products  133 us (14%)
  starting transfers between devices  108 us (11%)
  Pallas kernels  101 us (10%)
  local copies, waits for them, and re-layouts  96.2 us (10%)
  other arithmetic  89.9 us (9%)
  between operations  16.4 us (2%)
    ppermute x12, waiting for transfers between devices, ring_scatter(): ahead = lax.ppermute(ahead, 'fsdp', NEXT)  103 us
    ppermute x12, waiting for transfers between devices, ring_gather(): behind = lax.ppermute(behind, 'fsdp', PREV)  96 us
    dot_general x4, matrix products, dot_nt(): lax.dot_general(a, b, (((1,), (1,)), ((), ())), preferred_element_type=F32)  48.6 us
    dot_general x4, matrix products, dot_tn(): lax.dot_general(a, b, (((0,), (0,)), ((), ())), preferred_element_type=F32)  42.5 us
    dot_general x4, matrix products, dot_nn(): lax.dot_general(a, b, (((1,), (0,)), ((), ())), preferred_element_type=F32)  41.6 us
    pallas_call x1, Pallas kernels, attention_backward(): call(functools.partial(backward_kernel, block, slots), (pairs,), [pl.Bloc...  37.1 us
    ppermute x8, waiting for transfers between devices, seq_gather(): over = lax.ppermute(mine, 'seq', ROW)  36.8 us
    ppermute x4, waiting for transfers between devices, ring_gather(): top = lax.ppermute(ahead[:half], 'fsdp', NEXT)  35.2 us
  transfers between devices with their start and end apart: 116, of which 46 were waited for; matrix products, arithmetic and copies ran while one was open for 29% of the time, Pallas kernels for 9%

profile of v1, /device:TPU:0, one launch (start us, length us, event | category | flops | bytes accessed | tf_op | source)
XLA Modules:
  0.0 961.9 jit_solution(10351261324850396933)
XLA Ops:
  0.7 8.7 shard_map.229
  79.6 14.0 %collective-permute-done.1 = bf16[256,2048]{1,0:T(8,128)(2,1)} collective-permute-done((bf16[256,2048]{1,0:T(8,128)(2,1)}, bf16[256,2048]{1,0:T(8,128)(2,1)}, u32[]{:S(2)}, u32[]{:S(2)}) %collective-permute-start.1) | collective-permute-done | bytes 1048608 | tf_op jit(solution)/shard_map/ppermute | solution.py:93
  106.7 10.1 %collective-permute-done.12 = bf16[256,1536]{1,0:T(8,128)(2,1)S(1)} collective-permute-done((bf16[256,1536]{1,0:T(8,128)(2,1)}, bf16[256,1536]{1,0:T(8,128)(2,1)S(1)}, u32[]{:S(2)}, u32[]{:S(2)}) %collective-permute-start.12) | collective-permute-done | bytes 786464 | tf_op jit(solution)/shard_map/ppermute | solution.py:66
  137.6 12.8 %fusion.49.qkv = f32[1024,1536]{1,0:T(8,128)} fusion(bf16[2048,1536]{1,0:T(8,128)(2,1)S(1)} %constant_dynamic-update-slice_fusion.50, f32[2048]{0:T(1024)S(1)} %bitcast.219, f32[2048]{0:T(1024)S(1)} %bitcast.207, f32[1024]{0:T(1024)S(1)} %add_rsqrt_fusion, f32[1024]{0:T(1024)S(1)} %broadcast_multiply_fusion.2, ...), kind=kOutput, calls=%fused_computation.278 | convolution fusion | flops 6469713920 | bytes 16801792 | tf_op jit(solution)/shard_map/dot_general | solution.py:32
  152.6 28.0 %shard_map.230 = (bf16[1024,1536]{1,0:T(8,128)(2,1)}, bf16[1024,512]{1,0:T(8,128)(2,1)}) custom-call(s32[4]{0:T(128)} %iota_xor_fusion.slot_ref, s32[4]{0:T(128)} %and_select_fusion.3.first_ref, f32[1024,1536]{1,0:T(8,128)} %fusion.49.qkv, f32[1,1536]{1,0:T(1,128)} %reshape.336.bias, f32[1024,128]{1,0:T(8,128)} %concatenate.77.cosine, ...), custom_call_target="tpu_custom_call" | custom-call | flops 3221225472 | bytes 12582912 | tf_op jit(solution)/shard_map/pallas_call | solution.py:475
  205.6 28.6 %collective-permute-done.29 = bf16[352,2048]{1,0:T(8,128)(2,1)S(1)} collective-permute-done((bf16[352,2048]{1,0:T(8,128)(2,1)S(1)}, bf16[352,2048]{1,0:T(8,128)(2,1)S(1)}, u32[]{:S(2)}, u32[]{:S(2)}) %collective-permute-start.29) | collective-permute-done | bytes 1441824 | tf_op jit(solution)/shard_map/ppermute | solution.py:66
  237.6 28.4 %collective-permute-done.30 = bf16[352,2048]{1,0:T(8,128)(2,1)S(1)} collective-permute-done((bf16[352,2048]{1,0:T(8,128)(2,1)S(1)}, bf16[352,2048]{1,0:T(8,128)(2,1)S(1)}, u32[]{:S(2)}, u32[]{:S(2)}) %collective-permute-start.30) | collective-permute-done | bytes 1441824 | tf_op jit(solution)/shard_map/ppermute | solution.py:66
  270.9 26.1 %collective-permute-done.31 = bf16[352,2048]{1,0:T(8,128)(2,1)S(1)} collective-permute-done((bf16[352,2048]{1,0:T(8,128)(2,1)S(1)}, bf16[352,2048]{1,0:T(8,128)(2,1)S(1)}, u32[]{:S(2)}, u32[]{:S(2)}) %collective-permute-start.31) | collective-permute-done | bytes 1441824 | tf_op jit(solution)/shard_map/ppermute | solution.py:66
  305.0 24.6 %collective-permute-done.35 = bf16[176,2048]{1,0:T(8,128)(2,1)S(1)} collective-permute-done((bf16[176,2048]{1,0:T(8,128)(2,1)S(1)}, bf16[176,2048]{1,0:T(8,128)(2,1)S(1)}, u32[]{:S(2)}, u32[]{:S(2)}) %collective-permute-start.35) | collective-permute-done | bytes 720928 | tf_op jit(solution)/shard_map/ppermute | solution.py:69
  332.3 17.5 %fusion.35 = f32[2816,1024]{1,0:T(8,128)} fusion(bf16[2816,2048]{1,0:T(8,128)(2,1)S(1)} %constant_dynamic-update-slice_fusion.8, bf16[256,2048]{1,0:T(8,128)(2,1)S(1)} %collective-permute-done.39, bf16[256,2048]{1,0:T(8,128)(2,1)S(1)} %collective-permute-done.38, bf16[256,2048]{1,0:T(8,128)(2,1)S(1)} %collective-permute-done.37, ...), kind=kOutput, calls=%fused_computation.114 | convolution fusion | flops 11827937280 | bytes 27262976 | tf_op jit(solution)/shard_map/dot_general | solution.py:36
  349.8 8.8 fusion.57
  366.4 11.5 %collective-permute-done.45 = bf16[176,2048]{1,0:T(8,128)(2,1)S(1)} collective-permute-done((bf16[176,2048]{1,0:T(8,128)(2,1)}, bf16[176,2048]{1,0:T(8,128)(2,1)S(1)}, u32[]{:S(2)}, u32[]{:S(2)}) %collective-permute-start.45) | collective-permute-done | bytes 720928 | tf_op jit(solution)/shard_map/ppermute | solution.py:65
  395.1 9.0 fusion.67
  409.1 23.7 %collective-permute-done.50 = bf16[256,2048]{1,0:T(8,128)(2,1)S(1)} collective-permute-done((bf16[256,2048]{1,0:T(8,128)(2,1)S(1)}, bf16[256,2048]{1,0:T(8,128)(2,1)S(1)}, u32[]{:S(2)}, u32[]{:S(2)}) %collective-permute-start.50) | collective-permute-done | bytes 1048608 | tf_op jit(solution)/shard_map/ppermute | solution.py:102
  436.4 22.8 %collective-permute-done.52 = bf16[256,2048]{1,0:T(8,128)(2,1)S(1)} collective-permute-done((bf16[256,2048]{1,0:T(8,128)(2,1)S(1)}, bf16[256,2048]{1,0:T(8,128)(2,1)S(1)}, u32[]{:S(2)}, u32[]{:S(2)}) %collective-permute-start.52) | collective-permute-done | bytes 1048608 | tf_op jit(solution)/shard_map/ppermute | solution.py:93
  471.6 13.3 %fusion.34 = f32[1408,1024]{1,0:T(8,128)} fusion(bf16[1408,2048]{1,0:T(8,128)(2,1)} %constant_dynamic-update-slice_fusion.17, bf16[256,2048]{1,0:T(8,128)(2,1)} %copy-done.56, bf16[256,2048]{1,0:T(8,128)(2,1)} %copy-done.54, bf16[256,2048]{1,0:T(8,128)(2,1)} %copy-done.55, bf16[256,2048]{1,0:T(8,128)(2,1)} %copy-done.18), kind=kOutput, calls=%fused_computation.113 | convolution fusion | flops 5922357248 | bytes 15728640 | tf_op jit(solution)/shard_map/dot_general | solution.py:36
  491.0 20.2 %fusion.68 = (bf16[1024,2048]{1,0:T(8,128)(2,1)}, f32[1024,2048]{1,0:T(8,128)}) fusion(bf16[2816,1024]{1,0:T(8,128)(2,1)S(1)} %bitcast.195, bf16[2816,2048]{1,0:T(8,128)(2,1)} %copy-done.30), kind=kOutput, calls=%fused_computation.293 | convolution fusion | flops 11813257216 | bytes 29884416 | tf_op jit(solution)/shard_map/dot_general | solution.py:40
  515.0 18.4 %convolution_convert_fusion = bf16[2816,2048]{1,0:T(8,128)(2,1)} fusion(bf16[2816,1024]{1,0:T(8,128)(2,1)} %bitcast.196, bf16[256,2048]{1,0:T(8,128)(2,1)} %copy-done.51, bf16[256,2048]{1,0:T(8,128)(2,1)} %copy-done.49, bf16[256,2048]{1,0:T(8,128)(2,1)} %copy-done.50, bf16[256,2048]{1,0:T(8,128)(2,1)} %copy-done.21), kind=kOutput, calls=%fused_computation.5 | convolution fusion | flops 11833704448 | bytes 21495808 | tf_op jit(solution)/shard_map/dot_general | solution.py:32
  539.7 15.0 %collective-permute-done.94 = bf16[176,2048]{1,0:T(8,128)(2,1)S(1)} collective-permute-done((bf16[176,2048]{1,0:T(8,128)(2,1)S(1)}, bf16[176,2048]{1,0:T(8,128)(2,1)S(1)}, u32[]{:S(2)}, u32[]{:S(2)}) %collective-permute-start.94) | collective-permute-done | bytes 720928 | tf_op jit(solution)/shard_map/ppermute | solution.py:77
  557.2 12.0 %collective-permute-done.106 = bf16[176,2048]{1,0:T(8,128)(2,1)S(1)} collective-permute-done((bf16[176,2048]{1,0:T(8,128)(2,1)S(1)}, bf16[176,2048]{1,0:T(8,128)(2,1)S(1)}, u32[]{:S(2)}, u32[]{:S(2)}) %collective-permute-start.106) | collective-permute-done | bytes 720928 | tf_op jit(solution)/shard_map/ppermute | solution.py:83
  576.5 12.0 %collective-permute-done.107 = bf16[176,2048]{1,0:T(8,128)(2,1)S(1)} collective-permute-done((bf16[176,2048]{1,0:T(8,128)(2,1)S(1)}, bf16[176,2048]{1,0:T(8,128)(2,1)S(1)}, u32[]{:S(2)}, u32[]{:S(2)}) %collective-permute-start.107) | collective-permute-done | bytes 720928 | tf_op jit(solution)/shard_map/ppermute | solution.py:83
  602.6 16.8 %collective-permute-done.95 = bf16[352,2048]{1,0:T(8,128)(2,1)S(1)} collective-permute-done((bf16[352,2048]{1,0:T(8,128)(2,1)S(1)}, bf16[352,2048]{1,0:T(8,128)(2,1)S(1)}, u32[]{:S(2)}, u32[]{:S(2)}) %collective-permute-start.95) | collective-permute-done | bytes 1441824 | tf_op jit(solution)/shard_map/ppermute | solution.py:83
  643.5 20.6 %collective-permute-done.96 = bf16[352,2048]{1,0:T(8,128)(2,1)S(1)} collective-permute-done((bf16[352,2048]{1,0:T(8,128)(2,1)S(1)}, bf16[352,2048]{1,0:T(8,128)(2,1)S(1)}, u32[]{:S(2)}, u32[]{:S(2)}) %collective-permute-start.96) | collective-permute-done | bytes 1441824 | tf_op jit(solution)/shard_map/ppermute | solution.py:83
  676.0 37.1 %shard_map.231 = bf16[1024,1536]{1,0:T(8,128)(2,1)} custom-call(s32[4]{0:T(128)} %iota_xor_fusion.slot_ref, s32[4]{0:T(128)} %and_select_fusion.3.first_ref, bf16[1024,1536]{1,0:T(8,128)(2,1)} %get-tuple-element.23.turned, bf16[1024,512]{1,0:T(8,128)(2,1)} %convolution_convert_fusion.4.out_grad, f32[1024,128]{1,0:T(8,128)} %concatenate.77.cosine, ...), custom_call_target="tpu_custom_call" | custom-call | flops 8053063680 | bytes 9437184 | tf_op jit(solution)/shard_map/pallas_call | solution.py:600
  713.1 11.8 %fusion.69 = (bf16[1024,2048]{1,0:T(8,128)(2,1)S(1)}, f32[1024,2048]{1,0:T(8,128)}) fusion(bf16[1024,1536]{1,0:T(8,128)(2,1)} %shard_map.231, bf16[2048,1536]{1,0:T(8,128)(2,1)} %copy-done.8), kind=kOutput, calls=%fused_computation.294 | convolution fusion | flops 6444548096 | bytes 22020096 | tf_op jit(solution)/shard_map/dot_general | solution.py:36
  733.8 9.0 convolution_convert_fusion.2
  789.3 7.5 collective-permute-done.86
  823.2 21.4 %collective-permute-done.74 = bf16[256,1536]{1,0:T(8,128)(2,1)} collective-permute-done((bf16[256,1536]{1,0:T(8,128)(2,1)}, bf16[256,1536]{1,0:T(8,128)(2,1)}, u32[]{:S(2)}, u32[]{:S(2)}) %collective-permute-start.74) | collective-permute-done | bytes 786464 | tf_op jit(solution)/shard_map/ppermute | solution.py:83
  849.8 14.4 %collective-permute-done.64 = f32[16,128]{1,0:T(8,128)S(1)} collective-permute-done((f32[16,128]{1,0:T(8,128)S(1)}, f32[16,128]{1,0:T(8,128)S(1)}, u32[]{:S(2)}, u32[]{:S(2)}) %collective-permute-start.64) | collective-permute-done | bytes 8224 | tf_op jit(solution)/shard_map/ppermute | solution.py:197
  904.2 18.6 %collective-permute-done.71 = f32[16,128]{1,0:T(8,128)S(1)} collective-permute-done((f32[16,128]{1,0:T(8,128)S(1)}, f32[16,128]{1,0:T(8,128)S(1)}, u32[]{:S(2)}, u32[]{:S(2)}) %collective-permute-start.71) | collective-permute-done | bytes 8224 | tf_op jit(solution)/shard_map/ppermute | solution.py:202
  941.5 10.7 %shard_map.232 = f32[256,6144]{1,0:T(8,128)} custom-call(s32[1]{0:T(128)} %bitcast.12.s_ref, f32[1]{0:T(128)} %div.84.factor_ref, bf16[256,1536]{1,0:T(8,128)(2,1)} %copy-done.16, bf16[256,1536]{1,0:T(8,128)(2,1)} %copy-done.24, bf16[256,1536]{1,0:T(8,128)(2,1)} %collective-permute-done.81.p2, bf16[256,1536]{1,0:T(8,128)(2,1)} %collective-permute-done.82.p3), custom_call_target="tpu_custom_call" | custom-call | tf_op jit(solution)/shard_map/pallas_call | solution.py:332
  952.3 8.3 shard_map.234
  (569 shorter events, 403.5 us)
Async XLA Ops:
  9.4 68.1 %collective-permute-start.10 = (bf16[256,1536]{1,0:T(8,128)(2,1)}, bf16[256,1536]{1,0:T(8,128)(2,1)}, u32[]{:S(2)}, u32[]{:S(2)}) collective-permute-start(bf16[256,1536]{1,0:T(8,128)(2,1)} %shard_map.229), channel_id=1, source_target_pairs={{2,0},{4,2},{6,4},{7,6},{5,7},{3,5},{1,3},{0,1},{10,8},{12,10},{14... | collective-permute-start | bytes 2359304 | tf_op jit(solution)/shard_map/ppermute | solution.py:66
  12.3 66.7 %collective-permute-start.13 = (bf16[256,1536]{1,0:T(8,128)(2,1)}, bf16[256,1536]{1,0:T(8,128)(2,1)}, u32[]{:S(2)}, u32[]{:S(2)}) collective-permute-start(bf16[256,1536]{1,0:T(8,128)(2,1)} %shard_map.229), channel_id=1, source_target_pairs={{0,2},{2,4},{4,6},{6,7},{7,5},{5,3},{3,1},{1,0},{8,10},{10,12},{12... | collective-permute-start | bytes 2359304 | tf_op jit(solution)/shard_map/ppermute | solution.py:65
  16.5 50.0 %collective-permute-start.3 = (f32[14,128]{1,0:T(8,128)S(1)}, f32[14,128]{1,0:T(8,128)S(1)}, u32[]{:S(2)}, u32[]{:S(2)}) collective-permute-start(f32[14,128]{1,0:T(8,128)S(1)} %convert_bitcast_fusion.1), channel_id=1, source_target_pairs={{0,1},{1,2},{2,3},{3,4},{4,5},{5,6},{6,7},{7,0},{8,9},{9,10},{10,1... | collective-permute-start | bytes 21512 | tf_op jit(solution)/shard_map/ppermute | solution.py:190
  18.4 49.3 %collective-permute-start.4 = (f32[14,128]{1,0:T(8,128)S(1)}, f32[14,128]{1,0:T(8,128)S(1)}, u32[]{:S(2)}, u32[]{:S(2)}) collective-permute-start(f32[14,128]{1,0:T(8,128)S(1)} %convert_bitcast_fusion.1), channel_id=1, source_target_pairs={{0,2},{1,3},{2,4},{3,5},{4,6},{5,7},{6,0},{7,1},{8,10},{9,11},{10,... | collective-permute-start | bytes 21512 | tf_op jit(solution)/shard_map/ppermute | solution.py:190
  20.0 50.4 %collective-permute-start.5 = (f32[14,128]{1,0:T(8,128)S(1)}, f32[14,128]{1,0:T(8,128)S(1)}, u32[]{:S(2)}, u32[]{:S(2)}) collective-permute-start(f32[14,128]{1,0:T(8,128)S(1)} %convert_bitcast_fusion.1), channel_id=1, source_target_pairs={{0,3},{1,4},{2,5},{3,6},{4,7},{5,0},{6,1},{7,2},{8,11},{9,12},{10,... | collective-permute-start | bytes 21512 | tf_op jit(solution)/shard_map/ppermute | solution.py:190
  150.5 32.8 %collective-permute-start.20 = (bf16[64,2048]{1,0:T(8,128)(2,1)}, bf16[64,2048]{1,0:T(8,128)(2,1)}, u32[]{:S(2)}, u32[]{:S(2)}) collective-permute-start(bf16[64,2048]{1,0:T(8,128)(2,1)} %collective-permute-done.19), channel_id=1, source_target_pairs={{2,0},{4,2},{6,4},{7,6},{5,7},{3,5},{1,3},{0,1},{10,8},{12,10},{14... | collective-permute-start | bytes 786440 | tf_op jit(solution)/shard_map/ppermute | solution.py:66
  201.6 32.6 %collective-permute-start.29 = (bf16[352,2048]{1,0:T(8,128)(2,1)S(1)}, bf16[352,2048]{1,0:T(8,128)(2,1)S(1)}, u32[]{:S(2)}, u32[]{:S(2)}) collective-permute-start(bf16[352,2048]{1,0:T(8,128)(2,1)S(1)} %pad_maximum_fusion.5), channel_id=1, source_target_pairs={{2,0},{4,2},{6,4},{7,6},{5,7},{3,5},{1,3},{0,1},{10,8},{12,10},{14... | collective-permute-start | bytes 4325384 | tf_op jit(solution)/shard_map/ppermute | solution.py:66
  203.7 32.6 %collective-permute-start.32 = (bf16[352,2048]{1,0:T(8,128)(2,1)S(1)}, bf16[352,2048]{1,0:T(8,128)(2,1)S(1)}, u32[]{:S(2)}, u32[]{:S(2)}) collective-permute-start(bf16[352,2048]{1,0:T(8,128)(2,1)S(1)} %pad_maximum_fusion.5), channel_id=1, source_target_pairs={{0,2},{2,4},{4,6},{6,7},{7,5},{5,3},{3,1},{1,0},{8,10},{10,12},{12... | collective-permute-start | bytes 4325384 | tf_op jit(solution)/shard_map/ppermute | solution.py:65
  203.7 32.9 %collective-permute-start.26 = (bf16[256,2048]{1,0:T(8,128)(2,1)S(1)}, bf16[256,2048]{1,0:T(8,128)(2,1)S(1)}, u32[]{:S(2)}, u32[]{:S(2)}) collective-permute-start(bf16[256,2048]{1,0:T(8,128)(2,1)S(1)} %get-tuple-element.78), channel_id=1, source_target_pairs={{0,8},{8,0},{16,24},{24,16},{1,9},{9,1},{17,25},{25,17},{2,10},{10... | collective-permute-start | bytes 3145736 | tf_op jit(solution)/shard_map/ppermute | solution.py:100
  204.0 32.6 %collective-permute-start.28 = (bf16[256,2048]{1,0:T(8,128)(2,1)S(1)}, bf16[256,2048]{1,0:T(8,128)(2,1)S(1)}, u32[]{:S(2)}, u32[]{:S(2)}) collective-permute-start(bf16[256,2048]{1,0:T(8,128)(2,1)S(1)} %fusion.31), channel_id=1, source_target_pairs={{0,16},{8,24},{16,0},{24,8},{1,17},{9,25},{17,1},{25,9},{2,18},{10... | collective-permute-start | bytes 3145736 | tf_op jit(solution)/shard_map/ppermute | solution.py:102
  269.1 35.8 %collective-permute-start.38 = (bf16[256,2048]{1,0:T(8,128)(2,1)S(1)}, bf16[256,2048]{1,0:T(8,128)(2,1)S(1)}, u32[]{:S(2)}, u32[]{:S(2)}) collective-permute-start(bf16[256,2048]{1,0:T(8,128)(2,1)S(1)} %add_convert_fusion.6), channel_id=1, source_target_pairs={{0,16},{8,24},{16,0},{24,8},{1,17},{9,25},{17,1},{25,9},{2,18},{10... | collective-permute-start | bytes 3145736 | tf_op jit(solution)/shard_map/ppermute | solution.py:93
  469.4 66.7 %collective-permute-start.105 = (bf16[88,2048]{1,0:T(8,128)(2,1)}, bf16[88,2048]{1,0:T(8,128)(2,1)}, u32[]{:S(2)}, u32[]{:S(2)}) collective-permute-start(bf16[88,2048]{1,0:T(8,128)(2,1)} %get-tuple-element.66), channel_id=1, source_target_pairs={{0,2},{2,4},{4,6},{6,7},{7,5},{5,3},{3,1},{1,0},{8,10},{10,12},{12... | collective-permute-start | bytes 1081352 | tf_op jit(solution)/shard_map/ppermute | solution.py:77
  469.9 67.8 %collective-permute-start.109 = (bf16[88,2048]{1,0:T(8,128)(2,1)}, bf16[88,2048]{1,0:T(8,128)(2,1)}, u32[]{:S(2)}, u32[]{:S(2)}) collective-permute-start(bf16[88,2048]{1,0:T(8,128)(2,1)} %get-tuple-element.67), channel_id=1, source_target_pairs={{2,0},{4,2},{6,4},{7,6},{5,7},{3,5},{1,3},{0,1},{10,8},{12,10},{14... | collective-permute-start | bytes 1081352 | tf_op jit(solution)/shard_map/ppermute | solution.py:78
  514.5 55.5 %collective-permute-start.55 = (bf16[256,2048]{1,0:T(8,128)(2,1)}, bf16[256,2048]{1,0:T(8,128)(2,1)}, u32[]{:S(2)}, u32[]{:S(2)}) collective-permute-start(bf16[256,2048]{1,0:T(8,128)(2,1)} %get-tuple-element.75), channel_id=1, source_target_pairs={{0,8},{8,0},{16,24},{24,16},{1,9},{9,1},{17,25},{25,17},{2,10},{10... | collective-permute-start | bytes 3145736 | tf_op jit(solution)/shard_map/ppermute | solution.py:99
  514.5 76.1 %collective-permute-start.54 = (bf16[256,2048]{1,0:T(8,128)(2,1)}, bf16[256,2048]{1,0:T(8,128)(2,1)}, u32[]{:S(2)}, u32[]{:S(2)}) collective-permute-start(bf16[256,2048]{1,0:T(8,128)(2,1)} %get-tuple-element.74), channel_id=1, source_target_pairs={{0,8},{8,0},{16,24},{24,16},{1,9},{9,1},{17,25},{25,17},{2,10},{10... | collective-permute-start | bytes 3145736 | tf_op jit(solution)/shard_map/ppermute | solution.py:100
  574.3 69.2 %collective-permute-start.99 = (bf16[352,2048]{1,0:T(8,128)(2,1)}, bf16[352,2048]{1,0:T(8,128)(2,1)}, u32[]{:S(2)}, u32[]{:S(2)}) collective-permute-start(bf16[352,2048]{1,0:T(8,128)(2,1)} %pad_maximum_fusion.7), channel_id=1, source_target_pairs={{2,0},{4,2},{6,4},{7,6},{5,7},{3,5},{1,3},{0,1},{10,8},{12,10},{14... | collective-permute-start | bytes 4325384 | tf_op jit(solution)/shard_map/ppermute | solution.py:84
  576.0 43.4 %collective-permute-start.95 = (bf16[352,2048]{1,0:T(8,128)(2,1)S(1)}, bf16[352,2048]{1,0:T(8,128)(2,1)S(1)}, u32[]{:S(2)}, u32[]{:S(2)}) collective-permute-start(bf16[352,2048]{1,0:T(8,128)(2,1)S(1)} %pad_maximum_fusion.6), channel_id=1, source_target_pairs={{0,2},{2,4},{4,6},{6,7},{7,5},{5,3},{3,1},{1,0},{8,10},{10,12},{12... | collective-permute-start | bytes 4325384 | tf_op jit(solution)/shard_map/ppermute | solution.py:83
  590.6 44.3 %collective-permute-start.108 = (bf16[176,2048]{1,0:T(8,128)(2,1)}, bf16[176,2048]{1,0:T(8,128)(2,1)}, u32[]{:S(2)}, u32[]{:S(2)}) collective-permute-start(bf16[176,2048]{1,0:T(8,128)(2,1)} %get-tuple-element.62), channel_id=1, source_target_pairs={{0,2},{2,4},{4,6},{6,7},{7,5},{5,3},{3,1},{1,0},{8,10},{10,12},{12... | collective-permute-start | bytes 2162696 | tf_op jit(solution)/shard_map/ppermute | solution.py:87
  601.1 33.9 %collective-permute-start.58 = (bf16[256,2048]{1,0:T(8,128)(2,1)}, bf16[256,2048]{1,0:T(8,128)(2,1)}, u32[]{:S(2)}, u32[]{:S(2)}) collective-permute-start(bf16[256,2048]{1,0:T(8,128)(2,1)} %get-tuple-element.35), channel_id=1, source_target_pairs={{0,16},{8,24},{16,0},{24,8},{1,17},{9,25},{17,1},{25,9},{2,18},{10... | collective-permute-start | bytes 3145736 | tf_op jit(solution)/shard_map/ppermute | solution.py:93
  621.4 42.7 %collective-permute-start.96 = (bf16[352,2048]{1,0:T(8,128)(2,1)S(1)}, bf16[352,2048]{1,0:T(8,128)(2,1)S(1)}, u32[]{:S(2)}, u32[]{:S(2)}) collective-permute-start(bf16[352,2048]{1,0:T(8,128)(2,1)S(1)} %add_convert_fusion.5), channel_id=1, source_target_pairs={{0,2},{2,4},{4,6},{6,7},{7,5},{5,3},{3,1},{1,0},{8,10},{10,12},{12... | collective-permute-start | bytes 4325384 | tf_op jit(solution)/shard_map/ppermute | solution.py:83
  635.0 35.1 %collective-permute-start.57 = (bf16[256,2048]{1,0:T(8,128)(2,1)}, bf16[256,2048]{1,0:T(8,128)(2,1)S(1)}, u32[]{:S(2)}, u32[]{:S(2)}) collective-permute-start(bf16[256,2048]{1,0:T(8,128)(2,1)} %get-tuple-element.35), channel_id=1, source_target_pairs={{0,8},{8,0},{16,24},{24,16},{1,9},{9,1},{17,25},{25,17},{2,10},{10... | collective-permute-start | bytes 3145736 | tf_op jit(solution)/shard_map/ppermute | solution.py:94
  635.0 35.1 %collective-permute-start.59 = (bf16[256,2048]{1,0:T(8,128)(2,1)}, bf16[256,2048]{1,0:T(8,128)(2,1)S(1)}, u32[]{:S(2)}, u32[]{:S(2)}) collective-permute-start(bf16[256,2048]{1,0:T(8,128)(2,1)} %collective-permute-done.58), channel_id=1, source_target_pairs={{0,8},{8,0},{16,24},{24,16},{1,9},{9,1},{17,25},{25,17},{2,10},{10... | collective-permute-start | bytes 3145736 | tf_op jit(solution)/shard_map/ppermute | solution.py:95
  669.3 115.9 %collective-permute-start.100 = (bf16[352,2048]{1,0:T(8,128)(2,1)}, bf16[352,2048]{1,0:T(8,128)(2,1)}, u32[]{:S(2)}, u32[]{:S(2)}) collective-permute-start(bf16[352,2048]{1,0:T(8,128)(2,1)} %get-tuple-element.45), channel_id=1, source_target_pairs={{2,0},{4,2},{6,4},{7,6},{5,7},{3,5},{1,3},{0,1},{10,8},{12,10},{14... | collective-permute-start | bytes 4325384 | tf_op jit(solution)/shard_map/ppermute | solution.py:84
  726.5 55.1 %collective-permute-start.61 = (bf16[256,2048]{1,0:T(8,128)(2,1)}, bf16[256,2048]{1,0:T(8,128)(2,1)}, u32[]{:S(2)}, u32[]{:S(2)}) collective-permute-start(bf16[256,2048]{1,0:T(8,128)(2,1)} %get-tuple-element.73), channel_id=1, source_target_pairs={{0,8},{8,0},{16,24},{24,16},{1,9},{9,1},{17,25},{25,17},{2,10},{10... | collective-permute-start | bytes 3145736 | tf_op jit(solution)/shard_map/ppermute | solution.py:99
  726.5 78.2 %collective-permute-start.60 = (bf16[256,2048]{1,0:T(8,128)(2,1)}, bf16[256,2048]{1,0:T(8,128)(2,1)}, u32[]{:S(2)}, u32[]{:S(2)}) collective-permute-start(bf16[256,2048]{1,0:T(8,128)(2,1)} %get-tuple-element.72), channel_id=1, source_target_pairs={{0,8},{8,0},{16,24},{24,16},{1,9},{9,1},{17,25},{25,17},{2,10},{10... | collective-permute-start | bytes 3145736 | tf_op jit(solution)/shard_map/ppermute | solution.py:100
  796.8 95.6 %collective-permute-start.114 = (bf16[176,2048]{1,0:T(8,128)(2,1)}, bf16[176,2048]{1,0:T(8,128)(2,1)}, u32[]{:S(2)}, u32[]{:S(2)}) collective-permute-start(bf16[176,2048]{1,0:T(8,128)(2,1)} %add_convert_fusion.12.p0), channel_id=1, source_target_pairs={{0,16},{8,24},{16,0},{24,8},{1,17},{9,25},{17,1},{25,9},{2,18},{10... | collective-permute-start | bytes 2162696 | tf_op jit(solution)/shard_map/ppermute | solution.py:93
  799.4 79.6 %collective-permute-start.97 = (bf16[352,2048]{1,0:T(8,128)(2,1)}, bf16[352,2048]{1,0:T(8,128)(2,1)}, u32[]{:S(2)}, u32[]{:S(2)}) collective-permute-start(bf16[352,2048]{1,0:T(8,128)(2,1)} %get-tuple-element.44), channel_id=1, source_target_pairs={{0,2},{2,4},{4,6},{6,7},{7,5},{5,3},{3,1},{1,0},{8,10},{10,12},{12... | collective-permute-start | bytes 4325384 | tf_op jit(solution)/shard_map/ppermute | solution.py:87
  804.8 75.5 %collective-permute-start.101 = (bf16[352,2048]{1,0:T(8,128)(2,1)S(1)}, bf16[352,2048]{1,0:T(8,128)(2,1)}, u32[]{:S(2)}, u32[]{:S(2)}) collective-permute-start(bf16[352,2048]{1,0:T(8,128)(2,1)S(1)} %add_convert_fusion.2), channel_id=1, source_target_pairs={{2,0},{4,2},{6,4},{7,6},{5,7},{3,5},{1,3},{0,1},{10,8},{12,10},{14... | collective-permute-start | bytes 4325384 | tf_op jit(solution)/shard_map/ppermute | solution.py:88
  811.4 33.3 %collective-permute-start.74 = (bf16[256,1536]{1,0:T(8,128)(2,1)}, bf16[256,1536]{1,0:T(8,128)(2,1)}, u32[]{:S(2)}, u32[]{:S(2)}) collective-permute-start(bf16[256,1536]{1,0:T(8,128)(2,1)} %add_convert_fusion.11), channel_id=1, source_target_pairs={{0,2},{2,4},{4,6},{6,7},{7,5},{5,3},{3,1},{1,0},{8,10},{10,12},{12... | collective-permute-start | bytes 2359304 | tf_op jit(solution)/shard_map/ppermute | solution.py:83
  847.7 37.6 %collective-permute-start.78 = (bf16[256,1536]{1,0:T(8,128)(2,1)S(1)}, bf16[256,1536]{1,0:T(8,128)(2,1)S(1)}, u32[]{:S(2)}, u32[]{:S(2)}) collective-permute-start(bf16[256,1536]{1,0:T(8,128)(2,1)S(1)} %get-tuple-element.55), channel_id=1, source_target_pairs={{2,0},{4,2},{6,4},{7,6},{5,7},{3,5},{1,3},{0,1},{10,8},{12,10},{14... | collective-permute-start | bytes 2359304 | tf_op jit(solution)/shard_map/ppermute | solution.py:84
  885.3 37.8 %collective-permute-start.103 = (bf16[352,2048]{1,0:T(8,128)(2,1)S(1)}, bf16[352,2048]{1,0:T(8,128)(2,1)}, u32[]{:S(2)}, u32[]{:S(2)}) collective-permute-start(bf16[352,2048]{1,0:T(8,128)(2,1)S(1)} %add_convert_fusion.1.p0), channel_id=1, source_target_pairs={{0,16},{8,24},{16,0},{24,8},{1,17},{9,25},{17,1},{25,9},{2,18},{10... | collective-permute-start | bytes 4325384 | tf_op jit(solution)/shard_map/ppermute | solution.py:93
  904.1 48.1 %collective-permute-start.102 = (bf16[352,2048]{1,0:T(8,128)(2,1)S(1)}, bf16[352,2048]{1,0:T(8,128)(2,1)}, u32[]{:S(2)}, u32[]{:S(2)}) collective-permute-start(bf16[352,2048]{1,0:T(8,128)(2,1)S(1)} %add_convert_fusion.1.p0), channel_id=1, source_target_pairs={{0,8},{8,0},{16,24},{24,16},{1,9},{9,1},{17,25},{25,17},{2,10},{10... | collective-permute-start | bytes 4325384 | tf_op jit(solution)/shard_map/ppermute | solution.py:94
  (148 other events, 2866.8 us)

commit v2 on v1

--- a/solution.py
+++ b/solution.py
@@ -24,6 +24,7 @@
 NEXT = [(RING[i], RING[(i + 1) % 8]) for i in range(8)]
 PREV = [(RING[(i + 1) % 8], RING[i]) for i in range(8)]
 ORDER = np.array([[RING[(RING.index(f) + j) % 8] for j in range(8)] for f in range(8)], np.int32)
+PLACE = np.array([RING.index(f) for f in range(8)], np.int32)
 CORE = [(s, s ^ 1) for s in range(4)]
 ROW = [(s, s ^ 2) for s in range(4)]
 
@@ -55,38 +56,68 @@
     return inv_std * (scaled - mean_scaled - normed * mean_cross)
 
 
-def ring_gather(block, after=()):
-    if after:
-        block = lax.optimization_barrier((block,) + tuple(after))[0]
-    half = block.shape[0] // 2
-    blocks = [block] + [None] * 7
-    ahead = behind = block
-    for step in range(1, 4):
+def pin(value, *after):
+    return lax.optimization_barrier((value,) + after)[0] if after else value
+
+
+class RingGather:
+    def __init__(self, block):
+        self.ahead = self.behind = block
+        self.half = block.shape[0] // 2
+        self.blocks = [block] + [None] * 7
+        self.done = 0
+
+    def step(self, *after):
+        self.done += 1
+        ahead, behind = self.ahead, self.behind
+        if after:
+            ahead, behind = pin(ahead, *after), pin(behind, *after)
+        if self.done == 4:
+            ahead, behind = ahead[: self.half], behind[self.half :]
         ahead = lax.ppermute(ahead, "fsdp", NEXT)
         behind = lax.ppermute(behind, "fsdp", PREV)
-        blocks[8 - step] = ahead
-        blocks[step] = behind
-    top = lax.ppermute(ahead[:half], "fsdp", NEXT)
-    bottom = lax.ppermute(behind[half:], "fsdp", PREV)
-    blocks[4] = (top, bottom)
-    return blocks, (ahead, behind)
-
-
-def ring_scatter(blocks):
-    half = blocks[0].shape[0] // 2
-    ahead = lax.ppermute(blocks[4][:half], "fsdp", NEXT)
-    behind = lax.ppermute(blocks[4][half:], "fsdp", PREV)
-    up, down = blocks[3].astype(F32), blocks[5].astype(F32)
-    ahead = jnp.concatenate([up[:half] + ahead.astype(F32), up[half:]]).astype(BF16)
-    behind = jnp.concatenate([down[:half], down[half:] + behind.astype(F32)]).astype(BF16)
-    for step in (2, 1):
-        ahead = lax.ppermute(ahead, "fsdp", NEXT)
-        behind = lax.ppermute(behind, "fsdp", PREV)
-        ahead = (blocks[step].astype(F32) + ahead.astype(F32)).astype(BF16)
-        behind = (blocks[8 - step].astype(F32) + behind.astype(F32)).astype(BF16)
-    ahead = lax.ppermute(ahead, "fsdp", NEXT)
-    behind = lax.ppermute(behind, "fsdp", PREV)
-    return blocks[0].astype(F32) + ahead.astype(F32) + behind.astype(F32)
+        if self.done == 4:
+            self.blocks[4] = (ahead, behind)
+        else:
+            self.blocks[8 - self.done], self.blocks[self.done] = ahead, behind
+        self.ahead, self.behind = ahead, behind
+        return ahead, behind
+
+    def pieces(self):
+        for j, block in enumerate(self.blocks):
+            if j == 4:
+                yield j, 0, block[0]
+                yield j, self.half, block[1]
+            else:
+                yield j, 0, block
+
+
+class RingScatter:
+    def __init__(self, blocks):
+        self.blocks = blocks
+        self.half = blocks[0].shape[0] // 2
+        self.ahead, self.behind = blocks[4][: self.half], blocks[4][self.half :]
+        self.done = 0
+
+    def step(self, *after):
+        self.done += 1
+        half = self.half
+        ahead = lax.ppermute(pin(self.ahead, *after), "fsdp", NEXT)
+        behind = lax.ppermute(pin(self.behind, *after), "fsdp", PREV)
+        got = (ahead, behind)
+        ahead, behind = ahead.astype(F32), behind.astype(F32)
+        if self.done == 1:
+            up, down = self.blocks[3].astype(F32), self.blocks[5].astype(F32)
+            ahead = jnp.concatenate([up[:half] + ahead, up[half:]])
+            behind = jnp.concatenate([down[:half], down[half:] + behind])
+        elif self.done < 4:
+            ahead = self.blocks[4 - self.done].astype(F32) + ahead
+            behind = self.blocks[4 + self.done].astype(F32) + behind
+        else:
+            self.total = self.blocks[0].astype(F32) + ahead + behind
+            return got
+        self.ahead, self.behind = ahead.astype(BF16), behind.astype(BF16)
+        return got
 
 
 def seq_gather(mine):
@@ -100,7 +131,7 @@
     beside = lax.ppermute(parts[1].astype(BF16), "seq", CORE)
     far = (parts[2] + corner.astype(F32)).astype(BF16)
     over = lax.ppermute(far, "seq", ROW)
-    return parts[0] + beside.astype(F32) + over.astype(F32)
+    return parts[0] + beside.astype(F32) + over.astype(F32), far
 
 
 class Fast:
@@ -109,48 +140,55 @@
         table = lax.dynamic_index_in_dim(jnp.asarray(ORDER), f, 0, keepdims=False)
         self.order = [table[j] for j in range(8)]
         self.slots = jnp.arange(4, dtype=jnp.int32) ^ s
-        self.after = ()
-
-    def weights(self, block):
-        blocks, self.after = ring_gather(block, self.after)
-        return blocks
-
-    def weights_in_order(self, block):
-        size = block.shape[0]
-        blocks = self.weights(block)
-        whole = jnp.zeros((8 * size, block.shape[1]), BF16)
-        for j, part in enumerate(blocks):
-            at = self.order[j] * size
-            if j == 4:
-                whole = lax.dynamic_update_slice(whole, part[0], (at, 0))
-                whole = lax.dynamic_update_slice(whole, part[1], (at + size // 2, 0))
-            else:
-                whole = lax.dynamic_update_slice(whole, part, (at, 0))
+        self.rings = {}
+
+    def gather(self, **blocks):
+        self.rings.update({name: RingGather(block) for name, block in blocks.items()})
+
+    def scatter(self, **wholes):
+        for name, whole in wholes.items():
+            order = self.order if name in "FSO" else range(8)
+            size = whole.shape[0] // 8
+            self.rings[name] = RingScatter(
+                [lax.dynamic_slice_in_dim(whole, order[j] * size, size, 0) for j in range(8)]
+            )
+
+    def hop(self, names, *after):
+        got = ()
+        for name in names:
+            got += self.rings[name].step(*after)
+        return got
+
+    def whole(self, name):
+        form = {"q": self.in_order, "o": self.shuffled}.get(name, self.as_found)
+        return form(self.rings[name])
+
+    def total(self, name):
+        return self.rings[name].total
+
+    def in_order(self, ring):
+        size, cols = ring.blocks[0].shape
+        whole = jnp.zeros((8 * size, cols), BF16)
+        for j, first, part in ring.pieces():
+            at = self.order[j] * size + first
+            whole = lax.dynamic_update_slice(whole, part, (at, 0))
         return whole
 
-    def weights_as_found(self, block):
-        blocks = self.weights(block)
-        return jnp.concatenate(list(blocks[:4]) + list(blocks[4]) + list(blocks[5:]))
-
-    def reduce_in_order(self, whole):
-        size = whole.shape[0] // 8
-        return ring_scatter(
-            [lax.dynamic_slice_in_dim(whole, self.order[j] * size, size, 0) for j in range(8)]
-        )
-
-    def reduce_as_found(self, whole):
-        size = whole.shape[0] // 8
-        return ring_scatter([whole[j * size : (j + 1) * size] for j in range(8)])
+    def shuffled(self, ring):
+        size, cols = ring.blocks[0].shape
+        whole = self.as_found(ring).reshape(8, size, cols)
+        places = (jnp.asarray(PLACE) - jnp.asarray(PLACE)[self.f]) % 8
+        return jnp.take(whole, places, axis=0).reshape(8 * size, cols)
+
+    def as_found(self, ring):
+        return jnp.concatenate([part for unused, unused, part in ring.pieces()])
 
     def pick_qkv(self, w_qkv):
         return pick_columns(w_qkv, self.s)
 
-    def gather_out(self, w_out):
+    def own_out(self, w_out):
         rows = w_out.shape[0] // 4
-        return self.weights_in_order(lax.dynamic_slice_in_dim(w_out, self.s * rows, rows, 0))
-
-    def reduce_out(self, raw_out):
-        return self.reduce_in_order(raw_out)
+        return lax.dynamic_slice_in_dim(w_out, self.s * rows, rows, 0)
 
     def bias_of_heads(self, full_bias):
         split = full_bias.reshape(3, 4, 2, 4, HD)
@@ -162,8 +200,9 @@
         here = (jnp.arange(4) == self.s).astype(F32)[None, None, None, :, None]
         return (split[:, :, :, None, :] * here).reshape(-1)
 
-    def final_qkv(self, share, factor):
-        return unpick_columns(seq_gather(share.astype(BF16)), self.s, factor)
+    def final_qkv(self, shares, factor):
+        parts = [seq_gather(share.astype(BF16)) for share in shares]
+        return unpick_columns(parts, self.s, factor)
 
     def final_rows(self, share, factor):
         return place_rows(seq_gather(share.astype(BF16)), self.s, factor)
@@ -171,8 +210,9 @@
     def final_out(self, share, factor):
         return self.final_rows(share, factor)
 
-    def final_pairs(self, share, factor):
-        return place_pairs(seq_gather(share.astype(BF16)), self.s, factor)
+    def final_pairs(self, first, second, factor):
+        parts = [seq_gather(share.astype(BF16)) for share in (first, second)]
+        return place_pairs(parts[0] + parts[1], self.s, factor)
 
     def tokens(self, mine):
         return jnp.concatenate(seq_gather(mine))
@@ -187,17 +227,18 @@
 
     def small_gather(self, mine):
         got = [mine] + [
-            lax.ppermute(mine, "fsdp", [(i, (i + k) % 8) for i in range(8)]) for k in range(1, 8)
+            lax.ppermute(mine, "fsdp", [(i, i ^ k) for i in range(8)]) for k in range(1, 8)
         ]
-        return jnp.take(jnp.stack(got), (self.f - jnp.arange(8)) % 8, axis=0)
+        return jnp.take(jnp.stack(got), self.f ^ jnp.arange(8), axis=0)
 
     def small_reduce(self, values):
-        rolled = jnp.take(values, (self.f + jnp.arange(8)) % 8, axis=0)
-        got = [rolled[0]] + [
-            lax.ppermute(rolled[k], "fsdp", [(i, (i + k) % 8) for i in range(8)])
-            for k in range(1, 8)
-        ]
-        total = jnp.sum(jnp.take(jnp.stack(got), (self.f - jnp.arange(8)) % 8, axis=0), axis=0)
+        total = jnp.take(values, self.f ^ jnp.arange(8), axis=0)
+        for bit in (4, 2, 1):
+            other = lax.ppermute(total[bit:], "fsdp", [(i, i ^ bit) for i in range(8)])
+            total = total[:bit] + other
+        return self.seq_sum(total[0])
+
+    def seq_sum(self, total):
         total = total + lax.ppermute(total, "seq", CORE)
         return total + lax.ppermute(total, "seq", ROW)
 
@@ -208,31 +249,40 @@
         self.members, self.shards = lax.axis_size("seq"), lax.axis_size("fsdp")
         self.slots = jnp.arange(self.members, dtype=jnp.int32)
         self.pairs = H // self.members // 2
-
-    def weights_in_order(self, block):
-        return lax.all_gather(block, "fsdp", axis=0, tiled=True)
-
-    weights_as_found = weights_in_order
-
-    def reduce_in_order(self, whole):
-        return lax.psum_scatter(whole, "fsdp", scatter_dimension=0, tiled=True).astype(F32)
-
-    reduce_as_found = reduce_in_order
+        self.wholes, self.totals = {}, {}
+
+    def gather(self, **blocks):
+        for name, block in blocks.items():
+            self.wholes[name] = lax.all_gather(block, "fsdp", axis=0, tiled=True)
+
+    def scatter(self, **wholes):
+        for name, whole in wholes.items():
+            if name == "O":
+                rows = whole.shape[0]
+                every = jnp.zeros((rows * self.members, whole.shape[1]), whole.dtype)
+                whole = lax.dynamic_update_slice(every, whole, (self.s * rows, 0))
+            total = lax.psum_scatter(whole, "fsdp", scatter_dimension=0, tiled=True)
+            self.totals[name] = total.astype(F32)
+
+    def hop(self, names, *after):
+        return ()
+
+    def whole(self, name):
+        if name != "o":
+            return self.wholes[name]
+        rows = self.wholes[name].shape[0] // self.members
+        return lax.dynamic_slice_in_dim(self.wholes[name], self.s * rows, rows, 0)
+
+    def total(self, name):
+        return self.totals[name]
 
     def pick_qkv(self, w_qkv):
         split = w_qkv.reshape(w_qkv.shape[0], 3, self.members, self.pairs, LANES)
         own = lax.dynamic_index_in_dim(split, self.s, 2, keepdims=False)
         return own.transpose(0, 2, 1, 3).reshape(w_qkv.shape[0], -1)
 
-    def gather_out(self, w_out):
-        rows = w_out.shape[0] * self.shards // self.members
-        return lax.dynamic_slice_in_dim(self.weights_in_order(w_out), self.s * rows, rows, 0)
-
-    def reduce_out(self, raw_out):
-        rows = raw_out.shape[0]
-        whole = jnp.zeros((rows * self.members, raw_out.shape[1]), raw_out.dtype)
-        whole = lax.dynamic_update_slice(whole, raw_out, (self.s * rows, 0))
-        return self.reduce_in_order(whole)
+    def own_out(self, w_out):
+        return w_out
 
     def bias_of_heads(self, full_bias):
         split = full_bias.reshape(3, self.members, self.pairs, LANES)
@@ -247,7 +297,8 @@
     def gathered(self, share):
         return lax.all_gather(share.astype(BF16), "seq", axis=0, tiled=False)
 
-    def final_qkv(self, share, factor):
+    def final_qkv(self, shares, factor):
+        share = jnp.concatenate(shares, axis=1)
         parts = self.gathered(share).reshape(self.members, -1, self.pairs, 3, LANES)
         return factor * parts.transpose(1, 3, 0, 2, 4).reshape(parts.shape[1], -1).astype(F32)
 
@@ -257,17 +308,17 @@
     def final_out(self, share, factor):
         return factor * lax.psum(share.astype(BF16), "seq").astype(F32)
 
-    def final_pairs(self, share, factor):
-        parts = self.gathered(share).reshape(self.members, 2, -1, share.shape[1])
-        return factor * parts.transpose(0, 2, 1, 3).reshape(-1, 2, share.shape[1]).astype(F32)
+    def final_pairs(self, first, second, factor):
+        parts = jnp.stack([first, second], axis=1)
+        parts = lax.all_gather(parts.astype(BF16), "seq", axis=0, tiled=True)
+        return factor * parts.astype(F32)
 
     def tokens(self, mine):
         return lax.all_gather(mine, "seq", axis=0, tiled=True)
 
     def tokens_sum(self, partial):
-        return lax.psum_scatter(partial.astype(BF16), "seq", scatter_dimension=0, tiled=True).astype(
-            F32
-        )
+        total = lax.psum_scatter(partial.astype(BF16), "seq", scatter_dimension=0, tiled=True)
+        return total.astype(F32), total
 
     def by_slot(self, values):
         return values
@@ -278,6 +329,9 @@
     def small_reduce(self, values):
         total = lax.psum(values, ("seq", "fsdp"))
         return lax.dynamic_index_in_dim(total, self.f, 0, keepdims=False)
+
+    def seq_sum(self, total):
+        return lax.psum(total, "seq")
 
 
 def call(kernel, grid, in_specs, out_specs, out_shape, scratch=(), prefetch=0, cost=None):
@@ -296,48 +350,69 @@
     )
 
 
-def pick_matrix(member, rows, cols, turned):
-    lane = lax.broadcasted_iota(jnp.int32, (rows, cols), 0 if turned else 1)
-    place = lax.broadcasted_iota(jnp.int32, (rows, cols), 1 if turned else 0)
-    source = jnp.where(lane < HD, lane, lane + (256 - HD)) + member * HD
-    return jnp.where(place == source, 1.0, 0.0).astype(BF16)
-
-
 def pick_kernel(s_ref, w_ref, out_ref):
-    out_ref[...] = dot_nn(w_ref[...], pick_matrix(s_ref[0], 512, LANES, False)).astype(BF16)
+    s = s_ref[0]
+    lane = lax.broadcasted_iota(jnp.int32, (w_ref.shape[0], LANES), 1)
+    odd = (s & 1) == 1
+    for pair in range(4):
+        for part in range(3):
+            at = part * 2048 + pair * 512 + (s >> 1) * LANES
+            one = w_ref[:, pl.ds(pl.multiple_of(at, LANES), LANES)].astype(F32)
+            two = w_ref[:, pl.ds(pl.multiple_of(at + 256, LANES), LANES)].astype(F32)
+            one = jnp.where(odd, pltpu.roll(one, HD, 1), one)
+            two = jnp.where(odd, two, pltpu.roll(two, HD, 1))
+            to = (pair * 3 + part) * LANES
+            out_ref[:, to : to + LANES] = jnp.where(lane < HD, one, two).astype(BF16)
 
 
 def pick_columns(w_qkv, s):
-    rows = w_qkv.shape[0]
+    rows, cols = w_qkv.shape
+    step = rows // 4
     return call(
         pick_kernel,
-        (12,),
-        [pl.BlockSpec((rows, 512), lambda g, s_ref: (0, (g % 3) * 4 + g // 3))],
-        pl.BlockSpec((rows, LANES), lambda g, s_ref: (0, g)),
+        (4,),
+        [pl.BlockSpec((step, cols), lambda g, s_ref: (g, 0))],
+        pl.BlockSpec((step, 12 * LANES), lambda g, s_ref: (g, 0)),
         jax.ShapeDtypeStruct((rows, 12 * LANES), BF16),
         prefetch=1,
     )(s.reshape(1), w_qkv)
 
 
-def unpick_kernel(s_ref, factor_ref, p0, p1, p2, p3, out_ref):
-    total = None
-    for r, part in enumerate((p0, p1, p2, p3)):
-        term = dot_nn(part[...], pick_matrix(s_ref[0] ^ r, LANES, 512, True))
-        total = term if total is None else total + term
-    out_ref[...] = total * factor_ref[0]
+def unpick_kernel(s_ref, factor_ref, *refs):
+    out_ref, ordered = refs[-2:]
+    s = s_ref[0]
+    factor = factor_ref[0]
+    rows = out_ref.shape[0]
+    lane = lax.broadcasted_iota(jnp.int32, (rows, LANES), 1)
+    for half in range(2):
+        for r in range(4):
+            ordered[s ^ r] = refs[4 * half + r][...].astype(F32) * factor
+        for pair in range(2):
+            for part in range(3):
+                at = slice((pair * 3 + part) * LANES, (pair * 3 + part + 1) * LANES)
+                heads = [ordered[m, :, at] for m in range(4)]
+                turned = [pltpu.roll(h, HD, 1) for h in heads]
+                to = part * 2048 + (2 * half + pair) * 512
+                for m in (0, 2):
+                    low = jnp.where(lane < HD, heads[m], turned[m + 1])
+                    high = jnp.where(lane < HD, turned[m], heads[m + 1])
+                    out_ref[:, to + m * HD : to + m * HD + LANES] = low
+                    out_ref[:, to + 256 + m * HD : to + 256 + m * HD + LANES] = high
 
 
 def unpick_columns(parts, s, factor):
-    rows = parts[0].shape[0]
+    rows, cols = parts[0][0].shape
+    step = rows // 4
     return call(
         unpick_kernel,
-        (12,),
+        (4,),
         [pl.BlockSpec(memory_space=pltpu.SMEM)]
-        + [pl.BlockSpec((rows, LANES), lambda g, s_ref: (0, g))] * 4,
-        pl.BlockSpec((rows, 512), lambda g, s_ref: (0, (g % 3) * 4 + g // 3)),
-        jax.ShapeDtypeStruct((rows, 12 * 512), F32),
+        + [pl.BlockSpec((step, cols), lambda g, s_ref: (g, 0))] * 8,
+        pl.BlockSpec((step, 8 * cols), lambda g, s_ref: (g, 0)),
+        jax.ShapeDtypeStruct((rows, 8 * cols), F32),
+        scratch=[pltpu.VMEM((4, step, cols), F32)],
         prefetch=1,
-    )(s.reshape(1), factor.reshape(1), *parts)
+    )(s.reshape(1), factor.reshape(1), *parts[0], *parts[1])
 
 
 def place_kernel(s_ref, factor_ref, p0, p1, p2, p3, out_ref):
@@ -362,25 +437,24 @@
     )(s.reshape(1), factor.reshape(1), *parts)
 
 
-def place_pair_kernel(s_ref, factor_ref, p0, p1, p2, p3, out_ref):
+def place_pair_kernel(s_ref, factor_ref, *refs):
+    out_ref = refs[8]
     r = pl.program_id(0)
-    rows = out_ref.shape[0]
-    for k, part in enumerate((p0, p1, p2, p3)):
+    for k in range(4):
 
         @pl.when(r == k)
-        def _(part=part):
-            out_ref[:, 0, :] = part[:rows].astype(F32) * factor_ref[0]
-            out_ref[:, 1, :] = part[rows:].astype(F32) * factor_ref[0]
+        def _(k=k):
+            out_ref[:, 0, :] = refs[k][...].astype(F32) * factor_ref[0]
+            out_ref[:, 1, :] = refs[4 + k][...].astype(F32) * factor_ref[0]
 
 
 def place_pairs(parts, s, factor):
     rows, cols = parts[0].shape
-    rows = rows // 2
     return call(
         place_pair_kernel,
         (4,),
         [pl.BlockSpec(memory_space=pltpu.SMEM)]
-        + [pl.BlockSpec((2 * rows, cols), lambda r, s_ref: (0, 0))] * 4,
+        + [pl.BlockSpec((rows, cols), lambda r, s_ref: (0, 0))] * 8,
         pl.BlockSpec((rows, 2, cols), lambda r, s_ref: (s_ref[0] ^ r, 0, 0)),
         jax.ShapeDtypeStruct((4 * rows, 2, cols), F32),
         prefetch=1,
@@ -467,17 +541,17 @@
     lax.fori_loop(0, slots, query_block, 0)
 
 
-def attention_forward(qkv, bias, tables, start, slot_of, first_slot, block):
-    length, width = qkv.shape
-    pairs = width // (3 * LANES)
+def attention_forward(qkv, bias, tables, start, slot_of, first_slot, *, block, skip, pairs):
+    length = qkv.shape[0]
+    width = pairs * 3 * LANES
     slots = length // block
     whole = pl.BlockSpec((length, LANES), lambda p, *_: (0, 0))
     return call(
         functools.partial(forward_kernel, block, slots),
         (pairs,),
         [
-            pl.BlockSpec((length, 3 * LANES), lambda p, *_: (0, p)),
-            pl.BlockSpec((1, 3 * LANES), lambda p, *_: (0, p)),
+            pl.BlockSpec((length, 3 * LANES), lambda p, *_: (0, p + skip)),
+            pl.BlockSpec((1, 3 * LANES), lambda p, *_: (0, p + skip)),
             whole,
             whole,
             whole,
@@ -592,7 +666,7 @@
     lax.fori_loop(0, slots, finish, 0)
 
 
-def attention_backward(turned, out_grad, tables, start, slot_of, first_slot, block):
+def attention_backward(turned, out_grad, tables, start, slot_of, first_slot, block, skip):
     length, width = turned.shape
     pairs = width // (3 * LANES)
     slots = length // block
@@ -602,7 +676,7 @@
         (pairs,),
         [
             pl.BlockSpec((length, 3 * LANES), lambda p, *_: (0, p)),
-            pl.BlockSpec((length, LANES), lambda p, *_: (0, p)),
+            pl.BlockSpec((length, LANES), lambda p, *_: (0, p + skip)),
             whole,
             whole,
             whole,
@@ -625,28 +699,17 @@
     )(slot_of, first_slot, turned, out_grad, *tables, start)
 
 
-def doc_starts(segment):
-    places = jnp.arange(segment.shape[0], dtype=jnp.int32)
-    change = jnp.concatenate([jnp.ones((1,), dtype=bool), segment[1:] != segment[:-1]])
-    return lax.cummax(jnp.where(change, places, 0), axis=0)
-
-
 def turn_tables(positions):
     half = ROT // 2
-    inverse = 10000.0 ** (-(jnp.arange(half, dtype=F32) * 2.0) / ROT)
-    angles = inverse[:, None] * positions.astype(F32)[None, :]
-    cosine, sine = jnp.cos(angles).T, jnp.sin(angles).T
-    length = positions.shape[0]
-    rest = jnp.zeros((length, HD - ROT), F32)
-    none = jnp.zeros_like(sine)
-
-    def twice(*pieces):
-        return jnp.concatenate(pieces * 2, axis=1)
-
+    lane = jnp.arange(LANES, dtype=jnp.int32) % HD
+    inverse = 10000.0 ** (-((lane % half).astype(F32) * 2.0) / ROT)
+    angles = positions.astype(F32)[:, None] * jnp.where(lane < ROT, inverse, 0.0)[None, :]
+    cosine, sine = jnp.cos(angles), jnp.sin(angles)
+    lane = lane[None, :]
     return (
-        twice(cosine, cosine, rest + 1.0),
-        twice(-sine, none, rest),
-        twice(none, sine, rest),
+        cosine,
+        jnp.where(lane < half, -sine, 0.0),
+        jnp.where((lane >= half) & (lane < ROT), sine, 0.0),
     )
 
 
@@ -675,103 +738,171 @@
     units = w_down.shape[0] // members
     vec = ln1_gain.shape[0]
     bias_share = b_qkv.shape[0]
+    pairs = H // members // 2
+
+    tokens_all = net.tokens(tokens[0])
 
     mine_gate_up = lax.dynamic_slice_in_dim(w_gate_up, s * units, units, 0)
-    mine_gate_up = jnp.concatenate([mine_gate_up[:, 0], mine_gate_up[:, 1]])
-    mine_down = lax.dynamic_slice_in_dim(w_down, s * units, units, 0)
-
-    small = jnp.concatenate([ln1_gain, ln1_bias, ln2_gain, ln2_bias, b_qkv])
-    small = net.small_gather(small.reshape(-1, LANES).astype(F32))
-    small = small.reshape(shards, 4 * vec + bias_share)
+    net.gather(
+        q=net.pick_qkv(w_qkv),
+        o=net.own_out(w_out),
+        g=mine_gate_up[:, 0],
+        u=mine_gate_up[:, 1],
+        d=lax.dynamic_slice_in_dim(w_down, s * units, units, 0),
+    )
+    done = net.hop("qo")
+
+    segment = pin(segments, *done)[0]
+    slot_segment = net.by_slot(segment)
+    slot_start = jnp.sum((segment[None, :] < slot_segment[:, None]).astype(jnp.int32), axis=1)
+    slot_place = net.by_slot(jnp.arange(length, dtype=jnp.int32))
+    block_first = segment.reshape(members, rows)[:, 0]
+    first_slot = (
+        jnp.sum((segment[None, :] < block_first[:, None]).astype(jnp.int32), axis=1) // rows
+    )
+    tables = turn_tables(slot_place - slot_start)
+    done = net.hop("qo") + tables + (slot_start, first_slot)
+
+    counted = pin(valid, *done)[0].astype(F32)
+    small = [pin(v, *done) for v in (ln1_gain, ln1_bias, ln2_gain, ln2_bias, b_qkv)]
+    small = jnp.concatenate(small).astype(F32)
+    small = jnp.concatenate([small, jnp.full((LANES,), jnp.sum(counted))])
+    small = net.small_gather(small.reshape(-1, LANES)).reshape(shards, -1)
     gain_one, shift_one, gain_two, shift_two = (
         small[:, i * vec : (i + 1) * vec].reshape(width) for i in range(4)
     )
-    own_bias = net.bias_of_heads(small[:, 4 * vec :].reshape(-1))
-
-    tokens_all = net.tokens(tokens[0])
-    full_qkv = net.weights_in_order(net.pick_qkv(w_qkv))
-    full_out = net.gather_out(w_out)
-    full_gate_up = net.weights_as_found(mine_gate_up)
-    full_down = net.weights_as_found(mine_down)
-
-    starts = doc_starts(segments[0])
-    positions = jnp.arange(length, dtype=jnp.int32) - starts
-    first_slot = starts.reshape(members, rows)[:, 0] // rows
-    slot_start = net.by_slot(starts)
-    tables = turn_tables(net.by_slot(positions))
-
+    own_bias = net.bias_of_heads(small[:, 4 * vec : 4 * vec + bias_share].reshape(-1))
+    sum_count = net.seq_sum(jnp.sum(small[:, -LANES:], axis=0))[0]
+    factor = (rows * members * shards) / sum_count
+    done = net.hop("qo")
+
+    tokens_all = pin(tokens_all, own_bias, *done)
     normed_all, unused = norm_parts(tokens_all.astype(F32))
     hidden_one = (normed_all * gain_one + shift_one).astype(BF16)
-    qkv = dot_nn(hidden_one, full_qkv)
-    turned, heads_out = attention_forward(
-        qkv, own_bias, tables, slot_start[:, None], net.slots, first_slot, rows
-    )
+    net.hop("qo")
+    done = net.hop("g", *done)
+    qkv = dot_nn(hidden_one, pin(net.whole("q"), *done))
+    half_pairs = pairs // 2
+    forward = functools.partial(
+        attention_forward,
+        qkv,
+        own_bias,
+        tables,
+        slot_start[:, None],
+        net.slots,
+        block=rows,
+        pairs=half_pairs,
+    )
+    turned_one, heads_one = forward(first_slot, skip=0)
+    done = net.hop("gu", *done)
+    turned_two, heads_two = forward(pin(first_slot, heads_one, *done), skip=half_pairs)
+    heads_out = jnp.concatenate([heads_one, heads_two], axis=1)
     tokens_in = tokens[0].astype(F32)
-    resid = tokens_in + net.tokens_sum(dot_nn(heads_out, full_out))
+    done = net.hop("gu", heads_one)
+    partial = dot_nn(pin(heads_out, *done), net.whole("o"))
+    attended = net.tokens_sum(partial)[0]
+    done = net.hop("gu", heads_two)
+    resid = tokens_in + pin(attended, *done)
 
     normed_two, inv_std_two = norm_parts(resid)
-    hidden_two = net.tokens((normed_two * gain_two + shift_two).astype(BF16))
-    gate_up = dot_nt(full_gate_up, hidden_two).reshape(shards, 2, units, length)
-    gate, up = gate_up[:, 0], gate_up[:, 1]
-    hidden = (jax.nn.silu(gate) * up).astype(BF16).reshape(shards * units, length)
-    outputs = resid + net.tokens_sum(dot_tn(hidden, full_down))
-    counted = valid[0].astype(F32)
+    mine_two = (normed_two * gain_two + shift_two).astype(BF16)
+    hidden_two = net.tokens(mine_two)
+    done = net.hop("u", mine_two) + net.hop("d", mine_two)
+    full_gate = net.whole("g")
+    gate = dot_nt(full_gate, pin(hidden_two, *done))
+    done = net.hop("d")
+    full_up = net.whole("u")
+    up = dot_nt(pin(full_up, gate, *done), hidden_two)
+    hidden = (jax.nn.silu(gate) * up).astype(BF16)
+    done = net.hop("d", gate)
+    hidden = pin(hidden, *done)
+    net.hop("d", hidden)
+    full_down = net.whole("d")
+    outputs = resid + net.tokens_sum(dot_tn(hidden, full_down))[0]
     differ = outputs - teacher[0].astype(F32)
     cot = counted[:, None] * differ
     half_sum = 0.5 * jnp.sum(cot * differ)
-    count_here = jnp.sum(counted)
     cot_low = net.tokens(cot.astype(BF16))
 
     raw_down = dot_nn(hidden, cot_low).astype(BF16)
-    sum_down = net.reduce_as_found(raw_down)
-    hidden_grad = dot_nt(full_down, cot_low).reshape(shards, units, length)
+    net.scatter(D=raw_down)
+    done = net.hop("D")
+    hidden_grad = dot_nt(pin(full_down, raw_down), cot_low)
     sigma = jax.nn.sigmoid(gate)
     silu_grad = hidden_grad * up
-    gate_grad = silu_grad * sigma + silu_grad * gate * sigma * (1.0 - sigma)
-    up_grad = hidden_grad * (gate * sigma)
-    grads = jnp.stack([gate_grad, up_grad], axis=1).astype(BF16).reshape(2 * shards * units, length)
-    two_grad = net.tokens_sum(dot_tn(grads, full_gate_up))
-    raw_gate_up = dot_nn(grads, hidden_two).astype(BF16)
-    sum_gate_up = net.reduce_as_found(raw_gate_up)
+    gate_grad = (silu_grad * sigma + silu_grad * gate * sigma * (1.0 - sigma)).astype(BF16)
+    up_grad = (hidden_grad * (gate * sigma)).astype(BF16)
+
+    raw_gate = dot_nn(gate_grad, pin(hidden_two, *done)).astype(BF16)
+    done = net.hop("D", gate_grad)
+
+    net.scatter(G=pin(raw_gate, *done))
+    partial = dot_tn(gate_grad, pin(full_gate, raw_gate, *done)) + dot_tn(up_grad, full_up)
+    done = net.hop("DG", raw_gate)
+
+    two_grad, far = net.tokens_sum(pin(partial, *done))
+    raw_up = dot_nn(up_grad, pin(hidden_two, far)).astype(BF16)
+    done = net.hop("DG", partial)
+
+    two_grad = pin(two_grad, raw_up, *done)
     resid_grad = cot + norm_back(two_grad, normed_two, inv_std_two, gain_two)
     gain_two_grad = jnp.sum(two_grad * normed_two, axis=0)
     shift_two_grad = jnp.sum(two_grad, axis=0)
-    resid_low = net.tokens(resid_grad.astype(BF16))
-
-    out_grad = dot_nt(resid_low, full_out).astype(BF16)
-    raw_out = dot_tn(heads_out, resid_low).astype(BF16)
-    sum_out = net.reduce_out(raw_out)
-    qkv_grad = attention_backward(
-        turned, out_grad, tables, slot_start[None, :], net.slots, first_slot, rows
-    )
-    grad_one = net.tokens_sum(dot_nt(qkv_grad, full_qkv))
-    raw_qkv = dot_tn(hidden_one, qkv_grad).astype(BF16)
-    sum_qkv = net.reduce_in_order(raw_qkv)
+    mine_low = resid_grad.astype(BF16)
+    resid_low = net.tokens(mine_low)
+    net.scatter(U=pin(raw_up, *done))
+    done = net.hop("GU", raw_up)
+
+    full_out, full_qkv = net.whole("o"), net.whole("q")
+    out_grad = dot_nt(pin(resid_low, *done), full_out).astype(BF16)
+    backward = functools.partial(
+        attention_backward,
+        tables=tables,
+        start=slot_start[None, :],
+        slot_of=net.slots,
+        block=rows,
+    )
+    grad_first = backward(turned_one, out_grad, first_slot=first_slot, skip=0)
+    raw_first = dot_tn(hidden_one, grad_first).astype(BF16)
+    done = net.hop("GU", resid_low)
+
+    net.scatter(F=pin(raw_first, *done))
+    here = pin(first_slot, raw_first, *done)
+    grad_second = backward(turned_two, out_grad, first_slot=here, skip=half_pairs)
+    done = net.hop("UF", raw_first)
+
+    qkv_grad = pin(jnp.concatenate([grad_first, grad_second], axis=1), *done)
+    partial = dot_nt(qkv_grad, full_qkv)
+    grad_one, far = net.tokens_sum(partial)
+    raw_second = dot_tn(hidden_one, pin(grad_second, partial)).astype(BF16)
+    raw_out = dot_tn(heads_out, pin(resid_low, raw_second)).astype(BF16)
+    grad_w_down = net.final_rows(net.total("D"), factor)
+    done = net.hop("UF", grad_second)
+
+    grad_w_gate_up = net.final_pairs(net.total("G"), net.total("U"), factor)
+    net.scatter(S=pin(raw_second, far, *done), O=pin(raw_out, far, *done))
+    done = net.hop("FSO", raw_out)
+    grad_one = pin(grad_one, raw_out, *done)
     normed_one, inv_std_one = norm_parts(tokens_in)
     tokens_grad = resid_grad + norm_back(grad_one, normed_one, inv_std_one, gain_one)
     gain_one_grad = jnp.sum(grad_one * normed_one, axis=0)
     shift_one_grad = jnp.sum(grad_one, axis=0)
-
     bias_grad = net.bias_of_all(jnp.sum(qkv_grad.astype(F32), axis=0)).reshape(shards, -1)
-
     vectors = jnp.concatenate(
         [
             v.reshape(shards, vec)
             for v in (gain_one_grad, shift_one_grad, gain_two_grad, shift_two_grad)
         ]
-        + [
-            bias_grad,
-            jnp.full((shards, LANES), half_sum),
-            jnp.full((shards, LANES), count_here),
-        ],
+        + [bias_grad, jnp.full((shards, LANES), half_sum)],
         axis=1,
-    )
-    vectors = net.small_reduce(vectors.reshape(shards, -1, LANES)).reshape(-1)
-    sum_half = vectors[4 * vec + bias_share]
-    sum_count = vectors[4 * vec + bias_share + LANES]
-    factor = (rows * members * shards) / sum_count
-    loss = 2.0 * sum_half / (sum_count * width)
+    ).reshape(shards, -1, LANES)
+    done = net.hop("FSO")
+
+    vectors = net.small_reduce(pin(vectors, *done)).reshape(-1)
+    loss = 2.0 * vectors[4 * vec + bias_share] / (sum_count * width)
     scaled = factor * vectors
+    done = net.hop("SO", scaled, grad_w_down)
+    net.hop("SO", grad_w_gate_up)
 
     return (
         outputs.astype(BF16)[None],
@@ -779,13 +910,13 @@
         (factor * tokens_grad).astype(BF16)[None],
         scaled[:vec],
         scaled[vec : 2 * vec],
-        net.final_qkv(sum_qkv, factor),
+        net.final_qkv([net.total("F"), net.total("S")], factor),
         scaled[4 * vec : 4 * vec + bias_share],
-        net.final_out(sum_out, factor),
+        net.final_out(net.total("O"), factor),
         scaled[2 * vec : 3 * vec],
         scaled[3 * vec : 4 * vec],
-        net.final_pairs(sum_gate_up, factor),
-        net.final_rows(sum_down, factor),
+        grad_w_gate_up,
+        grad_w_down,
     )
 
 

time: 972 us -> 867 us (0.89)
  waiting for transfers between devices: 418 us -> 292 us
  starting transfers between devices: 108 us -> 122 us
    ppermute x80 -> x102, waiting for transfers between devices: 343 us -> 188 us  [the longest x24 53.9 us: step(): ahead = lax.ppermute(pin(self.ahead, *after), 'fsdp', NEXT)]
    unnamed x176 -> x233, local copies, waits for them, and re-layouts: 24.8 us -> 53.1 us
    ppermute x80 -> x102, starting transfers between devices: 87.1 us -> 106 us  [the longest x20 27.5 us: step(): behind = lax.ppermute(behind, 'fsdp', PREV)]
    ppermute x4, waiting for transfers between devices: 33.3 us -> 50.1 us  [seq_scatter(): over = lax.ppermute(far, 'seq', ROW)]
    ppermute x8 -> x10, waiting for transfers between devices: 36.8 us -> 51 us  [seq_gather(): over = lax.ppermute(mine, 'seq', ROW)]
    slice x18 -> x23, local copies, waits for them, and re-layouts: 20.8 us -> 10.9 us  [the longest x1 4.2 us: per_device(): mine_gate_up[:, 1]]
    dot_general x4 -> x5, matrix products: 41.6 us -> 36.7 us  [dot_nn(): lax.dot_general(a, b, (((1,), (0,)), ((), ())), preferred_element_type=F32)]
    dot_general x4 -> x5, matrix products: 48.6 us -> 52.6 us  [dot_nt(): lax.dot_general(a, b, (((1,), (1,)), ((), ())), preferred_element_type=F32)]
  transfers between devices with their start and end apart: 116 -> 144, of which waited for: 46 -> 60; matrix products, arithmetic and copies ran while one was open for 29% -> 33% of each run, Pallas kernels for 9% -> 10%
where the time goes in v2:
time: 867 us; the launch traced here: 856 us
  waiting for transfers between devices  292 us (34%)
  matrix products  130 us (15%)
  starting transfers between devices  122 us (14%)
  local copies, waits for them, and re-layouts  103 us (12%)
  Pallas kernels  98.5 us (11%)
  other arithmetic  94.4 us (11%)
  between operations  15.9 us (2%)
    ppermute x24, waiting for transfers between devices, step(): ahead = lax.ppermute(pin(self.ahead, *after), 'fsdp', NEXT)  53.9 us
    unnamed x233, local copies, waits for them, and re-layouts  53.1 us
    dot_general x5, matrix products, dot_nt(): lax.dot_general(a, b, (((1,), (1,)), ((), ())), preferred_element_type=F32)  52.6 us
    ppermute x10, waiting for transfers between devices, seq_gather(): over = lax.ppermute(mine, 'seq', ROW)  51 us
    ppermute x4, waiting for transfers between devices, seq_scatter(): over = lax.ppermute(far, 'seq', ROW)  50.1 us
    dot_general x6, matrix products, dot_tn(): lax.dot_general(a, b, (((0,), (0,)), ((), ())), preferred_element_type=F32)  41 us
    pallas_call x2, Pallas kernels, attention_backward(): call(functools.partial(backward_kernel, block, slots), (pairs,), [pl.Bloc...  40.5 us
    ppermute x20, waiting for transfers between devices, step(): ahead = lax.ppermute(ahead, 'fsdp', NEXT)  38.2 us
  transfers between devices with their start and end apart: 144, of which 60 were waited for; matrix products, arithmetic and copies ran while one was open for 33% of the time, Pallas kernels for 10%

profile of v2, /device:TPU:0, one launch (start us, length us, event | category | flops | bytes accessed | tf_op | source)
XLA Modules:
  0.0 855.8 jit_solution(16955697094173695204)
XLA Ops:
  119.5 10.5 %collective-permute-done.19 = bf16[256,1536]{1,0:T(8,128)(2,1)S(1)} collective-permute-done((bf16[256,1536]{1,0:T(8,128)(2,1)}, bf16[256,1536]{1,0:T(8,128)(2,1)S(1)}, u32[]{:S(2)}, u32[]{:S(2)}) %collective-permute-start.19) | collective-permute-done | bytes 786464 | tf_op jit(solution)/shard_map/ppermute | solution.py:78
  137.9 13.2 %collective-permute-done.22 = bf16[128,1536]{1,0:T(8,128)(2,1)S(1)} collective-permute-done((bf16[128,1536]{1,0:T(8,128)(2,1)S(1)}, bf16[128,1536]{1,0:T(8,128)(2,1)S(1)}, u32[]{:S(2)}, u32[]{:S(2)}) %collective-permute-start.22) | collective-permute-done | bytes 393248 | tf_op jit(solution)/shard_map/ppermute | solution.py:77
  159.5 11.5 %fusion.46.qkv = f32[1024,1536]{1,0:T(8,128)} fusion(bf16[2048,1536]{1,0:T(8,128)(2,1)} %constant_dynamic-update-slice_fusion.52, bf16[1024,2048]{1,0:T(8,128)(2,1)S(1)} %pad_maximum_fusion, f32[2048]{0:T(1024)S(1)} %bitcast.169, f32[2048]{0:T(1024)S(1)} %bitcast.152, f32[1024]{0:T(1024)S(1)} %add_rsqrt_fusion, f32[1024]{0:T(1024)S(1)} %broadcast_multiply_fusion.2), kind=kOutput, calls=%fused_computation.289 | convolution fusion | flops 6455033856 | bytes 16801792 | tf_op jit(solution)/shard_map/dot_general | solution.py:33
  171.0 16.0 %shard_map.239 = (bf16[1024,768]{1,0:T(8,128)(2,1)}, bf16[1024,256]{1,0:T(8,128)(2,1)}) custom-call(s32[4]{0:T(128)} %iota_xor_fusion.slot_ref, s32[4]{0:T(128)} %and_select_fusion.3.first_ref, f32[1024,1536]{1,0:T(8,128)} %fusion.46.qkv, f32[1,1536]{1,0:T(1,128)} %reshape.281.bias, f32[1024,128]{1,0:T(8,128)} %get-tuple-element.313.cosine, ...), custom_call_target="tpu_custom_call" | custom-call | flops 1610612736 | bytes 6291456 | tf_op jit(solution)/shard_map/pallas_call | solution.py:549
  193.8 15.8 %shard_map.240 = (bf16[1024,768]{1,0:T(8,128)(2,1)}, bf16[1024,256]{1,0:T(8,128)(2,1)}) custom-call(s32[4]{0:T(128)} %iota_xor_fusion.slot_ref, s32[4]{0:T(128)} %and_select_fusion.3.first_ref, f32[1024,1536]{1,0:T(8,128)} %fusion.46.qkv, f32[1,1536]{1,0:T(1,128)} %reshape.281.bias, f32[1024,128]{1,0:T(8,128)} %get-tuple-element.313.cosine, ...), custom_call_target="tpu_custom_call" | custom-call | flops 1610612736 | bytes 6291456 | tf_op jit(solution)/shard_map/pallas_call | solution.py:549
  239.9 7.8 collective-permute-done.38
  270.7 7.8 collective-permute-done.44
  287.0 8.2 fusion.63
  295.2 7.8 collective-permute-done.51
  305.8 14.3 %multiply_convert_fusion.1 = (bf16[1408,1024]{1,0:T(8,128)(2,1)}, f32[1408,1024]{1,0:T(8,128)}) fusion(f32[1408,1024]{1,0:T(8,128)} %fusion.63, bf16[1408,2048]{1,0:T(8,128)(2,1)} %constant_dynamic-update-slice_fusion.28, bf16[256,2048]{1,0:T(8,128)(2,1)S(1)} %collective-permute-done.45, bf16[256,2048]{1,0:T(8,128)(2,1)S(1)} %collective-permute-done.44, ...), kind=kOutput, calls=%fused_computation.19 | convolution fusion | flops 5931008000 | bytes 24379392 | tf_op jit(solution)/shard_map/dot_general | solution.py:37
  332.6 7.0 fusion.61
  344.0 24.1 %collective-permute-done.58 = bf16[256,2048]{1,0:T(8,128)(2,1)S(1)} collective-permute-done((bf16[256,2048]{1,0:T(8,128)(2,1)S(1)}, bf16[256,2048]{1,0:T(8,128)(2,1)S(1)}, u32[]{:S(2)}, u32[]{:S(2)}) %collective-permute-start.58) | collective-permute-done | bytes 1048608 | tf_op jit(solution)/shard_map/ppermute | solution.py:133
  372.6 24.4 %collective-permute-done.60 = bf16[256,2048]{1,0:T(8,128)(2,1)} collective-permute-done((bf16[256,2048]{1,0:T(8,128)(2,1)}, bf16[256,2048]{1,0:T(8,128)(2,1)}, u32[]{:S(2)}, u32[]{:S(2)}) %collective-permute-start.60) | collective-permute-done | bytes 1048608 | tf_op jit(solution)/shard_map/ppermute | solution.py:124
  400.1 8.9 %convolution_convert_fusion.2 = bf16[1408,2048]{1,0:T(8,128)(2,1)S(1)} fusion(bf16[1408,1024]{1,0:T(8,128)(2,1)} %get-tuple-element.144, bf16[256,2048]{1,0:T(8,128)(2,1)} %collective-permute-done.61, bf16[256,2048]{1,0:T(8,128)(2,1)} %collective-permute-done.60, bf16[256,2048]{1,0:T(8,128)(2,1)} %collective-permute-done.59, ...), kind=kOutput, calls=%fused_computation.15 | convolution fusion | flops 5925240832 | bytes 12845056 | tf_op jit(solution)/shard_map/dot_general | solution.py:33
  413.7 15.9 %add_convert_fusion = (bf16[1408,1024]{1,0:T(8,128)(2,1)}, bf16[1408,1024]{1,0:T(8,128)(2,1)}) fusion(f32[1408,1024]{1,0:T(8,128)} %fusion.63, f32[1408,1024]{1,0:T(8,128)} %get-tuple-element.327, bf16[1408,2048]{1,0:T(8,128)(2,1)} %copy-done.56, bf16[256,2048]{1,0:T(8,128)(2,1)} %collective-permute-done.61, bf16[256,2048]{1,0:T(8,128)(2,1)} %collective-permute-done.60, ...), kind=kOutput, calls=%fused_computation.18 | convolution fusion | flops 5942542336 | bytes 27262976 | tf_op jit(solution)/shard_map/dot_general | solution.py:37
  429.6 10.0 %fusion.64 = f32[1024,2048]{1,0:T(8,128)S(1)} fusion(bf16[1408,1024]{1,0:T(8,128)(2,1)} %get-tuple-element.234, bf16[1408,2048]{1,0:T(8,128)(2,1)} %constant_dynamic-update-slice_fusion.28), kind=kOutput, calls=%fused_computation.305 | convolution fusion | flops 5905580032 | bytes 17039360 | tf_op jit(solution)/shard_map/dot_general | solution.py:41
  443.4 6.4 convolution_convert_fusion.1
  449.8 9.5 %collective-permute-done.64 = bf16[176,2048]{1,0:T(8,128)(2,1)S(1)} collective-permute-done((bf16[176,2048]{1,0:T(8,128)(2,1)S(1)}, bf16[176,2048]{1,0:T(8,128)(2,1)S(1)}, u32[]{:S(2)}, u32[]{:S(2)}) %collective-permute-start.64) | collective-permute-done | bytes 720928 | tf_op jit(solution)/shard_map/ppermute | solution.py:105
  467.3 8.9 %convolution_add_fusion = f32[1024,2048]{1,0:T(8,128)S(1)} fusion(f32[1024,2048]{1,0:T(8,128)S(1)} %fusion.64, bf16[1408,1024]{1,0:T(8,128)(2,1)} %get-tuple-element.233, bf16[1408,2048]{1,0:T(8,128)(2,1)S(1)} %bitcast.141), kind=kOutput, calls=%fused_computation.27 | convolution fusion | flops 5907677184 | bytes 25427968 | tf_op jit(solution)/shard_map/dot_general | solution.py:41
  476.2 10.6 %collective-permute-done.68 = bf16[88,2048]{1,0:T(8,128)(2,1)S(1)} collective-permute-done((bf16[88,2048]{1,0:T(8,128)(2,1)}, bf16[88,2048]{1,0:T(8,128)(2,1)S(1)}, u32[]{:S(2)}, u32[]{:S(2)}) %collective-permute-start.68) | collective-permute-done | bytes 360480 | tf_op jit(solution)/shard_map/ppermute | solution.py:105
  500.1 6.4 convolution_convert_fusion
  506.5 18.2 %collective-permute-done.72 = bf16[256,2048]{1,0:T(8,128)(2,1)S(1)} collective-permute-done((bf16[256,2048]{1,0:T(8,128)(2,1)S(1)}, bf16[256,2048]{1,0:T(8,128)(2,1)S(1)}, u32[]{:S(2)}, u32[]{:S(2)}) %collective-permute-start.72) | collective-permute-done | bytes 1048608 | tf_op jit(solution)/shard_map/ppermute | solution.py:133
  544.5 13.0 %collective-permute-done.78 = bf16[256,2048]{1,0:T(8,128)(2,1)S(1)} collective-permute-done((bf16[256,2048]{1,0:T(8,128)(2,1)}, bf16[256,2048]{1,0:T(8,128)(2,1)S(1)}, u32[]{:S(2)}, u32[]{:S(2)}) %collective-permute-start.78) | collective-permute-done | bytes 1048608 | tf_op jit(solution)/shard_map/ppermute | solution.py:124
  571.9 20.3 %shard_map.241 = bf16[1024,768]{1,0:T(8,128)(2,1)} custom-call(s32[4]{0:T(128)} %iota_xor_fusion.slot_ref, s32[4]{0:T(128)} %and_select_fusion.3.first_ref, bf16[1024,768]{1,0:T(8,128)(2,1)} %get-tuple-element.147.turned, bf16[1024,512]{1,0:T(8,128)(2,1)} %convolution_convert_fusion.6.out_grad, f32[1024,128]{1,0:T(8,128)} %get-tuple-element.313.cosine, ...), custom_call_target="tpu_custom_call" | custom-call | flops 4026531840 | bytes 4718592 | tf_op jit(solution)/shard_map/pallas_call | solution.py:674
  592.3 6.8 convolution_convert_fusion.4
  610.6 20.2 %shard_map.242 = bf16[1024,768]{1,0:T(8,128)(2,1)} custom-call(s32[4]{0:T(128)} %iota_xor_fusion.slot_ref, s32[4]{0:T(128)} %and_select_fusion.3.first_ref, bf16[1024,768]{1,0:T(8,128)(2,1)} %get-tuple-element.176.turned, bf16[1024,512]{1,0:T(8,128)(2,1)} %convolution_convert_fusion.6.out_grad, f32[1024,128]{1,0:T(8,128)} %get-tuple-element.313.cosine, ...), custom_call_target="tpu_custom_call" | custom-call | flops 4026531840 | bytes 4718592 | tf_op jit(solution)/shard_map/pallas_call | solution.py:674
  646.9 10.8 %fusion.62 = (bf16[1024,2048]{1,0:T(8,128)(2,1)S(1)}, f32[1024,2048]{1,0:T(8,128)}) fusion(bf16[1024,1536]{1,0:T(8,128)(2,1)S(1)} %pad_maximum_fusion.4, bf16[2048,1536]{1,0:T(8,128)(2,1)} %constant_dynamic-update-slice_fusion.52), kind=kOutput, calls=%fused_computation.303 | convolution fusion | flops 6444548096 | bytes 22020096 | tf_op jit(solution)/shard_map/dot_general | solution.py:37
  687.9 10.8 %collective-permute-done.100 = bf16[176,2048]{1,0:T(8,128)(2,1)S(1)} collective-permute-done((bf16[176,2048]{1,0:T(8,128)(2,1)}, bf16[176,2048]{1,0:T(8,128)(2,1)S(1)}, u32[]{:S(2)}, u32[]{:S(2)}) %collective-permute-start.100) | collective-permute-done | bytes 720928 | tf_op jit(solution)/shard_map/ppermute | solution.py:106
  727.6 7.3 collective-permute-done.109
  752.2 17.1 %collective-permute-done.117 = f32[128]{0:T(128)S(1)} collective-permute-done((f32[128]{0:T(128)S(1)}, f32[128]{0:T(128)S(1)}, u32[]{:S(2)}, u32[]{:S(2)}) %collective-permute-start.117) | collective-permute-done | bytes 544 | tf_op jit(solution)/shard_map/ppermute | solution.py:243
  785.9 8.1 shard_map.244
  798.9 7.1 collective-permute-done.124
  (694 shorter events, 455.2 us)
Async XLA Ops:
  4.8 46.1 %collective-permute-start.1 = (bf16[256,1536]{1,0:T(8,128)(2,1)}, bf16[256,1536]{1,0:T(8,128)(2,1)S(1)}, u32[]{:S(2)}, u32[]{:S(2)}) collective-permute-start(bf16[256,1536]{1,0:T(8,128)(2,1)} %shard_map.238), channel_id=1, source_target_pairs={{2,0},{4,2},{6,4},{7,6},{5,7},{3,5},{1,3},{0,1},{10,8},{12,10},{14... | collective-permute-start | bytes 2359304 | tf_op jit(solution)/shard_map/ppermute | solution.py:78
  7.8 43.6 %collective-permute-start = (bf16[256,1536]{1,0:T(8,128)(2,1)}, bf16[256,1536]{1,0:T(8,128)(2,1)S(1)}, u32[]{:S(2)}, u32[]{:S(2)}) collective-permute-start(bf16[256,1536]{1,0:T(8,128)(2,1)} %shard_map.238), channel_id=1, source_target_pairs={{0,2},{2,4},{4,6},{6,7},{7,5},{5,3},{3,1},{1,0},{8,10},{10,12},{12... | collective-permute-start | bytes 2359304 | tf_op jit(solution)/shard_map/ppermute | solution.py:77
  11.7 63.4 %collective-permute-start.5 = (bf16[256,2048]{1,0:T(8,128)(2,1)S(1)}, bf16[256,2048]{1,0:T(8,128)(2,1)}, u32[]{:S(2)}, u32[]{:S(2)}) collective-permute-start(bf16[256,2048]{1,0:T(8,128)(2,1)S(1)} %bitcast.135), channel_id=1, source_target_pairs={{0,16},{8,24},{16,0},{24,8},{1,17},{9,25},{17,1},{25,9},{2,18},{10... | collective-permute-start | bytes 3145736 | tf_op jit(solution)/shard_map/ppermute | solution.py:124
  47.1 70.3 %collective-permute-start.4 = (bf16[256,2048]{1,0:T(8,128)(2,1)S(1)}, bf16[256,2048]{1,0:T(8,128)(2,1)}, u32[]{:S(2)}, u32[]{:S(2)}) collective-permute-start(bf16[256,2048]{1,0:T(8,128)(2,1)S(1)} %bitcast.136), channel_id=1, source_target_pairs={{0,8},{8,0},{16,24},{24,16},{1,9},{9,1},{17,25},{25,17},{2,10},{10... | collective-permute-start | bytes 3145736 | tf_op jit(solution)/shard_map/ppermute | solution.py:125
  75.2 42.2 %collective-permute-start.6 = (bf16[256,2048]{1,0:T(8,128)(2,1)}, bf16[256,2048]{1,0:T(8,128)(2,1)}, u32[]{:S(2)}, u32[]{:S(2)}) collective-permute-start(bf16[256,2048]{1,0:T(8,128)(2,1)} %collective-permute-done.5), channel_id=1, source_target_pairs={{0,8},{8,0},{16,24},{24,16},{1,9},{9,1},{17,25},{25,17},{2,10},{10... | collective-permute-start | bytes 3145736 | tf_op jit(solution)/shard_map/ppermute | solution.py:126
  86.2 28.9 %collective-permute-start.17 = (f32[15,128]{1,0:T(8,128)S(1)}, f32[15,128]{1,0:T(8,128)S(1)}, u32[]{:S(2)}, u32[]{:S(2)}) collective-permute-start(f32[15,128]{1,0:T(8,128)S(1)} %pad_bitcast_fusion), channel_id=1, source_target_pairs={{0,7},{1,6},{2,5},{3,4},{4,3},{5,2},{6,1},{7,0},{8,15},{9,14},{10,... | collective-permute-start | bytes 23048 | tf_op jit(solution)/shard_map/ppermute | solution.py:230
  155.4 31.5 %collective-permute-start.29 = (bf16[176,2048]{1,0:T(8,128)(2,1)}, bf16[176,2048]{1,0:T(8,128)(2,1)}, u32[]{:S(2)}, u32[]{:S(2)}) collective-permute-start(bf16[176,2048]{1,0:T(8,128)(2,1)} %get-tuple-element.124), channel_id=1, source_target_pairs={{2,0},{4,2},{6,4},{7,6},{5,7},{3,5},{1,3},{0,1},{10,8},{12,10},{14... | collective-permute-start | bytes 2162696 | tf_op jit(solution)/shard_map/ppermute | solution.py:78
  156.3 30.6 %collective-permute-start.28 = (bf16[176,2048]{1,0:T(8,128)(2,1)}, bf16[176,2048]{1,0:T(8,128)(2,1)}, u32[]{:S(2)}, u32[]{:S(2)}) collective-permute-start(bf16[176,2048]{1,0:T(8,128)(2,1)} %get-tuple-element.124), channel_id=1, source_target_pairs={{0,2},{2,4},{4,6},{6,7},{7,5},{5,3},{3,1},{1,0},{8,10},{10,12},{12... | collective-permute-start | bytes 2162696 | tf_op jit(solution)/shard_map/ppermute | solution.py:77
  157.5 29.5 %collective-permute-start.26 = (bf16[176,2048]{1,0:T(8,128)(2,1)}, bf16[176,2048]{1,0:T(8,128)(2,1)}, u32[]{:S(2)}, u32[]{:S(2)}) collective-permute-start(bf16[176,2048]{1,0:T(8,128)(2,1)} %collective-permute-done.24), channel_id=1, source_target_pairs={{0,2},{2,4},{4,6},{6,7},{7,5},{5,3},{3,1},{1,0},{8,10},{10,12},{12... | collective-permute-start | bytes 2162696 | tf_op jit(solution)/shard_map/ppermute | solution.py:77
  157.6 29.3 %collective-permute-start.27 = (bf16[176,2048]{1,0:T(8,128)(2,1)}, bf16[176,2048]{1,0:T(8,128)(2,1)}, u32[]{:S(2)}, u32[]{:S(2)}) collective-permute-start(bf16[176,2048]{1,0:T(8,128)(2,1)} %collective-permute-done.25), channel_id=1, source_target_pairs={{2,0},{4,2},{6,4},{7,6},{5,7},{3,5},{1,3},{0,1},{10,8},{12,10},{14... | collective-permute-start | bytes 2162696 | tf_op jit(solution)/shard_map/ppermute | solution.py:78
  411.4 28.2 %collective-permute-start.63 = (bf16[88,2048]{1,0:T(8,128)(2,1)S(1)}, bf16[88,2048]{1,0:T(8,128)(2,1)S(1)}, u32[]{:S(2)}, u32[]{:S(2)}) collective-permute-start(bf16[88,2048]{1,0:T(8,128)(2,1)S(1)} %get-tuple-element.261), channel_id=1, source_target_pairs={{2,0},{4,2},{6,4},{7,6},{5,7},{3,5},{1,3},{0,1},{10,8},{12,10},{14... | collective-permute-start | bytes 1081352 | tf_op jit(solution)/shard_map/ppermute | solution.py:106
  492.4 32.8 %collective-permute-start.75 = (bf16[176,2048]{1,0:T(8,128)(2,1)S(1)}, bf16[176,2048]{1,0:T(8,128)(2,1)S(1)}, u32[]{:S(2)}, u32[]{:S(2)}) collective-permute-start(bf16[176,2048]{1,0:T(8,128)(2,1)S(1)} %pad_maximum_fusion.7), channel_id=1, source_target_pairs={{0,2},{2,4},{4,6},{6,7},{7,5},{5,3},{3,1},{1,0},{8,10},{10,12},{12... | collective-permute-start | bytes 2162696 | tf_op jit(solution)/shard_map/ppermute | solution.py:105
  493.8 31.4 %collective-permute-start.76 = (bf16[176,2048]{1,0:T(8,128)(2,1)S(1)}, bf16[176,2048]{1,0:T(8,128)(2,1)S(1)}, u32[]{:S(2)}, u32[]{:S(2)}) collective-permute-start(bf16[176,2048]{1,0:T(8,128)(2,1)S(1)} %pad_maximum_fusion.8), channel_id=1, source_target_pairs={{2,0},{4,2},{6,4},{7,6},{5,7},{3,5},{1,3},{0,1},{10,8},{12,10},{14... | collective-permute-start | bytes 2162696 | tf_op jit(solution)/shard_map/ppermute | solution.py:106
  496.5 29.3 %collective-permute-start.73 = (bf16[176,2048]{1,0:T(8,128)(2,1)S(1)}, bf16[176,2048]{1,0:T(8,128)(2,1)S(1)}, u32[]{:S(2)}, u32[]{:S(2)}) collective-permute-start(bf16[176,2048]{1,0:T(8,128)(2,1)S(1)} %get-tuple-element.160), channel_id=1, source_target_pairs={{0,2},{2,4},{4,6},{6,7},{7,5},{5,3},{3,1},{1,0},{8,10},{10,12},{12... | collective-permute-start | bytes 2162696 | tf_op jit(solution)/shard_map/ppermute | solution.py:105
  497.9 29.3 %collective-permute-start.74 = (bf16[176,2048]{1,0:T(8,128)(2,1)S(1)}, bf16[176,2048]{1,0:T(8,128)(2,1)}, u32[]{:S(2)}, u32[]{:S(2)}) collective-permute-start(bf16[176,2048]{1,0:T(8,128)(2,1)S(1)} %get-tuple-element.161), channel_id=1, source_target_pairs={{2,0},{4,2},{6,4},{7,6},{5,7},{3,5},{1,3},{0,1},{10,8},{12,10},{14... | collective-permute-start | bytes 2162696 | tf_op jit(solution)/shard_map/ppermute | solution.py:106
  537.4 186.6 %collective-permute-start.122 = (bf16[176,2048]{1,0:T(8,128)(2,1)}, bf16[176,2048]{1,0:T(8,128)(2,1)}, u32[]{:S(2)}, u32[]{:S(2)}) collective-permute-start(bf16[176,2048]{1,0:T(8,128)(2,1)} %add_convert_fusion.5.p0), channel_id=1, source_target_pairs={{0,16},{8,24},{16,0},{24,8},{1,17},{9,25},{17,1},{25,9},{2,18},{10... | collective-permute-start | bytes 2162696 | tf_op jit(solution)/shard_map/ppermute | solution.py:124
  567.7 31.4 %collective-permute-start.86 = (bf16[176,2048]{1,0:T(8,128)(2,1)}, bf16[176,2048]{1,0:T(8,128)(2,1)}, u32[]{:S(2)}, u32[]{:S(2)}) collective-permute-start(bf16[176,2048]{1,0:T(8,128)(2,1)} %pad_maximum_fusion.9), channel_id=1, source_target_pairs={{0,2},{2,4},{4,6},{6,7},{7,5},{5,3},{3,1},{1,0},{8,10},{10,12},{12... | collective-permute-start | bytes 2162696 | tf_op jit(solution)/shard_map/ppermute | solution.py:105
  569.1 30.1 %collective-permute-start.87 = (bf16[176,2048]{1,0:T(8,128)(2,1)S(1)}, bf16[176,2048]{1,0:T(8,128)(2,1)}, u32[]{:S(2)}, u32[]{:S(2)}) collective-permute-start(bf16[176,2048]{1,0:T(8,128)(2,1)S(1)} %copy-done.32), channel_id=1, source_target_pairs={{2,0},{4,2},{6,4},{7,6},{5,7},{3,5},{1,3},{0,1},{10,8},{12,10},{14... | collective-permute-start | bytes 2162696 | tf_op jit(solution)/shard_map/ppermute | solution.py:106
  569.8 32.3 %collective-permute-start.84 = (bf16[176,2048]{1,0:T(8,128)(2,1)}, bf16[176,2048]{1,0:T(8,128)(2,1)}, u32[]{:S(2)}, u32[]{:S(2)}) collective-permute-start(bf16[176,2048]{1,0:T(8,128)(2,1)} %get-tuple-element.171), channel_id=1, source_target_pairs={{0,2},{2,4},{4,6},{6,7},{7,5},{5,3},{3,1},{1,0},{8,10},{10,12},{12... | collective-permute-start | bytes 2162696 | tf_op jit(solution)/shard_map/ppermute | solution.py:105
  571.1 31.8 %collective-permute-start.85 = (bf16[176,2048]{1,0:T(8,128)(2,1)}, bf16[176,2048]{1,0:T(8,128)(2,1)}, u32[]{:S(2)}, u32[]{:S(2)}) collective-permute-start(bf16[176,2048]{1,0:T(8,128)(2,1)} %get-tuple-element.172), channel_id=1, source_target_pairs={{2,0},{4,2},{6,4},{7,6},{5,7},{3,5},{1,3},{0,1},{10,8},{12,10},{14... | collective-permute-start | bytes 2162696 | tf_op jit(solution)/shard_map/ppermute | solution.py:106
  606.4 36.4 %collective-permute-start.88 = (bf16[176,2048]{1,0:T(8,128)(2,1)}, bf16[176,2048]{1,0:T(8,128)(2,1)}, u32[]{:S(2)}, u32[]{:S(2)}) collective-permute-start(bf16[176,2048]{1,0:T(8,128)(2,1)} %get-tuple-element.177), channel_id=1, source_target_pairs={{0,2},{2,4},{4,6},{6,7},{7,5},{5,3},{3,1},{1,0},{8,10},{10,12},{12... | collective-permute-start | bytes 2162696 | tf_op jit(solution)/shard_map/ppermute | solution.py:105
  607.1 35.7 %collective-permute-start.89 = (bf16[176,2048]{1,0:T(8,128)(2,1)}, bf16[176,2048]{1,0:T(8,128)(2,1)}, u32[]{:S(2)}, u32[]{:S(2)}) collective-permute-start(bf16[176,2048]{1,0:T(8,128)(2,1)} %get-tuple-element.178), channel_id=1, source_target_pairs={{2,0},{4,2},{6,4},{7,6},{5,7},{3,5},{1,3},{0,1},{10,8},{12,10},{14... | collective-permute-start | bytes 2162696 | tf_op jit(solution)/shard_map/ppermute | solution.py:106
  646.3 41.6 %collective-permute-start.99 = (bf16[176,2048]{1,0:T(8,128)(2,1)}, bf16[176,2048]{1,0:T(8,128)(2,1)}, u32[]{:S(2)}, u32[]{:S(2)}) collective-permute-start(bf16[176,2048]{1,0:T(8,128)(2,1)} %get-tuple-element.189), channel_id=1, source_target_pairs={{0,2},{2,4},{4,6},{6,7},{7,5},{5,3},{3,1},{1,0},{8,10},{10,12},{12... | collective-permute-start | bytes 2162696 | tf_op jit(solution)/shard_map/ppermute | solution.py:105
  682.5 31.7 %collective-permute-start.92 = (bf16[256,2048]{1,0:T(8,128)(2,1)}, bf16[256,2048]{1,0:T(8,128)(2,1)S(1)}, u32[]{:S(2)}, u32[]{:S(2)}) collective-permute-start(bf16[256,2048]{1,0:T(8,128)(2,1)} %get-tuple-element.267), channel_id=1, source_target_pairs={{0,8},{8,0},{16,24},{24,16},{1,9},{9,1},{17,25},{25,17},{2,10},{10... | collective-permute-start | bytes 3145736 | tf_op jit(solution)/shard_map/ppermute | solution.py:131
  687.1 28.0 %collective-permute-start.94 = (bf16[256,2048]{1,0:T(8,128)(2,1)S(1)}, bf16[256,2048]{1,0:T(8,128)(2,1)S(1)}, u32[]{:S(2)}, u32[]{:S(2)}) collective-permute-start(bf16[256,2048]{1,0:T(8,128)(2,1)S(1)} %fusion.21), channel_id=1, source_target_pairs={{0,16},{8,24},{16,0},{24,8},{1,17},{9,25},{17,1},{25,9},{2,18},{10... | collective-permute-start | bytes 3145736 | tf_op jit(solution)/shard_map/ppermute | solution.py:133
  727.6 44.2 %collective-permute-start.121 = (bf16[176,2048]{1,0:T(8,128)(2,1)}, bf16[176,2048]{1,0:T(8,128)(2,1)}, u32[]{:S(2)}, u32[]{:S(2)}) collective-permute-start(bf16[176,2048]{1,0:T(8,128)(2,1)} %add_convert_fusion.5.p0), channel_id=1, source_target_pairs={{0,8},{8,0},{16,24},{24,16},{1,9},{9,1},{17,25},{25,17},{2,10},{10... | collective-permute-start | bytes 2162696 | tf_op jit(solution)/shard_map/ppermute | solution.py:125
  735.0 36.8 %collective-permute-start.123 = (bf16[176,2048]{1,0:T(8,128)(2,1)}, bf16[176,2048]{1,0:T(8,128)(2,1)}, u32[]{:S(2)}, u32[]{:S(2)}) collective-permute-start(bf16[176,2048]{1,0:T(8,128)(2,1)} %collective-permute-done.122.p2), channel_id=1, source_target_pairs={{0,8},{8,0},{16,24},{24,16},{1,9},{9,1},{17,25},{25,17},{2,10},{10... | collective-permute-start | bytes 2162696 | tf_op jit(solution)/shard_map/ppermute | solution.py:126
  735.0 42.1 %collective-permute-start.126 = (bf16[176,2048]{1,0:T(8,128)(2,1)}, bf16[176,2048]{1,0:T(8,128)(2,1)}, u32[]{:S(2)}, u32[]{:S(2)}) collective-permute-start(bf16[176,2048]{1,0:T(8,128)(2,1)} %add_convert_fusion.4.refs_0_), channel_id=1, source_target_pairs={{0,16},{8,24},{16,0},{24,8},{1,17},{9,25},{17,1},{25,9},{2,18},{10... | collective-permute-start | bytes 2162696 | tf_op jit(solution)/shard_map/ppermute | solution.py:124
  740.8 36.8 %collective-permute-start.129 = (bf16[176,2048]{1,0:T(8,128)(2,1)}, bf16[176,2048]{1,0:T(8,128)(2,1)}, u32[]{:S(2)}, u32[]{:S(2)}) collective-permute-start(bf16[176,2048]{1,0:T(8,128)(2,1)} %add_convert_fusion.3.refs_4_), channel_id=1, source_target_pairs={{0,16},{8,24},{16,0},{24,8},{1,17},{9,25},{17,1},{25,9},{2,18},{10... | collective-permute-start | bytes 2162696 | tf_op jit(solution)/shard_map/ppermute | solution.py:124
  785.0 29.3 %collective-permute-start.119 = (bf16[256,768]{1,0:T(8,128)(2,1)S(1)}, bf16[256,768]{1,0:T(8,128)(2,1)}, u32[]{:S(2)}, u32[]{:S(2)}) collective-permute-start(bf16[256,768]{1,0:T(8,128)(2,1)S(1)} %add_convert_fusion.23.refs_0_), channel_id=1, source_target_pairs={{0,16},{8,24},{16,0},{24,8},{1,17},{9,25},{17,1},{25,9},{2,18},{10... | collective-permute-start | bytes 1179656 | tf_op jit(solution)/shard_map/ppermute | solution.py:124
  814.3 33.8 %collective-permute-start.118 = (bf16[256,768]{1,0:T(8,128)(2,1)S(1)}, bf16[256,768]{1,0:T(8,128)(2,1)}, u32[]{:S(2)}, u32[]{:S(2)}) collective-permute-start(bf16[256,768]{1,0:T(8,128)(2,1)S(1)} %add_convert_fusion.23.refs_0_), channel_id=1, source_target_pairs={{0,8},{8,0},{16,24},{24,16},{1,9},{9,1},{17,25},{25,17},{2,10},{10... | collective-permute-start | bytes 1179656 | tf_op jit(solution)/shard_map/ppermute | solution.py:125
  814.4 33.7 %collective-permute-start.120 = (bf16[256,768]{1,0:T(8,128)(2,1)}, bf16[256,768]{1,0:T(8,128)(2,1)}, u32[]{:S(2)}, u32[]{:S(2)}) collective-permute-start(bf16[256,768]{1,0:T(8,128)(2,1)} %collective-permute-done.119.refs_2_), channel_id=1, source_target_pairs={{0,8},{8,0},{16,24},{24,16},{1,9},{9,1},{17,25},{25,17},{2,10},{10... | collective-permute-start | bytes 1179656 | tf_op jit(solution)/shard_map/ppermute | solution.py:126
  (200 other events, 2919.9 us)

commit v3 on v2

--- a/solution.py
+++ b/solution.py
@@ -147,7 +147,7 @@
 
     def scatter(self, **wholes):
         for name, whole in wholes.items():
-            order = self.order if name in "FSO" else range(8)
+            order = self.order if name in "FS" else range(8)
             size = whole.shape[0] // 8
             self.rings[name] = RingScatter(
                 [lax.dynamic_slice_in_dim(whole, order[j] * size, size, 0) for j in range(8)]
@@ -159,12 +159,40 @@
             got += self.rings[name].step(*after)
         return got
 
+    def gather_out(self, w_out, small, count):
+        size = w_out.shape[0] // 4
+        self.out_rows = size
+        own = lax.dynamic_slice_in_dim(w_out, self.s * size, size, 0)
+        pad = jnp.full((w_out.shape[1] - small.shape[0],), count.astype(BF16))
+        line = jnp.broadcast_to(jnp.concatenate([small, pad])[None], (16, w_out.shape[1]))
+        self.gather(o=jnp.concatenate([own, line]))
+
+    def close_out(self):
+        whole = self.as_found(self.rings["o"])
+        whole = whole.reshape(8, -1, whole.shape[1])
+        places = (jnp.asarray(PLACE) - jnp.asarray(PLACE)[self.f]) % 8
+        rows = jnp.take(whole[:, : self.out_rows], places, axis=0)
+        small = jnp.take(whole[:, self.out_rows], places, axis=0)
+        return rows.reshape(-1, whole.shape[2]), small.astype(F32)
+
     def whole(self, name):
-        form = {"q": self.in_order, "o": self.shuffled}.get(name, self.as_found)
-        return form(self.rings[name])
+        return self.in_order(self.rings[name]) if name == "q" else self.as_found(self.rings[name])
+
+    def scatter_first(self, raw_first, raw_out, *after):
+        rows, cols = raw_out.shape
+        split = raw_out.reshape(8, rows // 8, 4, cols // 4).transpose(0, 2, 1, 3)
+        both = jnp.concatenate([raw_first, split.reshape(-1, cols // 4)], axis=1)
+        self.first_cols = raw_first.shape[1]
+        self.scatter(F=pin(both, *after))
 
     def total(self, name):
-        return self.rings[name].total
+        if name not in "FO":
+            return self.rings[name].total
+        total = self.rings["F"].total
+        if name == "F":
+            return total[:, : self.first_cols]
+        split = total[:, self.first_cols :].reshape(4, self.out_rows, -1)
+        return split.transpose(1, 0, 2).reshape(self.out_rows, -1)
 
     def in_order(self, ring):
         size, cols = ring.blocks[0].shape
@@ -174,21 +202,11 @@
             whole = lax.dynamic_update_slice(whole, part, (at, 0))
         return whole
 
-    def shuffled(self, ring):
-        size, cols = ring.blocks[0].shape
-        whole = self.as_found(ring).reshape(8, size, cols)
-        places = (jnp.asarray(PLACE) - jnp.asarray(PLACE)[self.f]) % 8
-        return jnp.take(whole, places, axis=0).reshape(8 * size, cols)
-
     def as_found(self, ring):
         return jnp.concatenate([part for unused, unused, part in ring.pieces()])
 
     def pick_qkv(self, w_qkv):
         return pick_columns(w_qkv, self.s)
-
-    def own_out(self, w_out):
-        rows = w_out.shape[0] // 4
-        return lax.dynamic_slice_in_dim(w_out, self.s * rows, rows, 0)
 
     def bias_of_heads(self, full_bias):
         split = full_bias.reshape(3, 4, 2, 4, HD)
@@ -200,19 +218,19 @@
         here = (jnp.arange(4) == self.s).astype(F32)[None, None, None, :, None]
         return (split[:, :, :, None, :] * here).reshape(-1)
 
-    def final_qkv(self, shares, factor):
-        parts = [seq_gather(share.astype(BF16)) for share in shares]
-        return unpick_columns(parts, self.s, factor)
-
-    def final_rows(self, share, factor):
-        return place_rows(seq_gather(share.astype(BF16)), self.s, factor)
-
-    def final_out(self, share, factor):
-        return self.final_rows(share, factor)
+    def spread(self, name):
+        return seq_gather(self.total(name).astype(BF16))
+
+    def final_qkv(self, first, second, factor):
+        return unpick_columns([first, second], self.s, factor)
+
+    def final_rows(self, parts, factor):
+        return place_rows(parts, self.s, factor)
+
+    final_out = final_rows
 
     def final_pairs(self, first, second, factor):
-        parts = [seq_gather(share.astype(BF16)) for share in (first, second)]
-        return place_pairs(parts[0] + parts[1], self.s, factor)
+        return place_pairs(first + second, self.s, factor)
 
     def tokens(self, mine):
         return jnp.concatenate(seq_gather(mine))
@@ -224,12 +242,6 @@
     def by_slot(self, values):
         split = values.reshape((4, values.shape[0] // 4) + values.shape[1:])
         return jnp.take(split, self.slots, axis=0).reshape(values.shape)
-
-    def small_gather(self, mine):
-        got = [mine] + [
-            lax.ppermute(mine, "fsdp", [(i, i ^ k) for i in range(8)]) for k in range(1, 8)
-        ]
-        return jnp.take(jnp.stack(got), self.f ^ jnp.arange(8), axis=0)
 
     def small_reduce(self, values):
         total = jnp.take(values, self.f ^ jnp.arange(8), axis=0)
@@ -267,11 +279,21 @@
     def hop(self, names, *after):
         return ()
 
+    def gather_out(self, w_out, small, count):
+        self.gather(o=w_out)
+        small = jnp.concatenate([small.astype(F32), jnp.full((LANES,), count)])
+        self.small = lax.all_gather(small, "fsdp", axis=0, tiled=False)
+
+    def close_out(self):
+        rows = self.wholes["o"].shape[0] // self.members
+        own = lax.dynamic_slice_in_dim(self.wholes["o"], self.s * rows, rows, 0)
+        return own, self.small
+
     def whole(self, name):
-        if name != "o":
-            return self.wholes[name]
-        rows = self.wholes[name].shape[0] // self.members
-        return lax.dynamic_slice_in_dim(self.wholes[name], self.s * rows, rows, 0)
+        return self.wholes[name]
+
+    def scatter_first(self, raw_first, raw_out, *after):
+        self.scatter(F=raw_first, O=raw_out)
 
     def total(self, name):
         return self.totals[name]
@@ -281,9 +303,6 @@
         own = lax.dynamic_index_in_dim(split, self.s, 2, keepdims=False)
         return own.transpose(0, 2, 1, 3).reshape(w_qkv.shape[0], -1)
 
-    def own_out(self, w_out):
-        return w_out
-
     def bias_of_heads(self, full_bias):
         split = full_bias.reshape(3, self.members, self.pairs, LANES)
         own = lax.dynamic_index_in_dim(split, self.s, 1, keepdims=False)
@@ -297,19 +316,23 @@
     def gathered(self, share):
         return lax.all_gather(share.astype(BF16), "seq", axis=0, tiled=False)
 
-    def final_qkv(self, shares, factor):
-        share = jnp.concatenate(shares, axis=1)
+    def spread(self, name):
+        return [self.total(name)]
+
+    def final_qkv(self, first, second, factor):
+        share = jnp.concatenate(first + second, axis=1)
         parts = self.gathered(share).reshape(self.members, -1, self.pairs, 3, LANES)
         return factor * parts.transpose(1, 3, 0, 2, 4).reshape(parts.shape[1], -1).astype(F32)
 
-    def final_rows(self, share, factor):
+    def final_rows(self, parts, factor):
+        share = parts[0]
         return factor * self.gathered(share).reshape(-1, share.shape[1]).astype(F32)
 
-    def final_out(self, share, factor):
-        return factor * lax.psum(share.astype(BF16), "seq").astype(F32)
+    def final_out(self, parts, factor):
+        return factor * lax.psum(parts[0].astype(BF16), "seq").astype(F32)
 
     def final_pairs(self, first, second, factor):
-        parts = jnp.stack([first, second], axis=1)
+        parts = jnp.stack(first + second, axis=1)
         parts = lax.all_gather(parts.astype(BF16), "seq", axis=0, tiled=True)
         return factor * parts.astype(F32)
 
@@ -322,9 +345,6 @@
 
     def by_slot(self, values):
         return values
-
-    def small_gather(self, mine):
-        return lax.all_gather(mine, "fsdp", axis=0, tiled=False)
 
     def small_reduce(self, values):
         total = lax.psum(values, ("seq", "fsdp"))
@@ -743,14 +763,19 @@
     tokens_all = net.tokens(tokens[0])
 
     mine_gate_up = lax.dynamic_slice_in_dim(w_gate_up, s * units, units, 0)
+    counted = valid[0].astype(F32)
+    small = jnp.concatenate([ln1_gain, ln1_bias, ln2_gain, ln2_bias, b_qkv])
+    net.gather_out(w_out, small, jnp.sum(counted))
     net.gather(
         q=net.pick_qkv(w_qkv),
-        o=net.own_out(w_out),
         g=mine_gate_up[:, 0],
         u=mine_gate_up[:, 1],
         d=lax.dynamic_slice_in_dim(w_down, s * units, units, 0),
     )
     done = net.hop("qo")
+
+    normed_all, unused = norm_parts(pin(tokens_all, *done).astype(F32))
+    done = net.hop("q")
 
     segment = pin(segments, *done)[0]
     slot_segment = net.by_slot(segment)
@@ -760,28 +785,20 @@
     first_slot = (
         jnp.sum((segment[None, :] < block_first[:, None]).astype(jnp.int32), axis=1) // rows
     )
-    tables = turn_tables(slot_place - slot_start)
-    done = net.hop("qo") + tables + (slot_start, first_slot)
-
-    counted = pin(valid, *done)[0].astype(F32)
-    small = [pin(v, *done) for v in (ln1_gain, ln1_bias, ln2_gain, ln2_bias, b_qkv)]
-    small = jnp.concatenate(small).astype(F32)
-    small = jnp.concatenate([small, jnp.full((LANES,), jnp.sum(counted))])
-    small = net.small_gather(small.reshape(-1, LANES)).reshape(shards, -1)
+    done = net.hop("q") + net.hop("o", *done)
+    tables = turn_tables(slot_place - pin(slot_start, *done))
+    net.hop("qo", *done)
+    net.hop("o")
+    full_out, small = net.close_out()
     gain_one, shift_one, gain_two, shift_two = (
         small[:, i * vec : (i + 1) * vec].reshape(width) for i in range(4)
     )
     own_bias = net.bias_of_heads(small[:, 4 * vec : 4 * vec + bias_share].reshape(-1))
     sum_count = net.seq_sum(jnp.sum(small[:, -LANES:], axis=0))[0]
     factor = (rows * members * shards) / sum_count
-    done = net.hop("qo")
-
-    tokens_all = pin(tokens_all, own_bias, *done)
-    normed_all, unused = norm_parts(tokens_all.astype(F32))
     hidden_one = (normed_all * gain_one + shift_one).astype(BF16)
-    net.hop("qo")
     done = net.hop("g", *done)
-    qkv = dot_nn(hidden_one, pin(net.whole("q"), *done))
+    qkv = dot_nn(hidden_one, pin(net.whole("q"), *done, *tables))
     half_pairs = pairs // 2
     forward = functools.partial(
         attention_forward,
@@ -793,13 +810,13 @@
         block=rows,
         pairs=half_pairs,
     )
-    turned_one, heads_one = forward(first_slot, skip=0)
+    turned_one, heads_one = forward(pin(first_slot, factor), skip=0)
     done = net.hop("gu", *done)
     turned_two, heads_two = forward(pin(first_slot, heads_one, *done), skip=half_pairs)
     heads_out = jnp.concatenate([heads_one, heads_two], axis=1)
     tokens_in = tokens[0].astype(F32)
     done = net.hop("gu", heads_one)
-    partial = dot_nn(pin(heads_out, *done), net.whole("o"))
+    partial = dot_nn(pin(heads_out, *done), full_out)
     attended = net.tokens_sum(partial)[0]
     done = net.hop("gu", heads_two)
     resid = tokens_in + pin(attended, *done)
@@ -835,25 +852,27 @@
 
     raw_gate = dot_nn(gate_grad, pin(hidden_two, *done)).astype(BF16)
     done = net.hop("D", gate_grad)
+    partial = dot_tn(gate_grad, pin(full_gate, raw_gate, *done))
 
     net.scatter(G=pin(raw_gate, *done))
-    partial = dot_tn(gate_grad, pin(full_gate, raw_gate, *done)) + dot_tn(up_grad, full_up)
-    done = net.hop("DG", raw_gate)
-
-    two_grad, far = net.tokens_sum(pin(partial, *done))
-    raw_up = dot_nn(up_grad, pin(hidden_two, far)).astype(BF16)
-    done = net.hop("DG", partial)
-
-    two_grad = pin(two_grad, raw_up, *done)
+    done = net.hop("G")
+    partial = partial + dot_tn(up_grad, pin(full_up, partial, *done))
+    two_grad, far = net.tokens_sum(partial)
+    done = net.hop("DG", *done)
+
+    raw_up = dot_nn(up_grad, pin(hidden_two, far, *done)).astype(BF16)
+    net.scatter(U=raw_up)
+    done = net.hop("D", *done)
+
+    two_grad = pin(two_grad, *done)
     resid_grad = cot + norm_back(two_grad, normed_two, inv_std_two, gain_two)
     gain_two_grad = jnp.sum(two_grad * normed_two, axis=0)
     shift_two_grad = jnp.sum(two_grad, axis=0)
     mine_low = resid_grad.astype(BF16)
     resid_low = net.tokens(mine_low)
-    net.scatter(U=pin(raw_up, *done))
-    done = net.hop("GU", raw_up)
-
-    full_out, full_qkv = net.whole("o"), net.whole("q")
+    done = net.hop("UG", *done)
+
+    full_qkv = net.whole("q")
     out_grad = dot_nt(pin(resid_low, *done), full_out).astype(BF16)
     backward = functools.partial(
         attention_backward,
@@ -862,27 +881,28 @@
         slot_of=net.slots,
         block=rows,
     )
-    grad_first = backward(turned_one, out_grad, first_slot=first_slot, skip=0)
+    raw_out = dot_tn(heads_out, pin(resid_low, out_grad)).astype(BF16)
+    grad_first = backward(turned_one, pin(out_grad, raw_out), first_slot=first_slot, skip=0)
     raw_first = dot_tn(hidden_one, grad_first).astype(BF16)
-    done = net.hop("GU", resid_low)
-
-    net.scatter(F=pin(raw_first, *done))
-    here = pin(first_slot, raw_first, *done)
+    done = net.hop("UG", resid_low)
+
+    net.scatter_first(raw_first, raw_out, *done)
+    parts_down = net.spread("D")
+    here = pin(first_slot, raw_first, *done, *parts_down)
     grad_second = backward(turned_two, out_grad, first_slot=here, skip=half_pairs)
-    done = net.hop("UF", raw_first)
-
-    qkv_grad = pin(jnp.concatenate([grad_first, grad_second], axis=1), *done)
+    done = net.hop("FU", raw_first)
+
+    parts_gate = net.spread("G")
+    qkv_grad = pin(jnp.concatenate([grad_first, grad_second], axis=1), *done, *parts_gate)
     partial = dot_nt(qkv_grad, full_qkv)
     grad_one, far = net.tokens_sum(partial)
     raw_second = dot_tn(hidden_one, pin(grad_second, partial)).astype(BF16)
-    raw_out = dot_tn(heads_out, pin(resid_low, raw_second)).astype(BF16)
-    grad_w_down = net.final_rows(net.total("D"), factor)
-    done = net.hop("UF", grad_second)
-
-    grad_w_gate_up = net.final_pairs(net.total("G"), net.total("U"), factor)
-    net.scatter(S=pin(raw_second, far, *done), O=pin(raw_out, far, *done))
-    done = net.hop("FSO", raw_out)
-    grad_one = pin(grad_one, raw_out, *done)
+    done = net.hop("FU", grad_second)
+
+    net.scatter(S=pin(raw_second, far, *done))
+    done = net.hop("SF", raw_second)
+
+    grad_one = pin(grad_one, raw_second, *done)
     normed_one, inv_std_one = norm_parts(tokens_in)
     tokens_grad = resid_grad + norm_back(grad_one, normed_one, inv_std_one, gain_one)
     gain_one_grad = jnp.sum(grad_one * normed_one, axis=0)
@@ -896,13 +916,18 @@
         + [bias_grad, jnp.full((shards, LANES), half_sum)],
         axis=1,
     ).reshape(shards, -1, LANES)
-    done = net.hop("FSO")
+    grad_w_down = net.final_rows(parts_down, factor)
+    parts_up = net.spread("U")
+    done = net.hop("SF", *done)
 
     vectors = net.small_reduce(pin(vectors, *done)).reshape(-1)
     loss = 2.0 * vectors[4 * vec + bias_share] / (sum_count * width)
     scaled = factor * vectors
-    done = net.hop("SO", scaled, grad_w_down)
-    net.hop("SO", grad_w_gate_up)
+    parts_first, parts_out = net.spread("F"), net.spread("O")
+    done = net.hop("S", grad_w_down, *done)
+    grad_w_gate_up = net.final_pairs(parts_gate, parts_up, factor)
+    grad_w_out = net.final_out(parts_out, factor)
+    net.hop("S", scaled, grad_w_gate_up, grad_w_out)
 
     return (
         outputs.astype(BF16)[None],
@@ -910,9 +935,9 @@
         (factor * tokens_grad).astype(BF16)[None],
         scaled[:vec],
         scaled[vec : 2 * vec],
-        net.final_qkv([net.total("F"), net.total("S")], factor),
+        net.final_qkv(parts_first, net.spread("S"), factor),
         scaled[4 * vec : 4 * vec + bias_share],
-        net.final_out(net.total("O"), factor),
+        grad_w_out,
         scaled[2 * vec : 3 * vec],
         scaled[3 * vec : 4 * vec],
         grad_w_gate_up,

time: 867 us -> 833 us (0.961)
  waiting for transfers between devices: 292 us -> 273 us
  starting transfers between devices: 122 us -> 112 us
    ppermute x20, waiting for transfers between devices: 38.2 us -> 58.5 us  [step(): ahead = lax.ppermute(ahead, 'fsdp', NEXT)]
    ppermute x2, waiting for transfers between devices: 18.3 us -> 0.01 us  [seq_sum(): return total + lax.ppermute(total, 'seq', ROW)]
    ppermute x20, starting transfers between devices: 15.4 us -> 33.5 us  [step(): ahead = lax.ppermute(ahead, 'fsdp', NEXT)]
    ppermute x20, starting transfers between devices: 27.5 us -> 11.5 us  [step(): behind = lax.ppermute(behind, 'fsdp', PREV)]
    ppermute x7 -> x0, waiting for transfers between devices: 15.3 us -> none  [small_gather(): lax.ppermute(mine, 'fsdp', [(i, i ^ k) for i in range(8)])]
    ppermute x20, waiting for transfers between devices: 28.4 us -> 14.6 us  [step(): behind = lax.ppermute(behind, 'fsdp', PREV)]
    ppermute x24 -> x20, waiting for transfers between devices: 53.9 us -> 65.8 us  [step(): ahead = lax.ppermute(pin(self.ahead, *after), 'fsdp', NEXT)]
    unnamed x233 -> x222, local copies, waits for them, and re-layouts: 53.1 us -> 42.3 us
  transfers between devices with their start and end apart: 144 -> 129, of which waited for: 60 -> 52; matrix products, arithmetic and copies ran while one was open for 33% -> 31% of each run, Pallas kernels for 10% -> 11%
where the time goes in v3:
time: 833 us; the launch traced here: 824 us
  waiting for transfers between devices  273 us (33%)
  matrix products  138 us (17%)
  starting transfers between devices  112 us (13%)
  local copies, waits for them, and re-layouts  98.9 us (12%)
  Pallas kernels  98.4 us (12%)
  other arithmetic  92.8 us (11%)
  between operations  10.5 us (1%)
    ppermute x20, waiting for transfers between devices, step(): ahead = lax.ppermute(pin(self.ahead, *after), 'fsdp', NEXT)  65.8 us
    ppermute x20, waiting for transfers between devices, step(): ahead = lax.ppermute(ahead, 'fsdp', NEXT)  58.5 us
    ppermute x4, waiting for transfers between devices, seq_scatter(): over = lax.ppermute(far, 'seq', ROW)  55.3 us
    dot_general x5, matrix products, dot_nt(): lax.dot_general(a, b, (((1,), (1,)), ((), ())), preferred_element_type=F32)  52.5 us
    dot_general x6, matrix products, dot_tn(): lax.dot_general(a, b, (((0,), (0,)), ((), ())), preferred_element_type=F32)  45.9 us
    ppermute x10, waiting for transfers between devices, seq_gather(): over = lax.ppermute(mine, 'seq', ROW)  45 us
    unnamed x222, local copies, waits for them, and re-layouts  42.3 us
    pallas_call x2, Pallas kernels, attention_backward(): call(functools.partial(backward_kernel, block, slots), (pairs,), [pl.Bloc...  40.6 us
  transfers between devices with their start and end apart: 129, of which 52 were waited for; matrix products, arithmetic and copies ran while one was open for 31% of the time, Pallas kernels for 11%

profile of v3, /device:TPU:0, one launch (start us, length us, event | category | flops | bytes accessed | tf_op | source)
XLA Modules:
  0.0 824.1 jit_solution(10909412123482033945)
XLA Ops:
  88.9 16.8 %collective-permute-done.11 = bf16[80,2048]{1,0:T(8,128)(2,1)S(1)} collective-permute-done((bf16[80,2048]{1,0:T(8,128)(2,1)S(1)}, bf16[80,2048]{1,0:T(8,128)(2,1)S(1)}, u32[]{:S(2)}, u32[]{:S(2)}) %collective-permute-start.11) | collective-permute-done | bytes 327712 | tf_op jit(solution)/shard_map/ppermute | solution.py:77
  137.8 12.3 %fusion.49.qkv = f32[1024,1536]{1,0:T(8,128)} fusion(bf16[2048,1536]{1,0:T(8,128)(2,1)} %constant_dynamic-update-slice_fusion.45, bf16[1024,2048]{1,0:T(8,128)(2,1)} %copy-done, f32[2048]{0:T(1024)S(1)} %bitcast.154, f32[2048]{0:T(1024)S(1)} %bitcast.137, f32[1024]{0:T(1024)S(1)} %add_rsqrt_fusion, f32[1024]{0:T(1024)S(1)} %broadcast_multiply_fusion.2), kind=kOutput, calls=%fused_computation.274 | convolution fusion | flops 6455033856 | bytes 16801792 | tf_op jit(solution)/shard_map/dot_general | solution.py:33
  150.1 15.8 %shard_map.239 = (bf16[1024,768]{1,0:T(8,128)(2,1)}, bf16[1024,256]{1,0:T(8,128)(2,1)}) custom-call(s32[4]{0:T(128)} %iota_xor_fusion.slot_ref, s32[4]{0:T(128)} %and_select_fusion.3.first_ref, f32[1024,1536]{1,0:T(8,128)} %fusion.49.qkv, f32[1,1536]{1,0:T(1,128)} %reshape.276.bias, f32[1024,128]{1,0:T(8,128)} %get-tuple-element.295.cosine, ...), custom_call_target="tpu_custom_call" | custom-call | flops 1610612736 | bytes 6291456 | tf_op jit(solution)/shard_map/pallas_call | solution.py:569
  175.2 15.9 %shard_map.240 = (bf16[1024,768]{1,0:T(8,128)(2,1)}, bf16[1024,256]{1,0:T(8,128)(2,1)}) custom-call(s32[4]{0:T(128)} %iota_xor_fusion.slot_ref, s32[4]{0:T(128)} %and_select_fusion.3.first_ref, f32[1024,1536]{1,0:T(8,128)} %fusion.49.qkv, f32[1,1536]{1,0:T(1,128)} %reshape.276.bias, f32[1024,128]{1,0:T(8,128)} %get-tuple-element.295.cosine, ...), custom_call_target="tpu_custom_call" | custom-call | flops 1610612736 | bytes 6291456 | tf_op jit(solution)/shard_map/pallas_call | solution.py:569
  193.1 8.0 collective-permute-done.29
  227.6 8.9 %collective-permute-done.33 = bf16[256,2048]{1,0:T(8,128)(2,1)S(1)} collective-permute-done((bf16[256,2048]{1,0:T(8,128)(2,1)S(1)}, bf16[256,2048]{1,0:T(8,128)(2,1)S(1)}, u32[]{:S(2)}, u32[]{:S(2)}) %collective-permute-start.33) | collective-permute-done | bytes 1048608 | tf_op jit(solution)/shard_map/ppermute | solution.py:133
  257.2 9.3 %collective-permute-done.39 = bf16[256,2048]{1,0:T(8,128)(2,1)S(1)} collective-permute-done((bf16[256,2048]{1,0:T(8,128)(2,1)S(1)}, bf16[256,2048]{1,0:T(8,128)(2,1)S(1)}, u32[]{:S(2)}, u32[]{:S(2)}) %collective-permute-start.39) | collective-permute-done | bytes 1048608 | tf_op jit(solution)/shard_map/ppermute | solution.py:124
  274.3 8.2 fusion.67
  291.6 14.3 %multiply_convert_fusion.1 = (bf16[1408,1024]{1,0:T(8,128)(2,1)}, f32[1408,1024]{1,0:T(8,128)}) fusion(f32[1408,1024]{1,0:T(8,128)} %fusion.67, bf16[1408,2048]{1,0:T(8,128)(2,1)} %copy-done.49, bf16[256,2048]{1,0:T(8,128)(2,1)S(1)} %collective-permute-done.40, bf16[256,2048]{1,0:T(8,128)(2,1)S(1)} %collective-permute-done.39, ...), kind=kOutput, calls=%fused_computation.19 | convolution fusion | flops 5931008000 | bytes 24379392 | tf_op jit(solution)/shard_map/dot_general | solution.py:37
  315.5 7.0 fusion.64
  327.0 24.1 %collective-permute-done.53 = bf16[256,2048]{1,0:T(8,128)(2,1)S(1)} collective-permute-done((bf16[256,2048]{1,0:T(8,128)(2,1)S(1)}, bf16[256,2048]{1,0:T(8,128)(2,1)S(1)}, u32[]{:S(2)}, u32[]{:S(2)}) %collective-permute-start.53) | collective-permute-done | bytes 1048608 | tf_op jit(solution)/shard_map/ppermute | solution.py:133
  355.7 24.3 %collective-permute-done.55 = bf16[256,2048]{1,0:T(8,128)(2,1)} collective-permute-done((bf16[256,2048]{1,0:T(8,128)(2,1)}, bf16[256,2048]{1,0:T(8,128)(2,1)}, u32[]{:S(2)}, u32[]{:S(2)}) %collective-permute-start.55) | collective-permute-done | bytes 1048608 | tf_op jit(solution)/shard_map/ppermute | solution.py:124
  382.9 8.8 %convolution_convert_fusion.2 = bf16[1408,2048]{1,0:T(8,128)(2,1)S(1)} fusion(bf16[1408,1024]{1,0:T(8,128)(2,1)} %get-tuple-element.141, bf16[256,2048]{1,0:T(8,128)(2,1)} %collective-permute-done.56, bf16[256,2048]{1,0:T(8,128)(2,1)} %collective-permute-done.55, bf16[256,2048]{1,0:T(8,128)(2,1)} %collective-permute-done.54, ...), kind=kOutput, calls=%fused_computation.15 | convolution fusion | flops 5925240832 | bytes 12845056 | tf_op jit(solution)/shard_map/dot_general | solution.py:33
  394.4 15.9 %multiply_convert_fusion = (bf16[1408,1024]{1,0:T(8,128)(2,1)}, bf16[1408,1024]{1,0:T(8,128)(2,1)}) fusion(f32[1408,1024]{1,0:T(8,128)} %fusion.67, f32[1408,1024]{1,0:T(8,128)} %get-tuple-element.309, bf16[1408,2048]{1,0:T(8,128)(2,1)} %copy-done.46, bf16[256,2048]{1,0:T(8,128)(2,1)} %collective-permute-done.56, ...), kind=kOutput, calls=%fused_computation.17 | convolution fusion | flops 5942542336 | bytes 27262976 | tf_op jit(solution)/shard_map/dot_general | solution.py:37
  412.8 8.5 %convolution_convert_fusion.1 = bf16[1408,2048]{1,0:T(8,128)(2,1)S(1)} fusion(bf16[1408,1024]{1,0:T(8,128)(2,1)} %get-tuple-element.226, bf16[1024,2048]{1,0:T(8,128)(2,1)S(1)} %copy-done.15), kind=kOutput, calls=%fused_computation.14 | convolution fusion | flops 5908463616 | bytes 12845056 | tf_op jit(solution)/shard_map/dot_general | solution.py:33
  421.3 7.0 collective-permute-done.59
  429.5 9.2 %fusion.68 = f32[1024,2048]{1,0:T(8,128)} fusion(bf16[1408,1024]{1,0:T(8,128)(2,1)S(1)} %copy-done.79, bf16[1408,2048]{1,0:T(8,128)(2,1)S(1)} %bitcast.133), kind=kOutput, calls=%fused_computation.291 | convolution fusion | flops 5905580032 | bytes 17039360 | tf_op jit(solution)/shard_map/dot_general | solution.py:41
  441.3 6.3 collective-permute-done.61
  448.0 13.0 %fusion.65 = (bf16[1024,2048]{1,0:T(8,128)(2,1)S(1)}, f32[1024,2048]{1,0:T(8,128)}) fusion(f32[1024,2048]{1,0:T(8,128)} %fusion.68, bf16[1408,1024]{1,0:T(8,128)(2,1)} %get-tuple-element.225, bf16[1408,2048]{1,0:T(8,128)(2,1)} %copy-done.49), kind=kOutput, calls=%fused_computation.288 | convolution fusion | flops 5909774336 | bytes 29622272 | tf_op jit(solution)/shard_map/dot_general | solution.py:41
  468.3 13.3 %collective-permute-done.67 = bf16[176,2048]{1,0:T(8,128)(2,1)S(1)} collective-permute-done((bf16[176,2048]{1,0:T(8,128)(2,1)S(1)}, bf16[176,2048]{1,0:T(8,128)(2,1)S(1)}, u32[]{:S(2)}, u32[]{:S(2)}) %collective-permute-start.67) | collective-permute-done | bytes 720928 | tf_op jit(solution)/shard_map/ppermute | solution.py:106
  489.9 10.0 %collective-permute-done.66 = bf16[176,2048]{1,0:T(8,128)(2,1)} collective-permute-done((bf16[176,2048]{1,0:T(8,128)(2,1)}, bf16[176,2048]{1,0:T(8,128)(2,1)}, u32[]{:S(2)}, u32[]{:S(2)}) %collective-permute-start.66) | collective-permute-done | bytes 720928 | tf_op jit(solution)/shard_map/ppermute | solution.py:105
  524.1 6.4 convolution_convert_fusion
  549.4 11.2 %collective-permute-done.77 = bf16[176,2048]{1,0:T(8,128)(2,1)} collective-permute-done((bf16[176,2048]{1,0:T(8,128)(2,1)}, bf16[176,2048]{1,0:T(8,128)(2,1)}, u32[]{:S(2)}, u32[]{:S(2)}) %collective-permute-start.77) | collective-permute-done | bytes 720928 | tf_op jit(solution)/shard_map/ppermute | solution.py:105
  586.9 20.4 %shard_map.241 = bf16[1024,768]{1,0:T(8,128)(2,1)} custom-call(s32[4]{0:T(128)} %iota_xor_fusion.slot_ref, s32[4]{0:T(128)} %and_select_fusion.3.first_ref, bf16[1024,768]{1,0:T(8,128)(2,1)} %get-tuple-element.144.turned, bf16[1024,512]{1,0:T(8,128)(2,1)} %convolution_convert_fusion.6.out_grad, f32[1024,128]{1,0:T(8,128)} %get-tuple-element.295.cosine, ...), custom_call_target="tpu_custom_call" | custom-call | flops 4026531840 | bytes 4718592 | tf_op jit(solution)/shard_map/pallas_call | solution.py:694
  607.3 8.5 %convolution_convert_fusion.4 = bf16[2048,768]{1,0:T(8,128)(2,1)} fusion(bf16[1024,768]{1,0:T(8,128)(2,1)} %shard_map.241, bf16[1024,2048]{1,0:T(8,128)(2,1)} %copy-done, f32[2048]{0:T(1024)S(1)} %bitcast.155, f32[2048]{0:T(1024)S(1)} %bitcast.138, f32[1024]{0:T(1024)S(1)} %copy-done.67, f32[1024]{0:T(1024)S(1)} %copy-done.55), kind=kOutput, calls=%fused_computation.30 | convolution fusion | flops 3235381248 | bytes 8937472 | tf_op jit(solution)/shard_map/dot_general | solution.py:41
  632.4 20.2 %shard_map.242 = bf16[1024,768]{1,0:T(8,128)(2,1)} custom-call(s32[4]{0:T(128)} %iota_xor_fusion.slot_ref, s32[4]{0:T(128)} %and_select_fusion.3.first_ref, bf16[1024,768]{1,0:T(8,128)(2,1)} %get-tuple-element.172.turned, bf16[1024,512]{1,0:T(8,128)(2,1)} %convolution_convert_fusion.6.out_grad, f32[1024,128]{1,0:T(8,128)} %get-tuple-element.295.cosine, ...), custom_call_target="tpu_custom_call" | custom-call | flops 4026531840 | bytes 4718592 | tf_op jit(solution)/shard_map/pallas_call | solution.py:694
  660.9 11.0 %collective-permute-done.96 = bf16[256,1280]{1,0:T(8,128)(2,1)S(1)} collective-permute-done((bf16[256,1280]{1,0:T(8,128)(2,1)S(1)}, bf16[256,1280]{1,0:T(8,128)(2,1)S(1)}, u32[]{:S(2)}, u32[]{:S(2)}) %collective-permute-start.96) | collective-permute-done | bytes 655392 | tf_op jit(solution)/shard_map/ppermute | solution.py:105
  677.0 10.8 %fusion.66 = (bf16[1024,2048]{1,0:T(8,128)(2,1)S(1)}, f32[1024,2048]{1,0:T(8,128)}) fusion(bf16[1024,1536]{1,0:T(8,128)(2,1)S(1)} %pad_maximum_fusion.5, bf16[2048,1536]{1,0:T(8,128)(2,1)} %constant_dynamic-update-slice_fusion.45), kind=kOutput, calls=%fused_computation.289 | convolution fusion | flops 6444548096 | bytes 22020096 | tf_op jit(solution)/shard_map/dot_general | solution.py:37
  722.5 18.3 %collective-permute-done.95 = bf16[256,2048]{1,0:T(8,128)(2,1)S(1)} collective-permute-done((bf16[256,2048]{1,0:T(8,128)(2,1)S(1)}, bf16[256,2048]{1,0:T(8,128)(2,1)S(1)}, u32[]{:S(2)}, u32[]{:S(2)}) %collective-permute-start.95) | collective-permute-done | bytes 1048608 | tf_op jit(solution)/shard_map/ppermute | solution.py:133
  774.5 8.1 shard_map.244
  802.7 7.8 collective-permute-done.127.refs_6_
  816.6 6.1 shard_map.246
  (654 shorter events, 428.0 us)
Async XLA Ops:
  13.6 32.7 %collective-permute-start.8 = (bf16[80,2048]{1,0:T(8,128)(2,1)}, bf16[80,2048]{1,0:T(8,128)(2,1)}, u32[]{:S(2)}, u32[]{:S(2)}) collective-permute-start(bf16[80,2048]{1,0:T(8,128)(2,1)} %pad_maximum_fusion.18), channel_id=1, source_target_pairs={{0,2},{2,4},{4,6},{6,7},{7,5},{5,3},{3,1},{1,0},{8,10},{10,12},{12... | collective-permute-start | bytes 983048 | tf_op jit(solution)/shard_map/ppermute | solution.py:77
  15.7 26.4 %collective-permute-start.4 = (bf16[80,2048]{1,0:T(8,128)(2,1)}, bf16[80,2048]{1,0:T(8,128)(2,1)}, u32[]{:S(2)}, u32[]{:S(2)}) collective-permute-start(bf16[80,2048]{1,0:T(8,128)(2,1)} %pad_maximum_fusion.18), channel_id=1, source_target_pairs={{2,0},{4,2},{6,4},{7,6},{5,7},{3,5},{1,3},{0,1},{10,8},{12,10},{14... | collective-permute-start | bytes 983048 | tf_op jit(solution)/shard_map/ppermute | solution.py:78
  15.7 30.1 %collective-permute-start.17 = (bf16[256,2048]{1,0:T(8,128)(2,1)S(1)}, bf16[256,2048]{1,0:T(8,128)(2,1)}, u32[]{:S(2)}, u32[]{:S(2)}) collective-permute-start(bf16[256,2048]{1,0:T(8,128)(2,1)S(1)} %bitcast.120), channel_id=1, source_target_pairs={{0,16},{8,24},{16,0},{24,8},{1,17},{9,25},{17,1},{25,9},{2,18},{10... | collective-permute-start | bytes 3145736 | tf_op jit(solution)/shard_map/ppermute | solution.py:124
  79.0 54.4 %collective-permute-start.22 = (bf16[176,2048]{1,0:T(8,128)(2,1)}, bf16[176,2048]{1,0:T(8,128)(2,1)}, u32[]{:S(2)}, u32[]{:S(2)}) collective-permute-start(bf16[176,2048]{1,0:T(8,128)(2,1)} %get-tuple-element.115), channel_id=1, source_target_pairs={{2,0},{4,2},{6,4},{7,6},{5,7},{3,5},{1,3},{0,1},{10,8},{12,10},{14... | collective-permute-start | bytes 2162696 | tf_op jit(solution)/shard_map/ppermute | solution.py:78
  79.4 53.9 %collective-permute-start.21 = (bf16[176,2048]{1,0:T(8,128)(2,1)}, bf16[176,2048]{1,0:T(8,128)(2,1)}, u32[]{:S(2)}, u32[]{:S(2)}) collective-permute-start(bf16[176,2048]{1,0:T(8,128)(2,1)} %get-tuple-element.115), channel_id=1, source_target_pairs={{0,2},{2,4},{4,6},{6,7},{7,5},{5,3},{3,1},{1,0},{8,10},{10,12},{12... | collective-permute-start | bytes 2162696 | tf_op jit(solution)/shard_map/ppermute | solution.py:77
  83.0 28.4 %collective-permute-start.19 = (bf16[128,1536]{1,0:T(8,128)(2,1)S(1)}, bf16[128,1536]{1,0:T(8,128)(2,1)S(1)}, u32[]{:S(2)}, u32[]{:S(2)}) collective-permute-start(bf16[128,1536]{1,0:T(8,128)(2,1)S(1)} %slice.358), channel_id=1, source_target_pairs={{0,2},{2,4},{4,6},{6,7},{7,5},{5,3},{3,1},{1,0},{8,10},{10,12},{12... | collective-permute-start | bytes 1179656 | tf_op jit(solution)/shard_map/ppermute | solution.py:77
  133.4 37.1 %collective-permute-start.25 = (bf16[176,2048]{1,0:T(8,128)(2,1)}, bf16[176,2048]{1,0:T(8,128)(2,1)}, u32[]{:S(2)}, u32[]{:S(2)}) collective-permute-start(bf16[176,2048]{1,0:T(8,128)(2,1)} %get-tuple-element.121), channel_id=1, source_target_pairs={{0,2},{2,4},{4,6},{6,7},{7,5},{5,3},{3,1},{1,0},{8,10},{10,12},{12... | collective-permute-start | bytes 2162696 | tf_op jit(solution)/shard_map/ppermute | solution.py:77
  135.0 37.0 %collective-permute-start.26 = (bf16[176,2048]{1,0:T(8,128)(2,1)}, bf16[176,2048]{1,0:T(8,128)(2,1)}, u32[]{:S(2)}, u32[]{:S(2)}) collective-permute-start(bf16[176,2048]{1,0:T(8,128)(2,1)} %get-tuple-element.121), channel_id=1, source_target_pairs={{2,0},{4,2},{6,4},{7,6},{5,7},{3,5},{1,3},{0,1},{10,8},{12,10},{14... | collective-permute-start | bytes 2162696 | tf_op jit(solution)/shard_map/ppermute | solution.py:78
  135.4 33.0 %collective-permute-start.24 = (bf16[176,2048]{1,0:T(8,128)(2,1)}, bf16[176,2048]{1,0:T(8,128)(2,1)}, u32[]{:S(2)}, u32[]{:S(2)}) collective-permute-start(bf16[176,2048]{1,0:T(8,128)(2,1)} %collective-permute-done.22), channel_id=1, source_target_pairs={{2,0},{4,2},{6,4},{7,6},{5,7},{3,5},{1,3},{0,1},{10,8},{12,10},{14... | collective-permute-start | bytes 2162696 | tf_op jit(solution)/shard_map/ppermute | solution.py:78
  137.0 31.8 %collective-permute-start.23 = (bf16[176,2048]{1,0:T(8,128)(2,1)}, bf16[176,2048]{1,0:T(8,128)(2,1)}, u32[]{:S(2)}, u32[]{:S(2)}) collective-permute-start(bf16[176,2048]{1,0:T(8,128)(2,1)} %collective-permute-done.21), channel_id=1, source_target_pairs={{0,2},{2,4},{4,6},{6,7},{7,5},{5,3},{3,1},{1,0},{8,10},{10,12},{12... | collective-permute-start | bytes 2162696 | tf_op jit(solution)/shard_map/ppermute | solution.py:77
  170.4 30.7 %collective-permute-start.29 = (bf16[176,2048]{1,0:T(8,128)(2,1)}, bf16[176,2048]{1,0:T(8,128)(2,1)}, u32[]{:S(2)}, u32[]{:S(2)}) collective-permute-start(bf16[176,2048]{1,0:T(8,128)(2,1)} %collective-permute-done.25), channel_id=1, source_target_pairs={{0,2},{2,4},{4,6},{6,7},{7,5},{5,3},{3,1},{1,0},{8,10},{10,12},{12... | collective-permute-start | bytes 2162696 | tf_op jit(solution)/shard_map/ppermute | solution.py:77
  172.0 29.1 %collective-permute-start.30 = (bf16[176,2048]{1,0:T(8,128)(2,1)}, bf16[176,2048]{1,0:T(8,128)(2,1)}, u32[]{:S(2)}, u32[]{:S(2)}) collective-permute-start(bf16[176,2048]{1,0:T(8,128)(2,1)} %collective-permute-done.26), channel_id=1, source_target_pairs={{2,0},{4,2},{6,4},{7,6},{5,7},{3,5},{1,3},{0,1},{10,8},{12,10},{14... | collective-permute-start | bytes 2162696 | tf_op jit(solution)/shard_map/ppermute | solution.py:78
  462.1 44.9 %collective-permute-start.63 = (bf16[256,2048]{1,0:T(8,128)(2,1)}, bf16[256,2048]{1,0:T(8,128)(2,1)}, u32[]{:S(2)}, u32[]{:S(2)}) collective-permute-start(bf16[256,2048]{1,0:T(8,128)(2,1)} %get-tuple-element.269), channel_id=1, source_target_pairs={{0,8},{8,0},{16,24},{24,16},{1,9},{9,1},{17,25},{25,17},{2,10},{10... | collective-permute-start | bytes 3145736 | tf_op jit(solution)/shard_map/ppermute | solution.py:131
  465.4 36.1 %collective-permute-start.68 = (bf16[176,2048]{1,0:T(8,128)(2,1)}, bf16[176,2048]{1,0:T(8,128)(2,1)}, u32[]{:S(2)}, u32[]{:S(2)}) collective-permute-start(bf16[176,2048]{1,0:T(8,128)(2,1)} %pad_maximum_fusion.8), channel_id=1, source_target_pairs={{0,2},{2,4},{4,6},{6,7},{7,5},{5,3},{3,1},{1,0},{8,10},{10,12},{12... | collective-permute-start | bytes 2162696 | tf_op jit(solution)/shard_map/ppermute | solution.py:105
  466.7 34.7 %collective-permute-start.69 = (bf16[176,2048]{1,0:T(8,128)(2,1)}, bf16[176,2048]{1,0:T(8,128)(2,1)}, u32[]{:S(2)}, u32[]{:S(2)}) collective-permute-start(bf16[176,2048]{1,0:T(8,128)(2,1)} %pad_maximum_fusion.9), channel_id=1, source_target_pairs={{2,0},{4,2},{6,4},{7,6},{5,7},{3,5},{1,3},{0,1},{10,8},{12,10},{14... | collective-permute-start | bytes 2162696 | tf_op jit(solution)/shard_map/ppermute | solution.py:106
  534.0 39.1 %collective-permute-start.72 = (bf16[256,2048]{1,0:T(8,128)(2,1)}, bf16[256,2048]{1,0:T(8,128)(2,1)S(1)}, u32[]{:S(2)}, u32[]{:S(2)}) collective-permute-start(bf16[256,2048]{1,0:T(8,128)(2,1)} %get-tuple-element.211), channel_id=1, source_target_pairs={{0,8},{8,0},{16,24},{24,16},{1,9},{9,1},{17,25},{25,17},{2,10},{10... | collective-permute-start | bytes 3145736 | tf_op jit(solution)/shard_map/ppermute | solution.py:125
  582.4 38.9 %collective-permute-start.79 = (bf16[176,2048]{1,0:T(8,128)(2,1)S(1)}, bf16[176,2048]{1,0:T(8,128)(2,1)}, u32[]{:S(2)}, u32[]{:S(2)}) collective-permute-start(bf16[176,2048]{1,0:T(8,128)(2,1)S(1)} %copy-done.31), channel_id=1, source_target_pairs={{0,2},{2,4},{4,6},{6,7},{7,5},{5,3},{3,1},{1,0},{8,10},{10,12},{12... | collective-permute-start | bytes 2162696 | tf_op jit(solution)/shard_map/ppermute | solution.py:105
  583.7 37.7 %collective-permute-start.80 = (bf16[176,2048]{1,0:T(8,128)(2,1)S(1)}, bf16[176,2048]{1,0:T(8,128)(2,1)}, u32[]{:S(2)}, u32[]{:S(2)}) collective-permute-start(bf16[176,2048]{1,0:T(8,128)(2,1)S(1)} %copy-done.32), channel_id=1, source_target_pairs={{2,0},{4,2},{6,4},{7,6},{5,7},{3,5},{1,3},{0,1},{10,8},{12,10},{14... | collective-permute-start | bytes 2162696 | tf_op jit(solution)/shard_map/ppermute | solution.py:106
  584.5 36.9 %collective-permute-start.81 = (bf16[176,2048]{1,0:T(8,128)(2,1)}, bf16[176,2048]{1,0:T(8,128)(2,1)}, u32[]{:S(2)}, u32[]{:S(2)}) collective-permute-start(bf16[176,2048]{1,0:T(8,128)(2,1)} %get-tuple-element.169), channel_id=1, source_target_pairs={{0,2},{2,4},{4,6},{6,7},{7,5},{5,3},{3,1},{1,0},{8,10},{10,12},{12... | collective-permute-start | bytes 2162696 | tf_op jit(solution)/shard_map/ppermute | solution.py:105
  585.7 35.7 %collective-permute-start.82 = (bf16[176,2048]{1,0:T(8,128)(2,1)}, bf16[176,2048]{1,0:T(8,128)(2,1)}, u32[]{:S(2)}, u32[]{:S(2)}) collective-permute-start(bf16[176,2048]{1,0:T(8,128)(2,1)} %get-tuple-element.170), channel_id=1, source_target_pairs={{2,0},{4,2},{6,4},{7,6},{5,7},{3,5},{1,3},{0,1},{10,8},{12,10},{14... | collective-permute-start | bytes 2162696 | tf_op jit(solution)/shard_map/ppermute | solution.py:106
  622.4 30.2 %collective-permute-start.86 = (bf16[128,1280]{1,0:T(8,128)(2,1)}, bf16[128,1280]{1,0:T(8,128)(2,1)}, u32[]{:S(2)}, u32[]{:S(2)}) collective-permute-start(bf16[128,1280]{1,0:T(8,128)(2,1)} %get-tuple-element.174), channel_id=1, source_target_pairs={{0,2},{2,4},{4,6},{6,7},{7,5},{5,3},{3,1},{1,0},{8,10},{10,12},{12... | collective-permute-start | bytes 983048 | tf_op jit(solution)/shard_map/ppermute | solution.py:105
  622.4 30.2 %collective-permute-start.87 = (bf16[128,1280]{1,0:T(8,128)(2,1)S(1)}, bf16[128,1280]{1,0:T(8,128)(2,1)}, u32[]{:S(2)}, u32[]{:S(2)}) collective-permute-start(bf16[128,1280]{1,0:T(8,128)(2,1)S(1)} %get-tuple-element.175), channel_id=1, source_target_pairs={{2,0},{4,2},{6,4},{7,6},{5,7},{3,5},{1,3},{0,1},{10,8},{12,10},{14... | collective-permute-start | bytes 983048 | tf_op jit(solution)/shard_map/ppermute | solution.py:106
  627.6 29.0 %collective-permute-start.88 = (bf16[176,2048]{1,0:T(8,128)(2,1)}, bf16[176,2048]{1,0:T(8,128)(2,1)S(1)}, u32[]{:S(2)}, u32[]{:S(2)}) collective-permute-start(bf16[176,2048]{1,0:T(8,128)(2,1)} %get-tuple-element.176), channel_id=1, source_target_pairs={{0,2},{2,4},{4,6},{6,7},{7,5},{5,3},{3,1},{1,0},{8,10},{10,12},{12... | collective-permute-start | bytes 2162696 | tf_op jit(solution)/shard_map/ppermute | solution.py:105
  627.9 29.4 %collective-permute-start.89 = (bf16[176,2048]{1,0:T(8,128)(2,1)S(1)}, bf16[176,2048]{1,0:T(8,128)(2,1)}, u32[]{:S(2)}, u32[]{:S(2)}) collective-permute-start(bf16[176,2048]{1,0:T(8,128)(2,1)S(1)} %get-tuple-element.177), channel_id=1, source_target_pairs={{2,0},{4,2},{6,4},{7,6},{5,7},{3,5},{1,3},{0,1},{10,8},{12,10},{14... | collective-permute-start | bytes 2162696 | tf_op jit(solution)/shard_map/ppermute | solution.py:106
  660.5 36.9 %collective-permute-start.98 = (bf16[176,2048]{1,0:T(8,128)(2,1)}, bf16[176,2048]{1,0:T(8,128)(2,1)}, u32[]{:S(2)}, u32[]{:S(2)}) collective-permute-start(bf16[176,2048]{1,0:T(8,128)(2,1)} %get-tuple-element.182), channel_id=1, source_target_pairs={{0,2},{2,4},{4,6},{6,7},{7,5},{5,3},{3,1},{1,0},{8,10},{10,12},{12... | collective-permute-start | bytes 2162696 | tf_op jit(solution)/shard_map/ppermute | solution.py:105
  671.9 26.8 %collective-permute-start.99 = (bf16[176,2048]{1,0:T(8,128)(2,1)}, bf16[176,2048]{1,0:T(8,128)(2,1)}, u32[]{:S(2)}, u32[]{:S(2)}) collective-permute-start(bf16[176,2048]{1,0:T(8,128)(2,1)} %get-tuple-element.183), channel_id=1, source_target_pairs={{2,0},{4,2},{6,4},{7,6},{5,7},{3,5},{1,3},{0,1},{10,8},{12,10},{14... | collective-permute-start | bytes 2162696 | tf_op jit(solution)/shard_map/ppermute | solution.py:106
  689.3 32.5 %collective-permute-start.93 = (bf16[256,2048]{1,0:T(8,128)(2,1)}, bf16[256,2048]{1,0:T(8,128)(2,1)}, u32[]{:S(2)}, u32[]{:S(2)}) collective-permute-start(bf16[256,2048]{1,0:T(8,128)(2,1)} %get-tuple-element.267), channel_id=1, source_target_pairs={{0,8},{8,0},{16,24},{24,16},{1,9},{9,1},{17,25},{25,17},{2,10},{10... | collective-permute-start | bytes 3145736 | tf_op jit(solution)/shard_map/ppermute | solution.py:131
  701.5 49.2 %collective-permute-start.118 = (bf16[176,2048]{1,0:T(8,128)(2,1)}, bf16[176,2048]{1,0:T(8,128)(2,1)}, u32[]{:S(2)}, u32[]{:S(2)}) collective-permute-start(bf16[176,2048]{1,0:T(8,128)(2,1)} %add_convert_fusion.2.refs_4_), channel_id=1, source_target_pairs={{0,16},{8,24},{16,0},{24,8},{1,17},{9,25},{17,1},{25,9},{2,18},{10... | collective-permute-start | bytes 2162696 | tf_op jit(solution)/shard_map/ppermute | solution.py:124
  704.9 35.9 %collective-permute-start.95 = (bf16[256,2048]{1,0:T(8,128)(2,1)S(1)}, bf16[256,2048]{1,0:T(8,128)(2,1)S(1)}, u32[]{:S(2)}, u32[]{:S(2)}) collective-permute-start(bf16[256,2048]{1,0:T(8,128)(2,1)S(1)} %fusion.21), channel_id=1, source_target_pairs={{0,16},{8,24},{16,0},{24,8},{1,17},{9,25},{17,1},{25,9},{2,18},{10... | collective-permute-start | bytes 3145736 | tf_op jit(solution)/shard_map/ppermute | solution.py:133
  719.0 31.6 %collective-permute-start.104 = (bf16[256,768]{1,0:T(8,128)(2,1)S(1)}, bf16[256,768]{1,0:T(8,128)(2,1)}, u32[]{:S(2)}, u32[]{:S(2)}) collective-permute-start(bf16[256,768]{1,0:T(8,128)(2,1)S(1)} %pad_maximum_fusion.16), channel_id=1, source_target_pairs={{0,2},{2,4},{4,6},{6,7},{7,5},{5,3},{3,1},{1,0},{8,10},{10,12},{12... | collective-permute-start | bytes 1179656 | tf_op jit(solution)/shard_map/ppermute | solution.py:105
  720.5 30.7 %collective-permute-start.105 = (bf16[256,768]{1,0:T(8,128)(2,1)}, bf16[256,768]{1,0:T(8,128)(2,1)}, u32[]{:S(2)}, u32[]{:S(2)}) collective-permute-start(bf16[256,768]{1,0:T(8,128)(2,1)} %pad_maximum_fusion.17), channel_id=1, source_target_pairs={{2,0},{4,2},{6,4},{7,6},{5,7},{3,5},{1,3},{0,1},{10,8},{12,10},{14... | collective-permute-start | bytes 1179656 | tf_op jit(solution)/shard_map/ppermute | solution.py:106
  721.9 29.3 %collective-permute-start.106 = (bf16[256,1280]{1,0:T(8,128)(2,1)}, bf16[256,1280]{1,0:T(8,128)(2,1)}, u32[]{:S(2)}, u32[]{:S(2)}) collective-permute-start(bf16[256,1280]{1,0:T(8,128)(2,1)} %get-tuple-element.192), channel_id=1, source_target_pairs={{0,2},{2,4},{4,6},{6,7},{7,5},{5,3},{3,1},{1,0},{8,10},{10,12},{12... | collective-permute-start | bytes 1966088 | tf_op jit(solution)/shard_map/ppermute | solution.py:105
  (182 other events, 2778.3 us)

commit v4 on v3

--- a/solution.py
+++ b/solution.py
@@ -120,10 +120,10 @@
         return got
 
 
-def seq_gather(mine):
+def seq_gather(mine, hold=()):
     over = lax.ppermute(mine, "seq", ROW)
     beside = lax.ppermute(mine, "seq", CORE)
-    return [mine, beside, over, lax.ppermute(over, "seq", CORE)]
+    return [mine, beside, over, lax.ppermute(pin(over, *hold), "seq", CORE)]
 
 
 def seq_scatter(parts):
@@ -177,6 +177,10 @@
 
     def whole(self, name):
         return self.in_order(self.rings[name]) if name == "q" else self.as_found(self.rings[name])
+
+    def scatter_pair(self, gate, up):
+        gates, ups = (v.reshape(8, -1, v.shape[1]) for v in (gate, up))
+        self.rings["W"] = RingScatter([jnp.concatenate([gates[j], ups[j]]) for j in range(8)])
 
     def scatter_first(self, raw_first, raw_out, *after):
         rows, cols = raw_out.shape
@@ -218,8 +222,8 @@
         here = (jnp.arange(4) == self.s).astype(F32)[None, None, None, :, None]
         return (split[:, :, :, None, :] * here).reshape(-1)
 
-    def spread(self, name):
-        return seq_gather(self.total(name).astype(BF16))
+    def spread(self, name, *after, hold=()):
+        return seq_gather(pin(self.total(name).astype(BF16), *after), hold)
 
     def final_qkv(self, first, second, factor):
         return unpick_columns([first, second], self.s, factor)
@@ -229,8 +233,8 @@
 
     final_out = final_rows
 
-    def final_pairs(self, first, second, factor):
-        return place_pairs(first + second, self.s, factor)
+    def final_pairs(self, parts, factor):
+        return place_pairs(parts, self.s, factor)
 
     def tokens(self, mine):
         return jnp.concatenate(seq_gather(mine))
@@ -243,12 +247,12 @@
         split = values.reshape((4, values.shape[0] // 4) + values.shape[1:])
         return jnp.take(split, self.slots, axis=0).reshape(values.shape)
 
-    def small_reduce(self, values):
+    def small_reduce(self, values, *after):
         total = jnp.take(values, self.f ^ jnp.arange(8), axis=0)
         for bit in (4, 2, 1):
             other = lax.ppermute(total[bit:], "fsdp", [(i, i ^ bit) for i in range(8)])
             total = total[:bit] + other
-        return self.seq_sum(total[0])
+        return self.seq_sum(pin(total[0], *after))
 
     def seq_sum(self, total):
         total = total + lax.ppermute(total, "seq", CORE)
@@ -292,6 +296,10 @@
     def whole(self, name):
         return self.wholes[name]
 
+    def scatter_pair(self, gate, up):
+        both = [v.reshape(self.shards, -1, v.shape[1]) for v in (gate, up)]
+        self.scatter(W=jnp.concatenate(both, axis=1).reshape(-1, gate.shape[1]))
+
     def scatter_first(self, raw_first, raw_out, *after):
         self.scatter(F=raw_first, O=raw_out)
 
@@ -316,7 +324,7 @@
     def gathered(self, share):
         return lax.all_gather(share.astype(BF16), "seq", axis=0, tiled=False)
 
-    def spread(self, name):
+    def spread(self, name, *after, hold=()):
         return [self.total(name)]
 
     def final_qkv(self, first, second, factor):
@@ -331,8 +339,9 @@
     def final_out(self, parts, factor):
         return factor * lax.psum(parts[0].astype(BF16), "seq").astype(F32)
 
-    def final_pairs(self, first, second, factor):
-        parts = jnp.stack(first + second, axis=1)
+    def final_pairs(self, parts, factor):
+        rows = parts[0].shape[0] // 2
+        parts = jnp.stack([parts[0][:rows], parts[0][rows:]], axis=1)
         parts = lax.all_gather(parts.astype(BF16), "seq", axis=0, tiled=True)
         return factor * parts.astype(F32)
 
@@ -346,7 +355,7 @@
     def by_slot(self, values):
         return values
 
-    def small_reduce(self, values):
+    def small_reduce(self, values, *after):
         total = lax.psum(values, ("seq", "fsdp"))
         return lax.dynamic_index_in_dim(total, self.f, 0, keepdims=False)
 
@@ -457,26 +466,27 @@
     )(s.reshape(1), factor.reshape(1), *parts)
 
 
-def place_pair_kernel(s_ref, factor_ref, *refs):
-    out_ref = refs[8]
+def place_pair_kernel(s_ref, factor_ref, p0, p1, p2, p3, out_ref):
     r = pl.program_id(0)
-    for k in range(4):
+    rows = out_ref.shape[0]
+    for k, part in enumerate((p0, p1, p2, p3)):
 
         @pl.when(r == k)
-        def _(k=k):
-            out_ref[:, 0, :] = refs[k][...].astype(F32) * factor_ref[0]
-            out_ref[:, 1, :] = refs[4 + k][...].astype(F32) * factor_ref[0]
+        def _(part=part):
+            out_ref[:, 0, :] = part[:rows, :].astype(F32) * factor_ref[0]
+            out_ref[:, 1, :] = part[rows:, :].astype(F32) * factor_ref[0]
 
 
 def place_pairs(parts, s, factor):
     rows, cols = parts[0].shape
+    half = rows // 2
     return call(
         place_pair_kernel,
         (4,),
         [pl.BlockSpec(memory_space=pltpu.SMEM)]
-        + [pl.BlockSpec((rows, cols), lambda r, s_ref: (0, 0))] * 8,
-        pl.BlockSpec((rows, 2, cols), lambda r, s_ref: (s_ref[0] ^ r, 0, 0)),
-        jax.ShapeDtypeStruct((4 * rows, 2, cols), F32),
+        + [pl.BlockSpec((rows, cols), lambda r, s_ref: (0, 0))] * 4,
+        pl.BlockSpec((half, 2, cols), lambda r, s_ref: (s_ref[0] ^ r, 0, 0)),
+        jax.ShapeDtypeStruct((4 * half, 2, cols), F32),
         prefetch=1,
     )(s.reshape(1), factor.reshape(1), *parts)
 
@@ -851,18 +861,14 @@
     up_grad = (hidden_grad * (gate * sigma)).astype(BF16)
 
     raw_gate = dot_nn(gate_grad, pin(hidden_two, *done)).astype(BF16)
+    raw_up = dot_nn(up_grad, pin(hidden_two, raw_gate)).astype(BF16)
     done = net.hop("D", gate_grad)
-    partial = dot_tn(gate_grad, pin(full_gate, raw_gate, *done))
-
-    net.scatter(G=pin(raw_gate, *done))
-    done = net.hop("G")
-    partial = partial + dot_tn(up_grad, pin(full_up, partial, *done))
-    two_grad, far = net.tokens_sum(partial)
-    done = net.hop("DG", *done)
-
-    raw_up = dot_nn(up_grad, pin(hidden_two, far, *done)).astype(BF16)
-    net.scatter(U=raw_up)
-    done = net.hop("D", *done)
+    partial = dot_tn(gate_grad, pin(full_gate, raw_up, *done))
+    done = net.hop("D")
+    partial = partial + dot_tn(up_grad, pin(full_up, partial))
+    two_grad, far = net.tokens_sum(pin(partial, *done))
+    net.scatter_pair(pin(raw_gate, *done), pin(raw_up, *done))
+    done = net.hop("DW", far)
 
     two_grad = pin(two_grad, *done)
     resid_grad = cot + norm_back(two_grad, normed_two, inv_std_two, gain_two)
@@ -870,7 +876,7 @@
     shift_two_grad = jnp.sum(two_grad, axis=0)
     mine_low = resid_grad.astype(BF16)
     resid_low = net.tokens(mine_low)
-    done = net.hop("UG", *done)
+    done = net.hop("W", mine_low)
 
     full_qkv = net.whole("q")
     out_grad = dot_nt(pin(resid_low, *done), full_out).astype(BF16)
@@ -881,28 +887,28 @@
         slot_of=net.slots,
         block=rows,
     )
-    raw_out = dot_tn(heads_out, pin(resid_low, out_grad)).astype(BF16)
-    grad_first = backward(turned_one, pin(out_grad, raw_out), first_slot=first_slot, skip=0)
+    grad_first = backward(turned_one, out_grad, first_slot=first_slot, skip=0)
+    raw_out = dot_tn(heads_out, pin(resid_low, grad_first)).astype(BF16)
     raw_first = dot_tn(hidden_one, grad_first).astype(BF16)
-    done = net.hop("UG", resid_low)
+    done = net.hop("W", out_grad)
 
     net.scatter_first(raw_first, raw_out, *done)
-    parts_down = net.spread("D")
+    parts_down = net.spread("D", out_grad)
     here = pin(first_slot, raw_first, *done, *parts_down)
     grad_second = backward(turned_two, out_grad, first_slot=here, skip=half_pairs)
-    done = net.hop("FU", raw_first)
-
-    parts_gate = net.spread("G")
-    qkv_grad = pin(jnp.concatenate([grad_first, grad_second], axis=1), *done, *parts_gate)
+    done = net.hop("F", raw_first) + net.hop("W")
+
+    raw_second = dot_tn(hidden_one, pin(grad_second, *done)).astype(BF16)
+    done = net.hop("F", grad_second)
+    qkv_grad = pin(jnp.concatenate([grad_first, grad_second], axis=1), raw_second, *done)
+    net.scatter(S=pin(raw_second, *done))
     partial = dot_nt(qkv_grad, full_qkv)
-    grad_one, far = net.tokens_sum(partial)
-    raw_second = dot_tn(hidden_one, pin(grad_second, partial)).astype(BF16)
-    done = net.hop("FU", grad_second)
-
-    net.scatter(S=pin(raw_second, far, *done))
-    done = net.hop("SF", raw_second)
-
-    grad_one = pin(grad_one, raw_second, *done)
+    done = net.hop("FS")
+
+    grad_one, far = net.tokens_sum(pin(partial, *done))
+    done = net.hop("FS", far)
+
+    third = net.hop("S", *done)
     normed_one, inv_std_one = norm_parts(tokens_in)
     tokens_grad = resid_grad + norm_back(grad_one, normed_one, inv_std_one, gain_one)
     gain_one_grad = jnp.sum(grad_one * normed_one, axis=0)
@@ -916,18 +922,16 @@
         + [bias_grad, jnp.full((shards, LANES), half_sum)],
         axis=1,
     ).reshape(shards, -1, LANES)
-    grad_w_down = net.final_rows(parts_down, factor)
-    parts_up = net.spread("U")
-    done = net.hop("SF", *done)
-
-    vectors = net.small_reduce(pin(vectors, *done)).reshape(-1)
+    grad_w_down = net.final_rows(parts_down, pin(factor, raw_second))
+    parts_first, parts_out = net.spread("F"), net.spread("O")
+    last = net.hop("S", *third)
+    parts_pair = net.spread("W", grad_one, hold=last)
+    vectors = net.small_reduce(pin(vectors, *third), *last).reshape(-1)
     loss = 2.0 * vectors[4 * vec + bias_share] / (sum_count * width)
     scaled = factor * vectors
-    parts_first, parts_out = net.spread("F"), net.spread("O")
-    done = net.hop("S", grad_w_down, *done)
-    grad_w_gate_up = net.final_pairs(parts_gate, parts_up, factor)
+    grad_w_gate_up = net.final_pairs(parts_pair, factor)
     grad_w_out = net.final_out(parts_out, factor)
-    net.hop("S", scaled, grad_w_gate_up, grad_w_out)
+    parts_second = net.spread("S", grad_w_down, grad_w_gate_up)
 
     return (
         outputs.astype(BF16)[None],
@@ -935,7 +939,7 @@
         (factor * tokens_grad).astype(BF16)[None],
         scaled[:vec],
         scaled[vec : 2 * vec],
-        net.final_qkv(parts_first, net.spread("S"), factor),
+        net.final_qkv(parts_first, parts_second, factor),
         scaled[4 * vec : 4 * vec + bias_share],
         grad_w_out,
         scaled[2 * vec : 3 * vec],

time: 833 us -> 828 us (level)
  local copies, waits for them, and re-layouts: 98.9 us -> 113 us
  starting transfers between devices: 112 us -> 102 us
    ppermute x4, waiting for transfers between devices: 55.3 us -> 38.5 us  [seq_scatter(): over = lax.ppermute(far, 'seq', ROW)]
    ppermute x10 -> x9, waiting for transfers between devices: 45 us -> 58.6 us  [seq_gather(): over = lax.ppermute(mine, 'seq', ROW)]
    ppermute x20 -> x16, waiting for transfers between devices: 25.2 us -> 16.4 us  [step(): behind = lax.ppermute(pin(self.behind, *after), 'fsdp', PREV)]
    ppermute x20 -> x16, starting transfers between devices: 18.6 us -> 12.7 us  [step(): ahead = lax.ppermute(pin(self.ahead, *after), 'fsdp', NEXT)]
    convert_element_type x12 -> x10, other arithmetic: 26.8 us -> 21.5 us  [step(): self.ahead, self.behind = (ahead.astype(BF16), behind.astype(BF16))]
    ppermute x20 -> x16, waiting for transfers between devices: 65.8 us -> 68.8 us  [step(): ahead = lax.ppermute(pin(self.ahead, *after), 'fsdp', NEXT)]
    ppermute x20 -> x16, starting transfers between devices: 23.3 us -> 21.1 us  [step(): behind = lax.ppermute(pin(self.behind, *after), 'fsdp', PREV)]
    unnamed x222 -> x237, local copies, waits for them, and re-layouts: 42.3 us -> 44 us
  transfers between devices with their start and end apart: 129 -> 118, of which waited for: 52 -> 51; matrix products, arithmetic and copies ran while one was open for 31% -> 33% of each run, Pallas kernels for 11% -> 11%
where the time goes in v4:
time: 828 us; the launch traced here: 820 us
  waiting for transfers between devices  266 us (32%)
  matrix products  136 us (16%)
  local copies, waits for them, and re-layouts  113 us (14%)
  starting transfers between devices  102 us (12%)
  Pallas kernels  98.2 us (12%)
  other arithmetic  93.3 us (11%)
  between operations  10.2 us (1%)
    ppermute x16, waiting for transfers between devices, step(): ahead = lax.ppermute(pin(self.ahead, *after), 'fsdp', NEXT)  68.8 us
    ppermute x9, waiting for transfers between devices, seq_gather(): over = lax.ppermute(mine, 'seq', ROW)  58.6 us
    ppermute x20, waiting for transfers between devices, step(): ahead = lax.ppermute(ahead, 'fsdp', NEXT)  57 us
    dot_general x5, matrix products, dot_nt(): lax.dot_general(a, b, (((1,), (1,)), ((), ())), preferred_element_type=F32)  48.5 us
    dot_general x6, matrix products, dot_tn(): lax.dot_general(a, b, (((0,), (0,)), ((), ())), preferred_element_type=F32)  46.8 us
    unnamed x237, local copies, waits for them, and re-layouts  44 us
    dot_general x5, matrix products, dot_nn(): lax.dot_general(a, b, (((1,), (0,)), ((), ())), preferred_element_type=F32)  40.9 us
    pallas_call x2, Pallas kernels, attention_backward(): call(functools.partial(backward_kernel, block, slots), (pairs,), [pl.Bloc...  40.5 us
  transfers between devices with their start and end apart: 118, of which 51 were waited for; matrix products, arithmetic and copies ran while one was open for 33% of the time, Pallas kernels for 11%

profile of v4, /device:TPU:0, one launch (start us, length us, event | category | flops | bytes accessed | tf_op | source)
XLA Modules:
  0.0 819.5 jit_solution(16747425219189119000)
XLA Ops:
  63.5 6.1 pad_maximum_fusion.1
  88.9 16.8 %collective-permute-done.11 = bf16[80,2048]{1,0:T(8,128)(2,1)S(1)} collective-permute-done((bf16[80,2048]{1,0:T(8,128)(2,1)S(1)}, bf16[80,2048]{1,0:T(8,128)(2,1)S(1)}, u32[]{:S(2)}, u32[]{:S(2)}) %collective-permute-start.11) | collective-permute-done | bytes 327712 | tf_op jit(solution)/shard_map/ppermute | solution.py:77
  137.9 12.3 %fusion.45.qkv = f32[1024,1536]{1,0:T(8,128)} fusion(bf16[2048,1536]{1,0:T(8,128)(2,1)} %constant_dynamic-update-slice_fusion.45, bf16[1024,2048]{1,0:T(8,128)(2,1)} %copy-done, f32[2048]{0:T(1024)S(1)} %bitcast.156, f32[2048]{0:T(1024)S(1)} %bitcast.139, f32[1024]{0:T(1024)S(1)} %add_rsqrt_fusion, f32[1024]{0:T(1024)S(1)} %broadcast_multiply_fusion.2), kind=kOutput, calls=%fused_computation.261 | convolution fusion | flops 6455033856 | bytes 16801792 | tf_op jit(solution)/shard_map/dot_general | solution.py:33
  150.2 15.8 %shard_map.239 = (bf16[1024,768]{1,0:T(8,128)(2,1)}, bf16[1024,256]{1,0:T(8,128)(2,1)}) custom-call(s32[4]{0:T(128)} %iota_xor_fusion.slot_ref, s32[4]{0:T(128)} %and_select_fusion.3.first_ref, f32[1024,1536]{1,0:T(8,128)} %fusion.45.qkv, f32[1,1536]{1,0:T(1,128)} %reshape.312.bias, f32[1024,128]{1,0:T(8,128)} %get-tuple-element.280.cosine, ...), custom_call_target="tpu_custom_call" | custom-call | flops 1610612736 | bytes 6291456 | tf_op jit(solution)/shard_map/pallas_call | solution.py:579
  175.3 15.8 %shard_map.240 = (bf16[1024,768]{1,0:T(8,128)(2,1)}, bf16[1024,256]{1,0:T(8,128)(2,1)}) custom-call(s32[4]{0:T(128)} %iota_xor_fusion.slot_ref, s32[4]{0:T(128)} %and_select_fusion.3.first_ref, f32[1024,1536]{1,0:T(8,128)} %fusion.45.qkv, f32[1,1536]{1,0:T(1,128)} %reshape.312.bias, f32[1024,128]{1,0:T(8,128)} %get-tuple-element.280.cosine, ...), custom_call_target="tpu_custom_call" | custom-call | flops 1610612736 | bytes 6291456 | tf_op jit(solution)/shard_map/pallas_call | solution.py:579
  192.9 8.2 %collective-permute-done.29 = bf16[176,2048]{1,0:T(8,128)(2,1)} collective-permute-done((bf16[176,2048]{1,0:T(8,128)(2,1)}, bf16[176,2048]{1,0:T(8,128)(2,1)}, u32[]{:S(2)}, u32[]{:S(2)}) %collective-permute-start.29) | collective-permute-done | bytes 720928 | tf_op jit(solution)/shard_map/ppermute | solution.py:77
  228.7 8.9 %collective-permute-done.33 = bf16[256,2048]{1,0:T(8,128)(2,1)S(1)} collective-permute-done((bf16[256,2048]{1,0:T(8,128)(2,1)S(1)}, bf16[256,2048]{1,0:T(8,128)(2,1)S(1)}, u32[]{:S(2)}, u32[]{:S(2)}) %collective-permute-start.33) | collective-permute-done | bytes 1048608 | tf_op jit(solution)/shard_map/ppermute | solution.py:133
  258.8 9.4 %collective-permute-done.39 = bf16[256,2048]{1,0:T(8,128)(2,1)S(1)} collective-permute-done((bf16[256,2048]{1,0:T(8,128)(2,1)S(1)}, bf16[256,2048]{1,0:T(8,128)(2,1)S(1)}, u32[]{:S(2)}, u32[]{:S(2)}) %collective-permute-start.39) | collective-permute-done | bytes 1048608 | tf_op jit(solution)/shard_map/ppermute | solution.py:124
  276.8 8.2 %fusion.61 = f32[1408,1024]{1,0:T(8,128)} fusion(bf16[1408,2048]{1,0:T(8,128)(2,1)S(1)} %constant_dynamic-update-slice_fusion.12, bf16[1024,2048]{1,0:T(8,128)(2,1)S(1)} %pad_maximum_fusion.2), kind=kOutput, calls=%fused_computation.275 | convolution fusion | flops 5905580032 | bytes 15728640 | tf_op jit(solution)/shard_map/dot_general | solution.py:37
  293.3 12.6 %multiply_convert_fusion.1 = (bf16[1408,1024]{1,0:T(8,128)(2,1)}, f32[1408,1024]{1,0:T(8,128)}) fusion(f32[1408,1024]{1,0:T(8,128)} %fusion.61, bf16[1408,2048]{1,0:T(8,128)(2,1)S(1)} %constant_dynamic-update-slice_fusion.21, bf16[256,2048]{1,0:T(8,128)(2,1)S(1)} %collective-permute-done.40, bf16[256,2048]{1,0:T(8,128)(2,1)S(1)} %collective-permute-done.39, ...), kind=kOutput, calls=%fused_computation.19 | convolution fusion | flops 5931008000 | bytes 24379392 | tf_op jit(solution)/shard_map/dot_general | solution.py:37
  321.3 8.9 %fusion.60 = (bf16[1024,2048]{1,0:T(8,128)(2,1)S(1)}, f32[1024,2048]{1,0:T(8,128)S(1)}) fusion(bf16[1408,1024]{1,0:T(8,128)(2,1)S(1)} %copy-done.83, bf16[1408,2048]{1,0:T(8,128)(2,1)} %constant_dynamic-update-slice_fusion.30), kind=kOutput, calls=%fused_computation.274 | convolution fusion | flops 5907677184 | bytes 21233664 | tf_op jit(solution)/shard_map/dot_general | solution.py:41
  334.6 24.1 %collective-permute-done.53 = bf16[256,2048]{1,0:T(8,128)(2,1)S(1)} collective-permute-done((bf16[256,2048]{1,0:T(8,128)(2,1)S(1)}, bf16[256,2048]{1,0:T(8,128)(2,1)S(1)}, u32[]{:S(2)}, u32[]{:S(2)}) %collective-permute-start.53) | collective-permute-done | bytes 1048608 | tf_op jit(solution)/shard_map/ppermute | solution.py:133
  361.8 23.4 %collective-permute-done.55 = bf16[256,2048]{1,0:T(8,128)(2,1)S(1)} collective-permute-done((bf16[256,2048]{1,0:T(8,128)(2,1)S(1)}, bf16[256,2048]{1,0:T(8,128)(2,1)S(1)}, u32[]{:S(2)}, u32[]{:S(2)}) %collective-permute-start.55) | collective-permute-done | bytes 1048608 | tf_op jit(solution)/shard_map/ppermute | solution.py:124
  387.8 6.4 convolution_convert_fusion.2
  397.8 15.6 %multiply_convert_fusion = (bf16[1408,1024]{1,0:T(8,128)(2,1)}, bf16[1408,1024]{1,0:T(8,128)(2,1)}) fusion(f32[1408,1024]{1,0:T(8,128)} %fusion.61, f32[1408,1024]{1,0:T(8,128)} %get-tuple-element.294, bf16[1408,2048]{1,0:T(8,128)(2,1)} %constant_dynamic-update-slice_fusion.30, bf16[256,2048]{1,0:T(8,128)(2,1)} %copy-done.80, ...), kind=kOutput, calls=%fused_computation.17 | convolution fusion | flops 5942542336 | bytes 27262976 | tf_op jit(solution)/shard_map/dot_general | solution.py:37
  413.5 10.6 %convolution_convert_fusion.1 = bf16[1408,2048]{1,0:T(8,128)(2,1)} fusion(bf16[1408,1024]{1,0:T(8,128)(2,1)} %get-tuple-element.213, bf16[1024,2048]{1,0:T(8,128)(2,1)} %copy-done.13), kind=kOutput, calls=%fused_computation.14 | convolution fusion | flops 5908463616 | bytes 12845056 | tf_op jit(solution)/shard_map/dot_general | solution.py:33
  428.1 8.0 convolution_convert_fusion
  436.1 7.3 collective-permute-done.59
  444.8 10.6 %fusion.62 = f32[1024,2048]{1,0:T(8,128)} fusion(bf16[1408,1024]{1,0:T(8,128)(2,1)} %get-tuple-element.213, bf16[1408,2048]{1,0:T(8,128)(2,1)S(1)} %bitcast.137), kind=kOutput, calls=%fused_computation.276 | convolution fusion | flops 5905580032 | bytes 17039360 | tf_op jit(solution)/shard_map/dot_general | solution.py:41
  457.9 10.2 %convolution_add_fusion = f32[1024,2048]{1,0:T(8,128)S(1)} fusion(f32[1024,2048]{1,0:T(8,128)} %fusion.62, bf16[1408,1024]{1,0:T(8,128)(2,1)} %get-tuple-element.212, bf16[1408,2048]{1,0:T(8,128)(2,1)S(1)} %bitcast.127), kind=kOutput, calls=%fused_computation.28 | convolution fusion | flops 5907677184 | bytes 25427968 | tf_op jit(solution)/shard_map/dot_general | solution.py:41
  487.9 11.0 %collective-permute-done.68 = bf16[176,2048]{1,0:T(8,128)(2,1)S(1)} collective-permute-done((bf16[176,2048]{1,0:T(8,128)(2,1)S(1)}, bf16[176,2048]{1,0:T(8,128)(2,1)S(1)}, u32[]{:S(2)}, u32[]{:S(2)}) %collective-permute-start.68) | collective-permute-done | bytes 720928 | tf_op jit(solution)/shard_map/ppermute | solution.py:105
  527.5 18.6 %collective-permute-done.71 = bf16[256,2048]{1,0:T(8,128)(2,1)} collective-permute-done((bf16[256,2048]{1,0:T(8,128)(2,1)S(1)}, bf16[256,2048]{1,0:T(8,128)(2,1)}, u32[]{:S(2)}, u32[]{:S(2)}) %collective-permute-start.71) | collective-permute-done | bytes 1048608 | tf_op jit(solution)/shard_map/ppermute | solution.py:124
  548.9 6.8 collective-permute-done.73
  562.2 6.1 pad_maximum_fusion.4
  575.0 20.3 %shard_map.241 = bf16[1024,768]{1,0:T(8,128)(2,1)} custom-call(s32[4]{0:T(128)} %iota_xor_fusion.slot_ref, s32[4]{0:T(128)} %and_select_fusion.3.first_ref, bf16[1024,768]{1,0:T(8,128)(2,1)} %get-tuple-element.137.turned, bf16[1024,512]{1,0:T(8,128)(2,1)} %convolution_convert_fusion.6.out_grad, f32[1024,128]{1,0:T(8,128)} %get-tuple-element.280.cosine, ...), custom_call_target="tpu_custom_call" | custom-call | flops 4026531840 | bytes 4718592 | tf_op jit(solution)/shard_map/pallas_call | solution.py:704
  595.4 8.7 %convolution_convert_fusion.4 = bf16[2048,768]{1,0:T(8,128)(2,1)} fusion(bf16[1024,768]{1,0:T(8,128)(2,1)} %shard_map.241, bf16[1024,2048]{1,0:T(8,128)(2,1)} %copy-done, f32[2048]{0:T(1024)S(1)} %bitcast.157, f32[2048]{0:T(1024)S(1)} %bitcast.140, f32[1024]{0:T(1024)S(1)} %copy-done.67, f32[1024]{0:T(1024)S(1)} %copy-done.58), kind=kOutput, calls=%fused_computation.30 | convolution fusion | flops 3235381248 | bytes 8937472 | tf_op jit(solution)/shard_map/dot_general | solution.py:41
  625.2 20.2 %shard_map.242 = bf16[1024,768]{1,0:T(8,128)(2,1)} custom-call(s32[4]{0:T(128)} %iota_xor_fusion.slot_ref, s32[4]{0:T(128)} %and_select_fusion.3.first_ref, bf16[1024,768]{1,0:T(8,128)(2,1)} %get-tuple-element.160.turned, bf16[1024,512]{1,0:T(8,128)(2,1)} %convolution_convert_fusion.6.out_grad, f32[1024,128]{1,0:T(8,128)} %get-tuple-element.280.cosine, ...), custom_call_target="tpu_custom_call" | custom-call | flops 4026531840 | bytes 4718592 | tf_op jit(solution)/shard_map/pallas_call | solution.py:704
  650.6 20.8 %collective-permute-done.84 = bf16[256,1280]{1,0:T(8,128)(2,1)S(1)} collective-permute-done((bf16[256,1280]{1,0:T(8,128)(2,1)S(1)}, bf16[256,1280]{1,0:T(8,128)(2,1)S(1)}, u32[]{:S(2)}, u32[]{:S(2)}) %collective-permute-start.84) | collective-permute-done | bytes 655392 | tf_op jit(solution)/shard_map/ppermute | solution.py:105
  683.3 8.8 %fusion.63 = f32[1024,2048]{1,0:T(8,128)S(1)} fusion(bf16[1024,1536]{1,0:T(8,128)(2,1)S(1)} %pad_maximum_fusion.5, bf16[2048,1536]{1,0:T(8,128)(2,1)} %constant_dynamic-update-slice_fusion.45), kind=kOutput, calls=%fused_computation.277 | convolution fusion | flops 6442450944 | bytes 17825792 | tf_op jit(solution)/shard_map/dot_general | solution.py:37
  710.7 6.6 collective-permute-done.96
  724.1 9.8 %collective-permute-done.94 = bf16[256,1280]{1,0:T(8,128)(2,1)S(1)} collective-permute-done((bf16[256,1280]{1,0:T(8,128)(2,1)S(1)}, bf16[256,1280]{1,0:T(8,128)(2,1)S(1)}, u32[]{:S(2)}, u32[]{:S(2)}) %collective-permute-start.94) | collective-permute-done | bytes 655392 | tf_op jit(solution)/shard_map/ppermute | solution.py:105
  787.9 8.1 shard_map.244
  (645 shorter events, 424.1 us)
Async XLA Ops:
  13.6 32.5 %collective-permute-start.8 = (bf16[80,2048]{1,0:T(8,128)(2,1)}, bf16[80,2048]{1,0:T(8,128)(2,1)}, u32[]{:S(2)}, u32[]{:S(2)}) collective-permute-start(bf16[80,2048]{1,0:T(8,128)(2,1)} %pad_maximum_fusion.16), channel_id=1, source_target_pairs={{0,2},{2,4},{4,6},{6,7},{7,5},{5,3},{3,1},{1,0},{8,10},{10,12},{12... | collective-permute-start | bytes 983048 | tf_op jit(solution)/shard_map/ppermute | solution.py:77
  15.7 26.2 %collective-permute-start.4 = (bf16[80,2048]{1,0:T(8,128)(2,1)}, bf16[80,2048]{1,0:T(8,128)(2,1)}, u32[]{:S(2)}, u32[]{:S(2)}) collective-permute-start(bf16[80,2048]{1,0:T(8,128)(2,1)} %pad_maximum_fusion.16), channel_id=1, source_target_pairs={{2,0},{4,2},{6,4},{7,6},{5,7},{3,5},{1,3},{0,1},{10,8},{12,10},{14... | collective-permute-start | bytes 983048 | tf_op jit(solution)/shard_map/ppermute | solution.py:78
  15.7 30.0 %collective-permute-start.17 = (bf16[256,2048]{1,0:T(8,128)(2,1)S(1)}, bf16[256,2048]{1,0:T(8,128)(2,1)}, u32[]{:S(2)}, u32[]{:S(2)}) collective-permute-start(bf16[256,2048]{1,0:T(8,128)(2,1)S(1)} %bitcast.120), channel_id=1, source_target_pairs={{0,16},{8,24},{16,0},{24,8},{1,17},{9,25},{17,1},{25,9},{2,18},{10... | collective-permute-start | bytes 3145736 | tf_op jit(solution)/shard_map/ppermute | solution.py:124
  79.0 54.4 %collective-permute-start.22 = (bf16[176,2048]{1,0:T(8,128)(2,1)}, bf16[176,2048]{1,0:T(8,128)(2,1)}, u32[]{:S(2)}, u32[]{:S(2)}) collective-permute-start(bf16[176,2048]{1,0:T(8,128)(2,1)} %get-tuple-element.108), channel_id=1, source_target_pairs={{2,0},{4,2},{6,4},{7,6},{5,7},{3,5},{1,3},{0,1},{10,8},{12,10},{14... | collective-permute-start | bytes 2162696 | tf_op jit(solution)/shard_map/ppermute | solution.py:78
  79.5 53.9 %collective-permute-start.21 = (bf16[176,2048]{1,0:T(8,128)(2,1)}, bf16[176,2048]{1,0:T(8,128)(2,1)}, u32[]{:S(2)}, u32[]{:S(2)}) collective-permute-start(bf16[176,2048]{1,0:T(8,128)(2,1)} %get-tuple-element.108), channel_id=1, source_target_pairs={{0,2},{2,4},{4,6},{6,7},{7,5},{5,3},{3,1},{1,0},{8,10},{10,12},{12... | collective-permute-start | bytes 2162696 | tf_op jit(solution)/shard_map/ppermute | solution.py:77
  83.1 28.4 %collective-permute-start.19 = (bf16[128,1536]{1,0:T(8,128)(2,1)S(1)}, bf16[128,1536]{1,0:T(8,128)(2,1)S(1)}, u32[]{:S(2)}, u32[]{:S(2)}) collective-permute-start(bf16[128,1536]{1,0:T(8,128)(2,1)S(1)} %slice.370), channel_id=1, source_target_pairs={{0,2},{2,4},{4,6},{6,7},{7,5},{5,3},{3,1},{1,0},{8,10},{10,12},{12... | collective-permute-start | bytes 1179656 | tf_op jit(solution)/shard_map/ppermute | solution.py:77
  133.4 37.1 %collective-permute-start.25 = (bf16[176,2048]{1,0:T(8,128)(2,1)}, bf16[176,2048]{1,0:T(8,128)(2,1)}, u32[]{:S(2)}, u32[]{:S(2)}) collective-permute-start(bf16[176,2048]{1,0:T(8,128)(2,1)} %get-tuple-element.114), channel_id=1, source_target_pairs={{0,2},{2,4},{4,6},{6,7},{7,5},{5,3},{3,1},{1,0},{8,10},{10,12},{12... | collective-permute-start | bytes 2162696 | tf_op jit(solution)/shard_map/ppermute | solution.py:77
  135.0 37.0 %collective-permute-start.26 = (bf16[176,2048]{1,0:T(8,128)(2,1)}, bf16[176,2048]{1,0:T(8,128)(2,1)}, u32[]{:S(2)}, u32[]{:S(2)}) collective-permute-start(bf16[176,2048]{1,0:T(8,128)(2,1)} %get-tuple-element.114), channel_id=1, source_target_pairs={{2,0},{4,2},{6,4},{7,6},{5,7},{3,5},{1,3},{0,1},{10,8},{12,10},{14... | collective-permute-start | bytes 2162696 | tf_op jit(solution)/shard_map/ppermute | solution.py:78
  135.5 33.0 %collective-permute-start.24 = (bf16[176,2048]{1,0:T(8,128)(2,1)}, bf16[176,2048]{1,0:T(8,128)(2,1)}, u32[]{:S(2)}, u32[]{:S(2)}) collective-permute-start(bf16[176,2048]{1,0:T(8,128)(2,1)} %collective-permute-done.22), channel_id=1, source_target_pairs={{2,0},{4,2},{6,4},{7,6},{5,7},{3,5},{1,3},{0,1},{10,8},{12,10},{14... | collective-permute-start | bytes 2162696 | tf_op jit(solution)/shard_map/ppermute | solution.py:78
  137.1 31.8 %collective-permute-start.23 = (bf16[176,2048]{1,0:T(8,128)(2,1)}, bf16[176,2048]{1,0:T(8,128)(2,1)}, u32[]{:S(2)}, u32[]{:S(2)}) collective-permute-start(bf16[176,2048]{1,0:T(8,128)(2,1)} %collective-permute-done.21), channel_id=1, source_target_pairs={{0,2},{2,4},{4,6},{6,7},{7,5},{5,3},{3,1},{1,0},{8,10},{10,12},{12... | collective-permute-start | bytes 2162696 | tf_op jit(solution)/shard_map/ppermute | solution.py:77
  170.5 30.7 %collective-permute-start.29 = (bf16[176,2048]{1,0:T(8,128)(2,1)}, bf16[176,2048]{1,0:T(8,128)(2,1)}, u32[]{:S(2)}, u32[]{:S(2)}) collective-permute-start(bf16[176,2048]{1,0:T(8,128)(2,1)} %collective-permute-done.25), channel_id=1, source_target_pairs={{0,2},{2,4},{4,6},{6,7},{7,5},{5,3},{3,1},{1,0},{8,10},{10,12},{12... | collective-permute-start | bytes 2162696 | tf_op jit(solution)/shard_map/ppermute | solution.py:77
  172.1 29.1 %collective-permute-start.30 = (bf16[176,2048]{1,0:T(8,128)(2,1)}, bf16[176,2048]{1,0:T(8,128)(2,1)}, u32[]{:S(2)}, u32[]{:S(2)}) collective-permute-start(bf16[176,2048]{1,0:T(8,128)(2,1)} %collective-permute-done.26), channel_id=1, source_target_pairs={{2,0},{4,2},{6,4},{7,6},{5,7},{3,5},{1,3},{0,1},{10,8},{12,10},{14... | collective-permute-start | bytes 2162696 | tf_op jit(solution)/shard_map/ppermute | solution.py:78
  212.4 25.3 %collective-permute-start.33 = (bf16[256,2048]{1,0:T(8,128)(2,1)S(1)}, bf16[256,2048]{1,0:T(8,128)(2,1)S(1)}, u32[]{:S(2)}, u32[]{:S(2)}) collective-permute-start(bf16[256,2048]{1,0:T(8,128)(2,1)S(1)} %fusion.24), channel_id=1, source_target_pairs={{0,16},{8,24},{16,0},{24,8},{1,17},{9,25},{17,1},{25,9},{2,18},{10... | collective-permute-start | bytes 3145736 | tf_op jit(solution)/shard_map/ppermute | solution.py:133
  474.4 27.7 %collective-permute-start.63 = (bf16[256,2048]{1,0:T(8,128)(2,1)S(1)}, bf16[256,2048]{1,0:T(8,128)(2,1)S(1)}, u32[]{:S(2)}, u32[]{:S(2)}) collective-permute-start(bf16[256,2048]{1,0:T(8,128)(2,1)S(1)} %get-tuple-element.252), channel_id=1, source_target_pairs={{0,8},{8,0},{16,24},{24,16},{1,9},{9,1},{17,25},{25,17},{2,10},{10... | collective-permute-start | bytes 3145736 | tf_op jit(solution)/shard_map/ppermute | solution.py:131
  485.7 27.6 %collective-permute-start.66 = (bf16[176,2048]{1,0:T(8,128)(2,1)S(1)}, bf16[176,2048]{1,0:T(8,128)(2,1)S(1)}, u32[]{:S(2)}, u32[]{:S(2)}) collective-permute-start(bf16[176,2048]{1,0:T(8,128)(2,1)S(1)} %get-tuple-element.146), channel_id=1, source_target_pairs={{0,2},{2,4},{4,6},{6,7},{7,5},{5,3},{3,1},{1,0},{8,10},{10,12},{12... | collective-permute-start | bytes 2162696 | tf_op jit(solution)/shard_map/ppermute | solution.py:105
  486.6 26.7 %collective-permute-start.67 = (bf16[176,2048]{1,0:T(8,128)(2,1)S(1)}, bf16[176,2048]{1,0:T(8,128)(2,1)S(1)}, u32[]{:S(2)}, u32[]{:S(2)}) collective-permute-start(bf16[176,2048]{1,0:T(8,128)(2,1)S(1)} %get-tuple-element.147), channel_id=1, source_target_pairs={{2,0},{4,2},{6,4},{7,6},{5,7},{3,5},{1,3},{0,1},{10,8},{12,10},{14... | collective-permute-start | bytes 2162696 | tf_op jit(solution)/shard_map/ppermute | solution.py:106
  524.1 31.6 %collective-permute-start.73 = (bf16[352,2048]{1,0:T(8,128)(2,1)}, bf16[352,2048]{1,0:T(8,128)(2,1)}, u32[]{:S(2)}, u32[]{:S(2)}) collective-permute-start(bf16[352,2048]{1,0:T(8,128)(2,1)} %pad_maximum_fusion.6), channel_id=1, source_target_pairs={{0,2},{2,4},{4,6},{6,7},{7,5},{5,3},{3,1},{1,0},{8,10},{10,12},{12... | collective-permute-start | bytes 4325384 | tf_op jit(solution)/shard_map/ppermute | solution.py:105
  526.0 33.2 %collective-permute-start.74 = (bf16[352,2048]{1,0:T(8,128)(2,1)}, bf16[352,2048]{1,0:T(8,128)(2,1)}, u32[]{:S(2)}, u32[]{:S(2)}) collective-permute-start(bf16[352,2048]{1,0:T(8,128)(2,1)} %pad_maximum_fusion.7), channel_id=1, source_target_pairs={{2,0},{4,2},{6,4},{7,6},{5,7},{3,5},{1,3},{0,1},{10,8},{12,10},{14... | collective-permute-start | bytes 4325384 | tf_op jit(solution)/shard_map/ppermute | solution.py:106
  527.5 34.7 %collective-permute-start.70 = (bf16[256,2048]{1,0:T(8,128)(2,1)S(1)}, bf16[256,2048]{1,0:T(8,128)(2,1)S(1)}, u32[]{:S(2)}, u32[]{:S(2)}) collective-permute-start(bf16[256,2048]{1,0:T(8,128)(2,1)S(1)} %get-tuple-element.198), channel_id=1, source_target_pairs={{0,8},{8,0},{16,24},{24,16},{1,9},{9,1},{17,25},{25,17},{2,10},{10... | collective-permute-start | bytes 3145736 | tf_op jit(solution)/shard_map/ppermute | solution.py:125
  571.7 43.4 %collective-permute-start.77 = (bf16[176,2048]{1,0:T(8,128)(2,1)}, bf16[176,2048]{1,0:T(8,128)(2,1)S(1)}, u32[]{:S(2)}, u32[]{:S(2)}) collective-permute-start(bf16[176,2048]{1,0:T(8,128)(2,1)} %add_convert_fusion.9.p0), channel_id=1, source_target_pairs={{0,8},{8,0},{16,24},{24,16},{1,9},{9,1},{17,25},{25,17},{2,10},{10... | collective-permute-start | bytes 2162696 | tf_op jit(solution)/shard_map/ppermute | solution.py:125
  571.7 32.3 %collective-permute-start.78 = (bf16[176,2048]{1,0:T(8,128)(2,1)}, bf16[176,2048]{1,0:T(8,128)(2,1)}, u32[]{:S(2)}, u32[]{:S(2)}) collective-permute-start(bf16[176,2048]{1,0:T(8,128)(2,1)} %add_convert_fusion.9.p0), channel_id=1, source_target_pairs={{0,16},{8,24},{16,0},{24,8},{1,17},{9,25},{17,1},{25,9},{2,18},{10... | collective-permute-start | bytes 2162696 | tf_op jit(solution)/shard_map/ppermute | solution.py:124
  572.6 42.7 %collective-permute-start.75 = (bf16[352,2048]{1,0:T(8,128)(2,1)}, bf16[352,2048]{1,0:T(8,128)(2,1)}, u32[]{:S(2)}, u32[]{:S(2)}) collective-permute-start(bf16[352,2048]{1,0:T(8,128)(2,1)} %add_convert_fusion.5), channel_id=1, source_target_pairs={{0,2},{2,4},{4,6},{6,7},{7,5},{5,3},{3,1},{1,0},{8,10},{10,12},{12... | collective-permute-start | bytes 4325384 | tf_op jit(solution)/shard_map/ppermute | solution.py:105
  573.0 42.2 %collective-permute-start.76 = (bf16[352,2048]{1,0:T(8,128)(2,1)}, bf16[352,2048]{1,0:T(8,128)(2,1)}, u32[]{:S(2)}, u32[]{:S(2)}) collective-permute-start(bf16[352,2048]{1,0:T(8,128)(2,1)} %add_convert_fusion.4), channel_id=1, source_target_pairs={{2,0},{4,2},{6,4},{7,6},{5,7},{3,5},{1,3},{0,1},{10,8},{12,10},{14... | collective-permute-start | bytes 4325384 | tf_op jit(solution)/shard_map/ppermute | solution.py:106
  616.2 29.2 %collective-permute-start.80 = (bf16[128,1280]{1,0:T(8,128)(2,1)}, bf16[128,1280]{1,0:T(8,128)(2,1)}, u32[]{:S(2)}, u32[]{:S(2)}) collective-permute-start(bf16[128,1280]{1,0:T(8,128)(2,1)} %get-tuple-element.163), channel_id=1, source_target_pairs={{0,2},{2,4},{4,6},{6,7},{7,5},{5,3},{3,1},{1,0},{8,10},{10,12},{12... | collective-permute-start | bytes 983048 | tf_op jit(solution)/shard_map/ppermute | solution.py:105
  616.6 28.8 %collective-permute-start.81 = (bf16[128,1280]{1,0:T(8,128)(2,1)}, bf16[128,1280]{1,0:T(8,128)(2,1)}, u32[]{:S(2)}, u32[]{:S(2)}) collective-permute-start(bf16[128,1280]{1,0:T(8,128)(2,1)} %get-tuple-element.164), channel_id=1, source_target_pairs={{2,0},{4,2},{6,4},{7,6},{5,7},{3,5},{1,3},{0,1},{10,8},{12,10},{14... | collective-permute-start | bytes 983048 | tf_op jit(solution)/shard_map/ppermute | solution.py:106
  620.1 55.2 %collective-permute-start.82 = (bf16[352,2048]{1,0:T(8,128)(2,1)S(1)}, bf16[352,2048]{1,0:T(8,128)(2,1)}, u32[]{:S(2)}, u32[]{:S(2)}) collective-permute-start(bf16[352,2048]{1,0:T(8,128)(2,1)S(1)} %add_convert_fusion.3), channel_id=1, source_target_pairs={{0,2},{2,4},{4,6},{6,7},{7,5},{5,3},{3,1},{1,0},{8,10},{10,12},{12... | collective-permute-start | bytes 4325384 | tf_op jit(solution)/shard_map/ppermute | solution.py:105
  623.6 51.7 %collective-permute-start.83 = (bf16[352,2048]{1,0:T(8,128)(2,1)}, bf16[352,2048]{1,0:T(8,128)(2,1)}, u32[]{:S(2)}, u32[]{:S(2)}) collective-permute-start(bf16[352,2048]{1,0:T(8,128)(2,1)} %add_convert_fusion.2), channel_id=1, source_target_pairs={{2,0},{4,2},{6,4},{7,6},{5,7},{3,5},{1,3},{0,1},{10,8},{12,10},{14... | collective-permute-start | bytes 4325384 | tf_op jit(solution)/shard_map/ppermute | solution.py:106
  700.9 35.1 %collective-permute-start.90 = (bf16[256,2048]{1,0:T(8,128)(2,1)}, bf16[256,2048]{1,0:T(8,128)(2,1)S(1)}, u32[]{:S(2)}, u32[]{:S(2)}) collective-permute-start(bf16[256,2048]{1,0:T(8,128)(2,1)} %get-tuple-element.250), channel_id=1, source_target_pairs={{0,8},{8,0},{16,24},{24,16},{1,9},{9,1},{17,25},{25,17},{2,10},{10... | collective-permute-start | bytes 3145736 | tf_op jit(solution)/shard_map/ppermute | solution.py:131
  705.2 30.8 %collective-permute-start.92 = (bf16[256,2048]{1,0:T(8,128)(2,1)S(1)}, bf16[256,2048]{1,0:T(8,128)(2,1)S(1)}, u32[]{:S(2)}, u32[]{:S(2)}) collective-permute-start(bf16[256,2048]{1,0:T(8,128)(2,1)S(1)} %add_convert_fusion.6), channel_id=1, source_target_pairs={{0,16},{8,24},{16,0},{24,8},{1,17},{9,25},{17,1},{25,9},{2,18},{10... | collective-permute-start | bytes 3145736 | tf_op jit(solution)/shard_map/ppermute | solution.py:133
  740.5 31.9 %collective-permute-start.110 = (bf16[352,2048]{1,0:T(8,128)(2,1)}, bf16[352,2048]{1,0:T(8,128)(2,1)}, u32[]{:S(2)}, u32[]{:S(2)}) collective-permute-start(bf16[352,2048]{1,0:T(8,128)(2,1)} %add_convert_fusion.1.p0), channel_id=1, source_target_pairs={{0,16},{8,24},{16,0},{24,8},{1,17},{9,25},{17,1},{25,9},{2,18},{10... | collective-permute-start | bytes 4325384 | tf_op jit(solution)/shard_map/ppermute | solution.py:124
  750.1 36.8 %collective-permute-start.109 = (bf16[352,2048]{1,0:T(8,128)(2,1)}, bf16[352,2048]{1,0:T(8,128)(2,1)}, u32[]{:S(2)}, u32[]{:S(2)}) collective-permute-start(bf16[352,2048]{1,0:T(8,128)(2,1)} %add_convert_fusion.1.p0), channel_id=1, source_target_pairs={{0,8},{8,0},{16,24},{24,16},{1,9},{9,1},{17,25},{25,17},{2,10},{10... | collective-permute-start | bytes 4325384 | tf_op jit(solution)/shard_map/ppermute | solution.py:125
  775.2 25.4 %collective-permute-start.115 = (bf16[64,2048]{1,0:T(8,128)(2,1)}, bf16[64,2048]{1,0:T(8,128)(2,1)}, u32[]{:S(2)}, u32[]{:S(2)}) collective-permute-start(bf16[64,2048]{1,0:T(8,128)(2,1)} %bitcast.53.p0), channel_id=1, source_target_pairs={{0,8},{8,0},{16,24},{24,16},{1,9},{9,1},{17,25},{25,17},{2,10},{10... | collective-permute-start | bytes 786440 | tf_op jit(solution)/shard_map/ppermute | solution.py:125
  (178 other events, 2642.9 us)

commit v5 on v4

--- a/solution.py
+++ b/solution.py
@@ -923,10 +923,10 @@
         axis=1,
     ).reshape(shards, -1, LANES)
     grad_w_down = net.final_rows(parts_down, pin(factor, raw_second))
-    parts_first, parts_out = net.spread("F"), net.spread("O")
+    parts_first, parts_out = net.spread("F"), net.spread("O", *third)
     last = net.hop("S", *third)
     parts_pair = net.spread("W", grad_one, hold=last)
-    vectors = net.small_reduce(pin(vectors, *third), *last).reshape(-1)
+    vectors = net.small_reduce(vectors, *last).reshape(-1)
     loss = 2.0 * vectors[4 * vec + bias_share] / (sum_count * width)
     scaled = factor * vectors
     grad_w_gate_up = net.final_pairs(parts_pair, factor)

time: 828 us -> 840 us (1.014)
  Pallas kernels: 98.2 us -> 85.8 us
  waiting for transfers between devices: 266 us -> 277 us
    ppermute x16, waiting for transfers between devices: 68.8 us -> 79.2 us  [step(): ahead = lax.ppermute(pin(self.ahead, *after), 'fsdp', NEXT)]
    convert_element_type x10 -> x11, other arithmetic: 21.5 us -> 23.9 us  [step(): self.ahead, self.behind = (ahead.astype(BF16), behind.astype(BF16))]
  transfers between devices with their start and end apart: 118 -> 118, of which waited for: 51 -> 50; matrix products, arithmetic and copies ran while one was open for 33% -> 33% of each run, Pallas kernels for 11% -> 9%
where the time goes in v5:
time: 840 us; the launch traced here: 831 us
  waiting for transfers between devices  277 us (33%)
  matrix products  136 us (16%)
  local copies, waits for them, and re-layouts  114 us (14%)
  starting transfers between devices  110 us (13%)
  other arithmetic  97.2 us (12%)
  Pallas kernels  85.8 us (10%)
  between operations  10.3 us (1%)
    ppermute x16, waiting for transfers between devices, step(): ahead = lax.ppermute(pin(self.ahead, *after), 'fsdp', NEXT)  79.2 us
    ppermute x20, waiting for transfers between devices, step(): ahead = lax.ppermute(ahead, 'fsdp', NEXT)  59.6 us
    ppermute x9, waiting for transfers between devices, seq_gather(): over = lax.ppermute(mine, 'seq', ROW)  56.7 us
    dot_general x5, matrix products, dot_nt(): lax.dot_general(a, b, (((1,), (1,)), ((), ())), preferred_element_type=F32)  48.5 us
    dot_general x6, matrix products, dot_tn(): lax.dot_general(a, b, (((0,), (0,)), ((), ())), preferred_element_type=F32)  46.8 us
    unnamed x237, local copies, waits for them, and re-layouts  44.3 us
    dot_general x5, matrix products, dot_nn(): lax.dot_general(a, b, (((1,), (0,)), ((), ())), preferred_element_type=F32)  40.9 us
    ppermute x4, waiting for transfers between devices, seq_scatter(): over = lax.ppermute(far, 'seq', ROW)  38.5 us
  transfers between devices with their start and end apart: 118, of which 50 were waited for; matrix products, arithmetic and copies ran while one was open for 33% of the time, Pallas kernels for 9%

profile of v5, /device:TPU:0, one launch (start us, length us, event | category | flops | bytes accessed | tf_op | source)
XLA Modules:
  0.0 830.8 jit_solution(9301241313806311965)
XLA Ops:
  63.5 6.1 pad_maximum_fusion.1
  88.9 16.8 %collective-permute-done.11 = bf16[80,2048]{1,0:T(8,128)(2,1)S(1)} collective-permute-done((bf16[80,2048]{1,0:T(8,128)(2,1)S(1)}, bf16[80,2048]{1,0:T(8,128)(2,1)S(1)}, u32[]{:S(2)}, u32[]{:S(2)}) %collective-permute-start.11) | collective-permute-done | bytes 327712 | tf_op jit(solution)/shard_map/ppermute | solution.py:77
  137.9 12.3 %fusion.45.qkv = f32[1024,1536]{1,0:T(8,128)} fusion(bf16[2048,1536]{1,0:T(8,128)(2,1)} %constant_dynamic-update-slice_fusion.45, bf16[1024,2048]{1,0:T(8,128)(2,1)} %copy-done, f32[2048]{0:T(1024)S(1)} %bitcast.156, f32[2048]{0:T(1024)S(1)} %bitcast.139, f32[1024]{0:T(1024)S(1)} %add_rsqrt_fusion, f32[1024]{0:T(1024)S(1)} %broadcast_multiply_fusion.2), kind=kOutput, calls=%fused_computation.261 | convolution fusion | flops 6455033856 | bytes 16801792 | tf_op jit(solution)/shard_map/dot_general | solution.py:33
  150.2 13.1 %shard_map.239 = (bf16[1024,768]{1,0:T(8,128)(2,1)}, bf16[1024,256]{1,0:T(8,128)(2,1)}) custom-call(s32[4]{0:T(128)} %iota_xor_fusion.slot_ref, s32[4]{0:T(128)} %and_select_fusion.3.first_ref, f32[1024,1536]{1,0:T(8,128)} %fusion.45.qkv, f32[1,1536]{1,0:T(1,128)} %reshape.312.bias, f32[1024,128]{1,0:T(8,128)} %get-tuple-element.278.cosine, ...), custom_call_target="tpu_custom_call" | custom-call | flops 1610612736 | bytes 6291456 | tf_op jit(solution)/shard_map/pallas_call | solution.py:579
  175.2 13.2 %shard_map.240 = (bf16[1024,768]{1,0:T(8,128)(2,1)}, bf16[1024,256]{1,0:T(8,128)(2,1)}) custom-call(s32[4]{0:T(128)} %iota_xor_fusion.slot_ref, s32[4]{0:T(128)} %and_select_fusion.3.first_ref, f32[1024,1536]{1,0:T(8,128)} %fusion.45.qkv, f32[1,1536]{1,0:T(1,128)} %reshape.312.bias, f32[1024,128]{1,0:T(8,128)} %get-tuple-element.278.cosine, ...), custom_call_target="tpu_custom_call" | custom-call | flops 1610612736 | bytes 6291456 | tf_op jit(solution)/shard_map/pallas_call | solution.py:579
  190.3 10.9 %collective-permute-done.29 = bf16[176,2048]{1,0:T(8,128)(2,1)} collective-permute-done((bf16[176,2048]{1,0:T(8,128)(2,1)}, bf16[176,2048]{1,0:T(8,128)(2,1)}, u32[]{:S(2)}, u32[]{:S(2)}) %collective-permute-start.29) | collective-permute-done | bytes 720928 | tf_op jit(solution)/shard_map/ppermute | solution.py:77
  228.7 8.9 %collective-permute-done.33 = bf16[256,2048]{1,0:T(8,128)(2,1)S(1)} collective-permute-done((bf16[256,2048]{1,0:T(8,128)(2,1)S(1)}, bf16[256,2048]{1,0:T(8,128)(2,1)S(1)}, u32[]{:S(2)}, u32[]{:S(2)}) %collective-permute-start.33) | collective-permute-done | bytes 1048608 | tf_op jit(solution)/shard_map/ppermute | solution.py:133
  258.8 9.4 %collective-permute-done.39 = bf16[256,2048]{1,0:T(8,128)(2,1)S(1)} collective-permute-done((bf16[256,2048]{1,0:T(8,128)(2,1)S(1)}, bf16[256,2048]{1,0:T(8,128)(2,1)S(1)}, u32[]{:S(2)}, u32[]{:S(2)}) %collective-permute-start.39) | collective-permute-done | bytes 1048608 | tf_op jit(solution)/shard_map/ppermute | solution.py:124
  276.8 8.2 fusion.61
  293.3 12.6 %multiply_convert_fusion.1 = (bf16[1408,1024]{1,0:T(8,128)(2,1)}, f32[1408,1024]{1,0:T(8,128)}) fusion(f32[1408,1024]{1,0:T(8,128)} %fusion.61, bf16[1408,2048]{1,0:T(8,128)(2,1)S(1)} %constant_dynamic-update-slice_fusion.21, bf16[256,2048]{1,0:T(8,128)(2,1)S(1)} %collective-permute-done.40, bf16[256,2048]{1,0:T(8,128)(2,1)S(1)} %collective-permute-done.39, ...), kind=kOutput, calls=%fused_computation.19 | convolution fusion | flops 5931008000 | bytes 24379392 | tf_op jit(solution)/shard_map/dot_general | solution.py:37
  321.3 8.9 %fusion.60 = (bf16[1024,2048]{1,0:T(8,128)(2,1)S(1)}, f32[1024,2048]{1,0:T(8,128)S(1)}) fusion(bf16[1408,1024]{1,0:T(8,128)(2,1)S(1)} %copy-done.83, bf16[1408,2048]{1,0:T(8,128)(2,1)} %constant_dynamic-update-slice_fusion.30), kind=kOutput, calls=%fused_computation.274 | convolution fusion | flops 5907677184 | bytes 21233664 | tf_op jit(solution)/shard_map/dot_general | solution.py:41
  334.6 24.1 %collective-permute-done.53 = bf16[256,2048]{1,0:T(8,128)(2,1)S(1)} collective-permute-done((bf16[256,2048]{1,0:T(8,128)(2,1)S(1)}, bf16[256,2048]{1,0:T(8,128)(2,1)S(1)}, u32[]{:S(2)}, u32[]{:S(2)}) %collective-permute-start.53) | collective-permute-done | bytes 1048608 | tf_op jit(solution)/shard_map/ppermute | solution.py:133
  361.8 23.3 %collective-permute-done.55 = bf16[256,2048]{1,0:T(8,128)(2,1)S(1)} collective-permute-done((bf16[256,2048]{1,0:T(8,128)(2,1)S(1)}, bf16[256,2048]{1,0:T(8,128)(2,1)S(1)}, u32[]{:S(2)}, u32[]{:S(2)}) %collective-permute-start.55) | collective-permute-done | bytes 1048608 | tf_op jit(solution)/shard_map/ppermute | solution.py:124
  387.7 6.4 convolution_convert_fusion.2
  397.8 15.6 %multiply_convert_fusion = (bf16[1408,1024]{1,0:T(8,128)(2,1)}, bf16[1408,1024]{1,0:T(8,128)(2,1)}) fusion(f32[1408,1024]{1,0:T(8,128)} %fusion.61, f32[1408,1024]{1,0:T(8,128)} %get-tuple-element.292, bf16[1408,2048]{1,0:T(8,128)(2,1)} %constant_dynamic-update-slice_fusion.30, bf16[256,2048]{1,0:T(8,128)(2,1)} %copy-done.80, ...), kind=kOutput, calls=%fused_computation.17 | convolution fusion | flops 5942542336 | bytes 27262976 | tf_op jit(solution)/shard_map/dot_general | solution.py:37
  413.5 10.6 %convolution_convert_fusion.1 = bf16[1408,2048]{1,0:T(8,128)(2,1)} fusion(bf16[1408,1024]{1,0:T(8,128)(2,1)} %get-tuple-element.213, bf16[1024,2048]{1,0:T(8,128)(2,1)} %copy-done.13), kind=kOutput, calls=%fused_computation.14 | convolution fusion | flops 5908463616 | bytes 12845056 | tf_op jit(solution)/shard_map/dot_general | solution.py:33
  428.0 8.0 convolution_convert_fusion
  436.0 7.3 collective-permute-done.59
  444.8 10.6 %fusion.62 = f32[1024,2048]{1,0:T(8,128)} fusion(bf16[1408,1024]{1,0:T(8,128)(2,1)} %get-tuple-element.213, bf16[1408,2048]{1,0:T(8,128)(2,1)S(1)} %bitcast.137), kind=kOutput, calls=%fused_computation.276 | convolution fusion | flops 5905580032 | bytes 17039360 | tf_op jit(solution)/shard_map/dot_general | solution.py:41
  457.9 10.2 %convolution_add_fusion = f32[1024,2048]{1,0:T(8,128)S(1)} fusion(f32[1024,2048]{1,0:T(8,128)} %fusion.62, bf16[1408,1024]{1,0:T(8,128)(2,1)} %get-tuple-element.212, bf16[1408,2048]{1,0:T(8,128)(2,1)S(1)} %bitcast.127), kind=kOutput, calls=%fused_computation.28 | convolution fusion | flops 5907677184 | bytes 25427968 | tf_op jit(solution)/shard_map/dot_general | solution.py:41
  488.0 10.9 %collective-permute-done.68 = bf16[176,2048]{1,0:T(8,128)(2,1)S(1)} collective-permute-done((bf16[176,2048]{1,0:T(8,128)(2,1)S(1)}, bf16[176,2048]{1,0:T(8,128)(2,1)S(1)}, u32[]{:S(2)}, u32[]{:S(2)}) %collective-permute-start.68) | collective-permute-done | bytes 720928 | tf_op jit(solution)/shard_map/ppermute | solution.py:105
  527.6 18.6 %collective-permute-done.71 = bf16[256,2048]{1,0:T(8,128)(2,1)} collective-permute-done((bf16[256,2048]{1,0:T(8,128)(2,1)S(1)}, bf16[256,2048]{1,0:T(8,128)(2,1)}, u32[]{:S(2)}, u32[]{:S(2)}) %collective-permute-start.71) | collective-permute-done | bytes 1048608 | tf_op jit(solution)/shard_map/ppermute | solution.py:124
  549.0 6.8 collective-permute-done.73
  562.3 6.1 pad_maximum_fusion.4
  575.0 16.8 %shard_map.241 = bf16[1024,768]{1,0:T(8,128)(2,1)} custom-call(s32[4]{0:T(128)} %iota_xor_fusion.slot_ref, s32[4]{0:T(128)} %and_select_fusion.3.first_ref, bf16[1024,768]{1,0:T(8,128)(2,1)} %get-tuple-element.137.turned, bf16[1024,512]{1,0:T(8,128)(2,1)} %convolution_convert_fusion.6.out_grad, f32[1024,128]{1,0:T(8,128)} %get-tuple-element.278.cosine, ...), custom_call_target="tpu_custom_call" | custom-call | flops 4026531840 | bytes 4718592 | tf_op jit(solution)/shard_map/pallas_call | solution.py:704
  591.9 8.7 %convolution_convert_fusion.4 = bf16[2048,768]{1,0:T(8,128)(2,1)} fusion(bf16[1024,768]{1,0:T(8,128)(2,1)} %shard_map.241, bf16[1024,2048]{1,0:T(8,128)(2,1)} %copy-done, f32[2048]{0:T(1024)S(1)} %bitcast.157, f32[2048]{0:T(1024)S(1)} %bitcast.140, f32[1024]{0:T(1024)S(1)} %copy-done.66, f32[1024]{0:T(1024)S(1)} %copy-done.57), kind=kOutput, calls=%fused_computation.30 | convolution fusion | flops 3235381248 | bytes 8937472 | tf_op jit(solution)/shard_map/dot_general | solution.py:41
  624.4 16.6 %shard_map.242 = bf16[1024,768]{1,0:T(8,128)(2,1)} custom-call(s32[4]{0:T(128)} %iota_xor_fusion.slot_ref, s32[4]{0:T(128)} %and_select_fusion.3.first_ref, bf16[1024,768]{1,0:T(8,128)(2,1)} %get-tuple-element.160.turned, bf16[1024,512]{1,0:T(8,128)(2,1)} %convolution_convert_fusion.6.out_grad, f32[1024,128]{1,0:T(8,128)} %get-tuple-element.278.cosine, ...), custom_call_target="tpu_custom_call" | custom-call | flops 4026531840 | bytes 4718592 | tf_op jit(solution)/shard_map/pallas_call | solution.py:704
  650.6 20.4 %collective-permute-done.84 = bf16[256,1280]{1,0:T(8,128)(2,1)S(1)} collective-permute-done((bf16[256,1280]{1,0:T(8,128)(2,1)S(1)}, bf16[256,1280]{1,0:T(8,128)(2,1)S(1)}, u32[]{:S(2)}, u32[]{:S(2)}) %collective-permute-start.84) | collective-permute-done | bytes 655392 | tf_op jit(solution)/shard_map/ppermute | solution.py:105
  682.9 8.8 %fusion.63 = f32[1024,2048]{1,0:T(8,128)S(1)} fusion(bf16[1024,1536]{1,0:T(8,128)(2,1)S(1)} %pad_maximum_fusion.5, bf16[2048,1536]{1,0:T(8,128)(2,1)} %constant_dynamic-update-slice_fusion.45), kind=kOutput, calls=%fused_computation.277 | convolution fusion | flops 6442450944 | bytes 17825792 | tf_op jit(solution)/shard_map/dot_general | solution.py:37
  725.1 10.7 %collective-permute-done.96 = bf16[256,768]{1,0:T(8,128)(2,1)} collective-permute-done((bf16[256,768]{1,0:T(8,128)(2,1)}, bf16[256,768]{1,0:T(8,128)(2,1)}, u32[]{:S(2)}, u32[]{:S(2)}) %collective-permute-start.96) | collective-permute-done | bytes 393248 | tf_op jit(solution)/shard_map/ppermute | solution.py:105
  757.6 8.4 %collective-permute-done.100 = bf16[256,768]{1,0:T(8,128)(2,1)S(1)} collective-permute-done((bf16[256,768]{1,0:T(8,128)(2,1)S(1)}, bf16[256,768]{1,0:T(8,128)(2,1)S(1)}, u32[]{:S(2)}, u32[]{:S(2)}) %collective-permute-start.100) | collective-permute-done | bytes 393248 | tf_op jit(solution)/shard_map/ppermute | solution.py:105
  795.9 8.1 shard_map.244
  (646 shorter events, 442.8 us)
Async XLA Ops:
  13.6 32.5 %collective-permute-start.8 = (bf16[80,2048]{1,0:T(8,128)(2,1)}, bf16[80,2048]{1,0:T(8,128)(2,1)}, u32[]{:S(2)}, u32[]{:S(2)}) collective-permute-start(bf16[80,2048]{1,0:T(8,128)(2,1)} %pad_maximum_fusion.16), channel_id=1, source_target_pairs={{0,2},{2,4},{4,6},{6,7},{7,5},{5,3},{3,1},{1,0},{8,10},{10,12},{12... | collective-permute-start | bytes 983048 | tf_op jit(solution)/shard_map/ppermute | solution.py:77
  15.7 29.9 %collective-permute-start.17 = (bf16[256,2048]{1,0:T(8,128)(2,1)S(1)}, bf16[256,2048]{1,0:T(8,128)(2,1)}, u32[]{:S(2)}, u32[]{:S(2)}) collective-permute-start(bf16[256,2048]{1,0:T(8,128)(2,1)S(1)} %bitcast.120), channel_id=1, source_target_pairs={{0,16},{8,24},{16,0},{24,8},{1,17},{9,25},{17,1},{25,9},{2,18},{10... | collective-permute-start | bytes 3145736 | tf_op jit(solution)/shard_map/ppermute | solution.py:124
  79.0 54.4 %collective-permute-start.22 = (bf16[176,2048]{1,0:T(8,128)(2,1)}, bf16[176,2048]{1,0:T(8,128)(2,1)}, u32[]{:S(2)}, u32[]{:S(2)}) collective-permute-start(bf16[176,2048]{1,0:T(8,128)(2,1)} %get-tuple-element.108), channel_id=1, source_target_pairs={{2,0},{4,2},{6,4},{7,6},{5,7},{3,5},{1,3},{0,1},{10,8},{12,10},{14... | collective-permute-start | bytes 2162696 | tf_op jit(solution)/shard_map/ppermute | solution.py:78
  79.4 53.9 %collective-permute-start.21 = (bf16[176,2048]{1,0:T(8,128)(2,1)}, bf16[176,2048]{1,0:T(8,128)(2,1)}, u32[]{:S(2)}, u32[]{:S(2)}) collective-permute-start(bf16[176,2048]{1,0:T(8,128)(2,1)} %get-tuple-element.108), channel_id=1, source_target_pairs={{0,2},{2,4},{4,6},{6,7},{7,5},{5,3},{3,1},{1,0},{8,10},{10,12},{12... | collective-permute-start | bytes 2162696 | tf_op jit(solution)/shard_map/ppermute | solution.py:77
  83.1 28.4 %collective-permute-start.19 = (bf16[128,1536]{1,0:T(8,128)(2,1)S(1)}, bf16[128,1536]{1,0:T(8,128)(2,1)S(1)}, u32[]{:S(2)}, u32[]{:S(2)}) collective-permute-start(bf16[128,1536]{1,0:T(8,128)(2,1)S(1)} %slice.370), channel_id=1, source_target_pairs={{0,2},{2,4},{4,6},{6,7},{7,5},{5,3},{3,1},{1,0},{8,10},{10,12},{12... | collective-permute-start | bytes 1179656 | tf_op jit(solution)/shard_map/ppermute | solution.py:77
  133.4 37.1 %collective-permute-start.25 = (bf16[176,2048]{1,0:T(8,128)(2,1)}, bf16[176,2048]{1,0:T(8,128)(2,1)}, u32[]{:S(2)}, u32[]{:S(2)}) collective-permute-start(bf16[176,2048]{1,0:T(8,128)(2,1)} %get-tuple-element.114), channel_id=1, source_target_pairs={{0,2},{2,4},{4,6},{6,7},{7,5},{5,3},{3,1},{1,0},{8,10},{10,12},{12... | collective-permute-start | bytes 2162696 | tf_op jit(solution)/shard_map/ppermute | solution.py:77
  135.0 37.0 %collective-permute-start.26 = (bf16[176,2048]{1,0:T(8,128)(2,1)}, bf16[176,2048]{1,0:T(8,128)(2,1)}, u32[]{:S(2)}, u32[]{:S(2)}) collective-permute-start(bf16[176,2048]{1,0:T(8,128)(2,1)} %get-tuple-element.114), channel_id=1, source_target_pairs={{2,0},{4,2},{6,4},{7,6},{5,7},{3,5},{1,3},{0,1},{10,8},{12,10},{14... | collective-permute-start | bytes 2162696 | tf_op jit(solution)/shard_map/ppermute | solution.py:78
  135.5 33.0 %collective-permute-start.24 = (bf16[176,2048]{1,0:T(8,128)(2,1)}, bf16[176,2048]{1,0:T(8,128)(2,1)}, u32[]{:S(2)}, u32[]{:S(2)}) collective-permute-start(bf16[176,2048]{1,0:T(8,128)(2,1)} %collective-permute-done.22), channel_id=1, source_target_pairs={{2,0},{4,2},{6,4},{7,6},{5,7},{3,5},{1,3},{0,1},{10,8},{12,10},{14... | collective-permute-start | bytes 2162696 | tf_op jit(solution)/shard_map/ppermute | solution.py:78
  137.0 31.8 %collective-permute-start.23 = (bf16[176,2048]{1,0:T(8,128)(2,1)}, bf16[176,2048]{1,0:T(8,128)(2,1)}, u32[]{:S(2)}, u32[]{:S(2)}) collective-permute-start(bf16[176,2048]{1,0:T(8,128)(2,1)} %collective-permute-done.21), channel_id=1, source_target_pairs={{0,2},{2,4},{4,6},{6,7},{7,5},{5,3},{3,1},{1,0},{8,10},{10,12},{12... | collective-permute-start | bytes 2162696 | tf_op jit(solution)/shard_map/ppermute | solution.py:77
  170.5 30.7 %collective-permute-start.29 = (bf16[176,2048]{1,0:T(8,128)(2,1)}, bf16[176,2048]{1,0:T(8,128)(2,1)}, u32[]{:S(2)}, u32[]{:S(2)}) collective-permute-start(bf16[176,2048]{1,0:T(8,128)(2,1)} %collective-permute-done.25), channel_id=1, source_target_pairs={{0,2},{2,4},{4,6},{6,7},{7,5},{5,3},{3,1},{1,0},{8,10},{10,12},{12... | collective-permute-start | bytes 2162696 | tf_op jit(solution)/shard_map/ppermute | solution.py:77
  172.0 29.1 %collective-permute-start.30 = (bf16[176,2048]{1,0:T(8,128)(2,1)}, bf16[176,2048]{1,0:T(8,128)(2,1)}, u32[]{:S(2)}, u32[]{:S(2)}) collective-permute-start(bf16[176,2048]{1,0:T(8,128)(2,1)} %collective-permute-done.26), channel_id=1, source_target_pairs={{2,0},{4,2},{6,4},{7,6},{5,7},{3,5},{1,3},{0,1},{10,8},{12,10},{14... | collective-permute-start | bytes 2162696 | tf_op jit(solution)/shard_map/ppermute | solution.py:78
  474.3 27.9 %collective-permute-start.63 = (bf16[256,2048]{1,0:T(8,128)(2,1)S(1)}, bf16[256,2048]{1,0:T(8,128)(2,1)S(1)}, u32[]{:S(2)}, u32[]{:S(2)}) collective-permute-start(bf16[256,2048]{1,0:T(8,128)(2,1)S(1)} %get-tuple-element.252), channel_id=1, source_target_pairs={{0,8},{8,0},{16,24},{24,16},{1,9},{9,1},{17,25},{25,17},{2,10},{10... | collective-permute-start | bytes 3145736 | tf_op jit(solution)/shard_map/ppermute | solution.py:131
  485.8 27.4 %collective-permute-start.66 = (bf16[176,2048]{1,0:T(8,128)(2,1)S(1)}, bf16[176,2048]{1,0:T(8,128)(2,1)S(1)}, u32[]{:S(2)}, u32[]{:S(2)}) collective-permute-start(bf16[176,2048]{1,0:T(8,128)(2,1)S(1)} %get-tuple-element.146), channel_id=1, source_target_pairs={{0,2},{2,4},{4,6},{6,7},{7,5},{5,3},{3,1},{1,0},{8,10},{10,12},{12... | collective-permute-start | bytes 2162696 | tf_op jit(solution)/shard_map/ppermute | solution.py:105
  486.6 26.6 %collective-permute-start.67 = (bf16[176,2048]{1,0:T(8,128)(2,1)S(1)}, bf16[176,2048]{1,0:T(8,128)(2,1)S(1)}, u32[]{:S(2)}, u32[]{:S(2)}) collective-permute-start(bf16[176,2048]{1,0:T(8,128)(2,1)S(1)} %get-tuple-element.147), channel_id=1, source_target_pairs={{2,0},{4,2},{6,4},{7,6},{5,7},{3,5},{1,3},{0,1},{10,8},{12,10},{14... | collective-permute-start | bytes 2162696 | tf_op jit(solution)/shard_map/ppermute | solution.py:106
  524.1 31.6 %collective-permute-start.73 = (bf16[352,2048]{1,0:T(8,128)(2,1)}, bf16[352,2048]{1,0:T(8,128)(2,1)}, u32[]{:S(2)}, u32[]{:S(2)}) collective-permute-start(bf16[352,2048]{1,0:T(8,128)(2,1)} %pad_maximum_fusion.6), channel_id=1, source_target_pairs={{0,2},{2,4},{4,6},{6,7},{7,5},{5,3},{3,1},{1,0},{8,10},{10,12},{12... | collective-permute-start | bytes 4325384 | tf_op jit(solution)/shard_map/ppermute | solution.py:105
  526.0 33.3 %collective-permute-start.74 = (bf16[352,2048]{1,0:T(8,128)(2,1)}, bf16[352,2048]{1,0:T(8,128)(2,1)}, u32[]{:S(2)}, u32[]{:S(2)}) collective-permute-start(bf16[352,2048]{1,0:T(8,128)(2,1)} %pad_maximum_fusion.7), channel_id=1, source_target_pairs={{2,0},{4,2},{6,4},{7,6},{5,7},{3,5},{1,3},{0,1},{10,8},{12,10},{14... | collective-permute-start | bytes 4325384 | tf_op jit(solution)/shard_map/ppermute | solution.py:106
  527.6 34.7 %collective-permute-start.70 = (bf16[256,2048]{1,0:T(8,128)(2,1)S(1)}, bf16[256,2048]{1,0:T(8,128)(2,1)S(1)}, u32[]{:S(2)}, u32[]{:S(2)}) collective-permute-start(bf16[256,2048]{1,0:T(8,128)(2,1)S(1)} %get-tuple-element.198), channel_id=1, source_target_pairs={{0,8},{8,0},{16,24},{24,16},{1,9},{9,1},{17,25},{25,17},{2,10},{10... | collective-permute-start | bytes 3145736 | tf_op jit(solution)/shard_map/ppermute | solution.py:125
  571.8 39.9 %collective-permute-start.77 = (bf16[176,2048]{1,0:T(8,128)(2,1)}, bf16[176,2048]{1,0:T(8,128)(2,1)S(1)}, u32[]{:S(2)}, u32[]{:S(2)}) collective-permute-start(bf16[176,2048]{1,0:T(8,128)(2,1)} %add_convert_fusion.9.p0), channel_id=1, source_target_pairs={{0,8},{8,0},{16,24},{24,16},{1,9},{9,1},{17,25},{25,17},{2,10},{10... | collective-permute-start | bytes 2162696 | tf_op jit(solution)/shard_map/ppermute | solution.py:125
  571.8 28.7 %collective-permute-start.78 = (bf16[176,2048]{1,0:T(8,128)(2,1)}, bf16[176,2048]{1,0:T(8,128)(2,1)}, u32[]{:S(2)}, u32[]{:S(2)}) collective-permute-start(bf16[176,2048]{1,0:T(8,128)(2,1)} %add_convert_fusion.9.p0), channel_id=1, source_target_pairs={{0,16},{8,24},{16,0},{24,8},{1,17},{9,25},{17,1},{25,9},{2,18},{10... | collective-permute-start | bytes 2162696 | tf_op jit(solution)/shard_map/ppermute | solution.py:124
  572.6 39.1 %collective-permute-start.75 = (bf16[352,2048]{1,0:T(8,128)(2,1)}, bf16[352,2048]{1,0:T(8,128)(2,1)}, u32[]{:S(2)}, u32[]{:S(2)}) collective-permute-start(bf16[352,2048]{1,0:T(8,128)(2,1)} %add_convert_fusion.5), channel_id=1, source_target_pairs={{0,2},{2,4},{4,6},{6,7},{7,5},{5,3},{3,1},{1,0},{8,10},{10,12},{12... | collective-permute-start | bytes 4325384 | tf_op jit(solution)/shard_map/ppermute | solution.py:105
  573.1 38.7 %collective-permute-start.76 = (bf16[352,2048]{1,0:T(8,128)(2,1)}, bf16[352,2048]{1,0:T(8,128)(2,1)}, u32[]{:S(2)}, u32[]{:S(2)}) collective-permute-start(bf16[352,2048]{1,0:T(8,128)(2,1)} %add_convert_fusion.4), channel_id=1, source_target_pairs={{2,0},{4,2},{6,4},{7,6},{5,7},{3,5},{1,3},{0,1},{10,8},{12,10},{14... | collective-permute-start | bytes 4325384 | tf_op jit(solution)/shard_map/ppermute | solution.py:106
  612.7 28.4 %collective-permute-start.80 = (bf16[128,1280]{1,0:T(8,128)(2,1)}, bf16[128,1280]{1,0:T(8,128)(2,1)}, u32[]{:S(2)}, u32[]{:S(2)}) collective-permute-start(bf16[128,1280]{1,0:T(8,128)(2,1)} %get-tuple-element.163), channel_id=1, source_target_pairs={{0,2},{2,4},{4,6},{6,7},{7,5},{5,3},{3,1},{1,0},{8,10},{10,12},{12... | collective-permute-start | bytes 983048 | tf_op jit(solution)/shard_map/ppermute | solution.py:105
  613.2 27.9 %collective-permute-start.81 = (bf16[128,1280]{1,0:T(8,128)(2,1)}, bf16[128,1280]{1,0:T(8,128)(2,1)}, u32[]{:S(2)}, u32[]{:S(2)}) collective-permute-start(bf16[128,1280]{1,0:T(8,128)(2,1)} %get-tuple-element.164), channel_id=1, source_target_pairs={{2,0},{4,2},{6,4},{7,6},{5,7},{3,5},{1,3},{0,1},{10,8},{12,10},{14... | collective-permute-start | bytes 983048 | tf_op jit(solution)/shard_map/ppermute | solution.py:106
  619.3 55.3 %collective-permute-start.82 = (bf16[352,2048]{1,0:T(8,128)(2,1)S(1)}, bf16[352,2048]{1,0:T(8,128)(2,1)}, u32[]{:S(2)}, u32[]{:S(2)}) collective-permute-start(bf16[352,2048]{1,0:T(8,128)(2,1)S(1)} %add_convert_fusion.3), channel_id=1, source_target_pairs={{0,2},{2,4},{4,6},{6,7},{7,5},{5,3},{3,1},{1,0},{8,10},{10,12},{12... | collective-permute-start | bytes 4325384 | tf_op jit(solution)/shard_map/ppermute | solution.py:105
  622.4 52.3 %collective-permute-start.83 = (bf16[352,2048]{1,0:T(8,128)(2,1)}, bf16[352,2048]{1,0:T(8,128)(2,1)}, u32[]{:S(2)}, u32[]{:S(2)}) collective-permute-start(bf16[352,2048]{1,0:T(8,128)(2,1)} %add_convert_fusion.2), channel_id=1, source_target_pairs={{2,0},{4,2},{6,4},{7,6},{5,7},{3,5},{1,3},{0,1},{10,8},{12,10},{14... | collective-permute-start | bytes 4325384 | tf_op jit(solution)/shard_map/ppermute | solution.py:106
  643.7 27.2 %collective-permute-start.84 = (bf16[256,1280]{1,0:T(8,128)(2,1)S(1)}, bf16[256,1280]{1,0:T(8,128)(2,1)S(1)}, u32[]{:S(2)}, u32[]{:S(2)}) collective-permute-start(bf16[256,1280]{1,0:T(8,128)(2,1)S(1)} %pad_maximum_fusion.12), channel_id=1, source_target_pairs={{0,2},{2,4},{4,6},{6,7},{7,5},{5,3},{3,1},{1,0},{8,10},{10,12},{12... | collective-permute-start | bytes 1966088 | tf_op jit(solution)/shard_map/ppermute | solution.py:105
  643.8 27.1 %collective-permute-start.85 = (bf16[256,1280]{1,0:T(8,128)(2,1)S(1)}, bf16[256,1280]{1,0:T(8,128)(2,1)S(1)}, u32[]{:S(2)}, u32[]{:S(2)}) collective-permute-start(bf16[256,1280]{1,0:T(8,128)(2,1)S(1)} %pad_maximum_fusion.13), channel_id=1, source_target_pairs={{2,0},{4,2},{6,4},{7,6},{5,7},{3,5},{1,3},{0,1},{10,8},{12,10},{14... | collective-permute-start | bytes 1966088 | tf_op jit(solution)/shard_map/ppermute | solution.py:106
  699.8 37.1 %collective-permute-start.90 = (bf16[256,2048]{1,0:T(8,128)(2,1)}, bf16[256,2048]{1,0:T(8,128)(2,1)}, u32[]{:S(2)}, u32[]{:S(2)}) collective-permute-start(bf16[256,2048]{1,0:T(8,128)(2,1)} %get-tuple-element.250), channel_id=1, source_target_pairs={{0,8},{8,0},{16,24},{24,16},{1,9},{9,1},{17,25},{25,17},{2,10},{10... | collective-permute-start | bytes 3145736 | tf_op jit(solution)/shard_map/ppermute | solution.py:131
  708.0 28.9 %collective-permute-start.92 = (bf16[256,2048]{1,0:T(8,128)(2,1)}, bf16[256,2048]{1,0:T(8,128)(2,1)}, u32[]{:S(2)}, u32[]{:S(2)}) collective-permute-start(bf16[256,2048]{1,0:T(8,128)(2,1)} %add_convert_fusion.6), channel_id=1, source_target_pairs={{0,16},{8,24},{16,0},{24,8},{1,17},{9,25},{17,1},{25,9},{2,18},{10... | collective-permute-start | bytes 3145736 | tf_op jit(solution)/shard_map/ppermute | solution.py:133
  742.1 38.2 %collective-permute-start.110 = (bf16[352,2048]{1,0:T(8,128)(2,1)}, bf16[352,2048]{1,0:T(8,128)(2,1)}, u32[]{:S(2)}, u32[]{:S(2)}) collective-permute-start(bf16[352,2048]{1,0:T(8,128)(2,1)} %add_convert_fusion.1.p0), channel_id=1, source_target_pairs={{0,16},{8,24},{16,0},{24,8},{1,17},{9,25},{17,1},{25,9},{2,18},{10... | collective-permute-start | bytes 4325384 | tf_op jit(solution)/shard_map/ppermute | solution.py:124
  749.7 44.9 %collective-permute-start.109 = (bf16[352,2048]{1,0:T(8,128)(2,1)}, bf16[352,2048]{1,0:T(8,128)(2,1)}, u32[]{:S(2)}, u32[]{:S(2)}) collective-permute-start(bf16[352,2048]{1,0:T(8,128)(2,1)} %add_convert_fusion.1.p0), channel_id=1, source_target_pairs={{0,8},{8,0},{16,24},{24,16},{1,9},{9,1},{17,25},{25,17},{2,10},{10... | collective-permute-start | bytes 4325384 | tf_op jit(solution)/shard_map/ppermute | solution.py:125
  782.0 26.2 %collective-permute-start.107 = (bf16[256,768]{1,0:T(8,128)(2,1)S(1)}, bf16[256,768]{1,0:T(8,128)(2,1)}, u32[]{:S(2)}, u32[]{:S(2)}) collective-permute-start(bf16[256,768]{1,0:T(8,128)(2,1)S(1)} %slice.508.refs_0_), channel_id=1, source_target_pairs={{0,16},{8,24},{16,0},{24,8},{1,17},{9,25},{17,1},{25,9},{2,18},{10... | collective-permute-start | bytes 1179656 | tf_op jit(solution)/shard_map/ppermute | solution.py:124
  (178 other events, 2675.0 us)
